TPU v7x, 256 devices: a whole 4x4x8 slice. The times are simulated.
256 devices in a mesh: pipe: 2 (over core), dp: 64 (over z, y, x_lo), tensor: 2 (over x_hi).
Axes of the slice: x: 4 (x_hi: 2, x_lo: 2; x = x_hi * 2 + x_lo), y: 4, z: 8, core: 2. Of those that a mesh axis runs over, the one named last changes fastest.
Arguments:
- hidden_in: bfloat16 [2, 128, 2, 64, 3584], P('pipe', 'dp'), may hold values from -60 to 60, as said below
- attention_probs: bfloat16 [2, 128, 2, 14, 64, 64], P('pipe', 'dp', None, 'tensor'), may hold values from 0 to 1, as said below
- norm_gain: float32 [2, 3584], P('pipe'), may hold values from 0.5 to 1.5
- value_weight: bfloat16 [2, 3584, 256], P('pipe', None, 'tensor'), may hold values from -0.09375 to 0.09375
- output_weight: bfloat16 [2, 1792, 3584], P('pipe', 'tensor'), may hold values from -0.125 to 0.125
- head_grad: bfloat16 [128, 2, 64, 3584], P('dp', 'tensor'), may hold values from -16 to 16
- policy_logprob: float32 [128, 2, 64], P('dp'), may hold values from -3 to -0.2
- reference_logprob: float32 [128, 2], P('dp'), may hold values from -96 to -12.8
- sequence_bounds: int32 [128, 3], P('dp'), may hold values from 1 to 64, as said below
Outputs:
- section_cotangent: bfloat16 [2, 128, 2, 64, 3584], P('pipe', 'dp', 'tensor')
- value_gradient: float32 [2, 3584, 256], P('pipe', 'dp', 'tensor')
- output_gradient: float32 [2, 3584, 1792], P('pipe', 'dp', 'tensor')
- gain_gradient: float32 [2, 3584], P('pipe', 'dp')
Inputs may be any that keep to these rules, and one draw needn't show every extreme that they name: `sequence_bounds`: entry 0 is the prompt length, shared by the two sequences of a pair; a sequence's response is the positions from entry 0 up to its end (entry 1 for the chosen, entry 2 for the rejected sequence), and holds one position or more. `attention_probs`: each row is a causal attention distribution: zero above the diagonal, summing to one before rounding. `hidden_in`: activations of varying size from token to token.
All inputs are finite; a program needn't handle non-finite values.
Results may differ from a plain program's by a relative error of at most 0.017.
Values may be sent and summed in bfloat16 or wider, within the bound.
No kernel may reach another device: no remote copies, remote signals or barrier semaphores. Data moves between devices by JAX's collectives and lax.ppermute only.
A program may use at most 128 MiB of HBM per device.

v0:
```python
import jax
import jax.numpy as jnp
from jax import lax
from jax.experimental import pallas as pl
from jax.experimental.pallas import tpu as pltpu
from jax.sharding import Mesh, PartitionSpec as P


HEAD_DIM = 128
EPSILON = 1e-06
DPO_BETA = 0.25
LIKELIHOOD_COEF = 0.2
NZ, NY, NX, NT = 8, 4, 2, 2
F32, BF16 = jnp.float32, jnp.bfloat16


def paired(block, axis, size, distance, section=None):
    if section is None:
        return lax.ppermute(block, axis, [(i, i ^ distance) for i in range(size)])
    base = section * size
    route = [(base + i, base + (i ^ distance)) for i in range(size)]
    return lax.ppermute(block, ("pipe", axis), route)


def over_xz(block, k):
    route = [
        (z * NX + x, (z ^ (k >> 1)) * NX + (x ^ (k & 1))) for z in range(NZ) for x in range(NX)
    ]
    return lax.ppermute(block, ("z", "x"), route)


VMEM = pl.BlockSpec(memory_space=pltpu.VMEM)
SMEM = pl.BlockSpec(memory_space=pltpu.SMEM)


def dot(a, b, contract):
    return lax.dot_general(a, b, (contract, ((), ())), preferred_element_type=F32)


def rms_of(x):
    return lax.rsqrt(jnp.mean(x * x, axis=-1, keepdims=True) + EPSILON)


def forward_kernel(x_ref, gain_ref, wv_ref, pattern_ref, normed_ref, mixed_ref):
    rows = 2 * pattern_ref.shape[2]
    heads, seq = pattern_ref.shape[1:3]
    for start in range(0, x_ref.shape[0], rows):
        x = x_ref[start : start + rows].astype(F32)
        normed = (x * rms_of(x) * gain_ref[...]).astype(BF16)
        normed_ref[start : start + rows] = normed
        values = dot(normed, wv_ref[...], ((1,), (0,))).astype(BF16)
        for part in range(2):
            pattern = pattern_ref[start // seq + part].reshape(heads * seq, seq)
            mixed = dot(pattern, values[part * seq : (part + 1) * seq], ((1,), (0,))).astype(BF16)
            for h in range(heads):
                mixed_ref[
                    start + part * seq : start + (part + 1) * seq, h * HEAD_DIM : (h + 1) * HEAD_DIM
                ] = mixed[h * seq : (h + 1) * seq]


def values_kernel(active_ref, dy_ref, wo_ref, pattern_ref, values_ref, mixed_ref):
    step = pl.program_id(0)

    @pl.when(active_ref[0] == 1)
    def _():
        part = dot(dy_ref[...], wo_ref[...], ((1,), (1,)))

        @pl.when(step == 0)
        def _():
            mixed_ref[...] = part

        @pl.when(step > 0)
        def _():
            mixed_ref[...] += part

        @pl.when(step == pl.num_programs(0) - 1)
        def _():
            sequences, heads, seq, _ = pattern_ref.shape
            for n in range(sequences):
                stacked = jnp.concatenate(
                    [
                        mixed_ref[
                            n * seq : (n + 1) * seq, h * HEAD_DIM : (h + 1) * HEAD_DIM
                        ].astype(BF16)
                        for h in range(heads)
                    ],
                    axis=0,
                )
                pattern = pattern_ref[n].reshape(heads * seq, seq)
                values = dot(pattern, stacked, ((0,), (0,))).astype(BF16)
                values_ref[n * seq : (n + 1) * seq] = values


def rows_kernel(
    active_ref, tensor_ref, own_ref, other_ref, own_wv_ref, other_wv_ref, x_ref, gain_ref, dy_ref,
    rows_ref,
):
    @pl.when(active_ref[0] == 1)
    def _():
        first = dot(own_ref[...], own_wv_ref[...], ((1,), (1,))).astype(BF16)
        second = dot(other_ref[...], other_wv_ref[...], ((1,), (1,))).astype(BF16)
        scaled = (first.astype(F32) + second.astype(F32)) * gain_ref[...]
        x = x_ref[...].astype(F32)
        inverse = rms_of(x)
        pull = (inverse * inverse * inverse) * jnp.mean(x * scaled, axis=-1, keepdims=True)
        rows_ref[...] = (dy_ref[...].astype(F32) + (inverse * scaled - x * pull)).astype(BF16)


def owners_kernel(active_ref, y_ref, dy_ref, weight_ref, values_ref, normed_ref, *refs):
    out_refs, turned_ref = refs[:-1], refs[-1]

    @pl.when(active_ref[0] == 1)
    def _():
        tokens, width = dy_ref.shape
        weight = weight_ref[...]
        values = (weight * values_ref[...].astype(F32)).astype(BF16)
        for start in range(0, width, 512):
            at = slice(start, start + 512)
            dy = (weight * dy_ref[:, at].astype(F32)).astype(BF16)
            turned_ref[at, :tokens] = dy.T
            turned_ref[at, tokens:] = dot(normed_ref[:, at], values, ((0,), (0,))).astype(BF16)
        size = out_refs[0].shape[0] // NZ
        for s, out_ref in enumerate(out_refs):
            owner = (y_ref[0] + s) % NY
            for z in range(NZ):
                start = pl.multiple_of((z * NY + owner) * size, 16)
                out_ref[z * size : (z + 1) * size] = turned_ref[pl.ds(start, size)]


def products_kernel(upper_ref, own_ref, *refs):
    upper_blocks, lower_blocks, mixed_refs = refs[:NY], refs[NY : 2 * NY], refs[2 * NY : 3 * NY]
    out_refs, total_ref = refs[3 * NY : -1], refs[-1]
    tokens = mixed_refs[0].shape[0]

    def add_up(blocks):
        total_ref[:, :HEAD_DIM] = sum(b[:, tokens:].astype(F32) for b in blocks)
        total_ref[:, HEAD_DIM:] = sum(
            dot(b[:, :tokens], m[...], ((1,), (0,))) for b, m in zip(blocks, mixed_refs)
        )

    @pl.when(upper_ref[0] == 1)
    def _():
        add_up(upper_blocks)

    @pl.when(upper_ref[0] == 0)
    def _():
        add_up(lower_blocks)

    size = out_refs[0].shape[1]
    for k, out_ref in enumerate(out_refs):
        start = pl.multiple_of((own_ref[0] ^ k) * size, 8)
        out_ref[0] = total_ref[pl.ds(start, size)].astype(BF16)


def stage_kernel(own_ref, a_ref, b_ref, c_ref, d_ref, *out_refs):
    for k, out_ref in enumerate(out_refs):
        j = own_ref[0] ^ k
        total = sum(r[j].astype(F32) for r in (a_ref, b_ref, c_ref, d_ref))
        out_ref[...] = total.astype(out_ref.dtype)


def last_kernel(a_ref, b_ref, c_ref, d_ref, wv_ref, gain_ref, value_ref, output_ref, part_ref):
    total = a_ref[...] + sum(r[...].astype(F32) for r in (b_ref, c_ref, d_ref))
    value = total[:, :HEAD_DIM]
    value_ref[0] = value
    output_ref[0] = total[:, HEAD_DIM:]
    part_ref[...] = jnp.sum(wv_ref[...] * value, axis=1, keepdims=True) / gain_ref[...]


def shaped(*dims):
    return jax.ShapeDtypeStruct(dims, BF16)


def after(block, *others):
    return lax.optimization_barrier((block, *others))[0]


def section_step(
    hidden_in,
    attention_probs,
    norm_gain,
    value_weight,
    output_weight,
    head_grad,
    policy_logprob,
    reference_logprob,
    sequence_bounds,
):
    section = lax.axis_index("pipe")
    zi, yi, xi, ti = (lax.axis_index(a) for a in ("z", "y", "x", "t"))
    pairs, _, seq, width = hidden_in.shape[1:]
    heads = attention_probs.shape[3]
    tokens = pairs * 2 * seq
    gain = norm_gain[0]
    wv = value_weight[0]
    wo = output_weight[0]
    inputs = hidden_in[0]
    pattern = attention_probs[0]
    own_head = head_grad[:, 0]

    other_head = lax.ppermute(own_head, ("pipe", "t"), [(2, 3), (3, 2)])

    positions = jnp.arange(seq, dtype=jnp.int32)
    response_bool = (positions[None, None, :] >= sequence_bounds[:, 0:1, None]) & (
        positions[None, None, :] < sequence_bounds[:, 1:3, None]
    )
    ends = jnp.clip(sequence_bounds[:, :2], 0, seq)
    count = jnp.sum(jnp.maximum(ends[:, 1] - ends[:, 0], 0)).reshape(1, 1)
    count = lax.optimization_barrier(jnp.broadcast_to(count, (8, 128)))
    steps = (("y", NY, 1), ("y", NY, 2), ("x", NX, 1), ("z", NZ, 1), ("z", NZ, 2), ("z", NZ, 4))
    for axis, size, distance in steps:
        got = paired(count, axis, size, distance, 0)
        count = count + got
    mask = response_bool.astype(F32)
    sequence_logprob = jnp.sum(mask * policy_logprob, axis=-1)
    margin = DPO_BETA * (
        sequence_logprob[:, 0]
        - reference_logprob[:, 0]
        - (sequence_logprob[:, 1] - reference_logprob[:, 1])
    )
    weight_pair = jax.nn.sigmoid(-margin)

    def across(block, section_id):
        pairs_xt = ((0, 3), (3, 0), (1, 2), (2, 1))
        base = section_id * 4
        route = [(base + a, base + b) for a, b in pairs_xt]
        return lax.ppermute(block, ("pipe", "x", "t"), route)

    other_wv_1 = across(after(wv, other_head), 1)

    x = inputs.reshape(tokens, width)
    patterns = pattern.reshape(pairs * 2, heads, seq, seq)
    normed, mixed = pl.pallas_call(
        forward_kernel,
        out_shape=(shaped(tokens, width), shaped(tokens, heads * HEAD_DIM)),
        in_specs=[VMEM] * 4,
        out_specs=(VMEM, VMEM),
    )(x, norm_gain, wv, patterns)

    def around(block, shift):
        return lax.ppermute(block, "y", [(i, (i + shift) % NY) for i in range(NY)])

    mixed_all = [mixed] + [around(mixed, s) for s in range(1, NY)]

    def values_of(active, dy):
        block = 512
        return pl.pallas_call(
            values_kernel,
            out_shape=shaped(tokens, HEAD_DIM),
            grid_spec=pltpu.PrefetchScalarGridSpec(
                num_scalar_prefetch=1,
                grid=(width // block,),
                in_specs=[
                    pl.BlockSpec((tokens, block), lambda i, on: (0, i * on[0])),
                    pl.BlockSpec((heads * HEAD_DIM, block), lambda i, on: (0, i * on[0])),
                    pl.BlockSpec((pairs * 2, heads, seq, seq), lambda i, on: (0, 0, 0, 0)),
                ],
                out_specs=pl.BlockSpec((tokens, HEAD_DIM), lambda i, on: (0, 0)),
                scratch_shapes=[pltpu.VMEM((tokens, heads * HEAD_DIM), F32)],
            ),
        )(active, dy, wo, patterns)

    def rows_of(active, own, other, other_wv, dy, own_only):
        count = pairs if own_only else pairs * 2

        def pick(n, on, t):
            return ((n * 2 + t[0] if own_only else n) * on[0], 0)

        def whole(n, on, t):
            return (0, 0)

        return pl.pallas_call(
            rows_kernel,
            out_shape=shaped(count * seq, width),
            grid_spec=pltpu.PrefetchScalarGridSpec(
                num_scalar_prefetch=2,
                grid=(count,),
                in_specs=[
                    pl.BlockSpec((seq, HEAD_DIM), pick),
                    pl.BlockSpec((seq, HEAD_DIM), pick),
                    pl.BlockSpec((width, HEAD_DIM), whole),
                    pl.BlockSpec((width, HEAD_DIM), whole),
                    pl.BlockSpec((seq, width), pick),
                    pl.BlockSpec((1, width), whole),
                    pl.BlockSpec((seq, width), pick),
                ],
                out_specs=pl.BlockSpec((seq, width), lambda n, on, t: (n, 0)),
            ),
        )(active, ti.astype(jnp.int32).reshape(1), own, other, wv, other_wv, x, norm_gain, dy)

    def owners_of(active, dy, weight, values):
        return pl.pallas_call(
            owners_kernel,
            out_shape=(shaped(width // NY, tokens + HEAD_DIM),) * NY,
            in_specs=[SMEM, SMEM] + [VMEM] * 4,
            out_specs=(VMEM,) * NY,
            scratch_shapes=[pltpu.VMEM((width, tokens + HEAD_DIM), BF16)],
        )(active, yi.astype(jnp.int32).reshape(1), dy, weight, values, normed)

    def swapped(values, section_id):
        route = [(section_id * 2, section_id * 2 + 1), (section_id * 2 + 1, section_id * 2)]
        return lax.ppermute(values, ("pipe", "t"), route)

    def sent(blocks, section_id):
        base = section_id * NY
        got = [blocks[0]]
        for s in range(1, NY):
            route = [(base + i, base + (i + s) % NY) for i in range(NY)]
            got.append(lax.ppermute(blocks[s], ("pipe", "y"), route))
        return got

    upper = section == 1
    is_upper = upper.astype(jnp.int32).reshape(1)
    is_lower = 1 - is_upper
    columns = HEAD_DIM * (heads + 1)
    share_rows = width // (NZ * NY * NX)

    top = jnp.where(
        ti == 0, jnp.stack([own_head, other_head], 1), jnp.stack([other_head, own_head], 1)
    )
    raw = jnp.where(response_bool[..., None], top, jnp.zeros((), BF16)).reshape(tokens, width)
    raw = after(raw, mixed)
    own_1 = values_of(is_upper, raw)
    other_1 = swapped(own_1, 1)
    rows_1 = rows_of(is_upper, own_1, other_1, other_wv_1, raw, False)
    incoming = lax.ppermute(rows_1, "pipe", [(1, 0)])

    count = after(count, rows_1)
    count_up = lax.ppermute(count, "pipe", [(0, 1)])
    chosen_total = jnp.where(upper, count_up, count)[0, 0]
    pair_total = pairs * NZ * NY * NX
    scale = LIKELIHOOD_COEF * jnp.asarray(pair_total, F32) / chosen_total.astype(F32)
    weights = jnp.stack([-DPO_BETA * weight_pair - scale, DPO_BETA * weight_pair], axis=1)
    weight = jnp.broadcast_to(weights[:, :, None], (pairs, 2, seq)).reshape(tokens, 1)

    turned_1 = owners_of(is_upper, raw, weight, own_1)
    blocks_1 = sent(turned_1, 1)

    other_wv_0 = across(after(wv, count, mixed), 0)
    own_0 = values_of(is_lower, incoming)
    other_0 = swapped(own_0, 0)
    turned_0 = owners_of(is_lower, incoming, weight, own_0)
    blocks_0 = sent(turned_0, 0)

    first_own = ((zi % 2) * NX + xi).astype(jnp.int32).reshape(1)
    group = width // NY // 4

    def rows_if(wanted):
        return pl.BlockSpec(
            (group, tokens + HEAD_DIM),
            lambda i, on, own: ((i * on[0] if wanted else i * (1 - on[0])), 0),
        )

    parts = pl.pallas_call(
        products_kernel,
        out_shape=(shaped(4, share_rows, columns),) * 4,
        grid_spec=pltpu.PrefetchScalarGridSpec(
            num_scalar_prefetch=2,
            grid=(4,),
            in_specs=[rows_if(True)] * NY
            + [rows_if(False)] * NY
            + [pl.BlockSpec((tokens, heads * HEAD_DIM), lambda i, on, own: (0, 0))] * NY,
            out_specs=(pl.BlockSpec((1, share_rows, columns), lambda i, on, own: (i, 0, 0)),) * 4,
            scratch_shapes=[pltpu.VMEM((group, columns), F32)],
        ),
    )(is_upper, first_own, *blocks_1, *after(tuple(blocks_0), other_0), *mixed_all)
    got = [parts[0]] + [over_xz(parts[k], k) for k in (1, 2, 3)]
    parts = pl.pallas_call(
        stage_kernel,
        out_shape=(jax.ShapeDtypeStruct((share_rows, columns), F32),)
        + (shaped(share_rows, columns),) * 3,
        in_specs=[SMEM] + [VMEM] * 4,
        out_specs=(VMEM,) * 4,
    )((zi // 2).astype(jnp.int32).reshape(1), *got)
    got = [parts[0]] + [over_xz(parts[k], k << 2) for k in (1, 2, 3)]

    rows_0 = rows_of(is_lower, own_0, other_0, other_wv_0, incoming, True)
    own_1_rows = lax.dynamic_index_in_dim(rows_1.reshape(pairs, 2, seq, width), ti, 1, False)
    own_rows = jnp.where(upper, own_1_rows, rows_0.reshape(pairs, seq, width)).astype(F32)
    own_weight = lax.dynamic_index_in_dim(weights, ti, 1, False)[:, None, None]
    own_rows = (own_weight * own_rows).astype(BF16)[:, None]

    start = ((zi * NY + yi) * NX + xi) * share_rows
    own_wv = lax.dynamic_slice_in_dim(wv, start, share_rows, 0).astype(F32)
    own_gain = lax.dynamic_slice_in_dim(gain, start, share_rows, 0).reshape(share_rows, 1)
    value_share, output_share, gain_part = pl.pallas_call(
        last_kernel,
        out_shape=(
            jax.ShapeDtypeStruct((1, share_rows, HEAD_DIM), F32),
            jax.ShapeDtypeStruct((1, share_rows, columns - HEAD_DIM), F32),
            jax.ShapeDtypeStruct((share_rows, 1), F32),
        ),
        in_specs=[VMEM] * 6,
        out_specs=(VMEM,) * 3,
    )(*got, own_wv, own_gain)
    gain_part = gain_part.reshape(1, share_rows)
    gain_rows = gain_part + paired(gain_part, "t", NT, 1)
    return own_rows[None], value_share, output_share, gain_rows


def solution(mesh):
    fine = Mesh(
        mesh.devices.reshape(2, NZ, NY, NX, NT), ("pipe", "z", "y", "x", "t")
    )
    dp = ("z", "y", "x")
    in_specs = (
        P("pipe", dp, None, None, None),
        P("pipe", dp, None, "t", None, None),
        P("pipe", None),
        P("pipe", None, "t"),
        P("pipe", "t", None),
        P(dp, "t", None, None),
        P(dp, None, None),
        P(dp, None),
        P(dp, None),
    )
    out_specs = (
        P("pipe", dp, "t", None, None),
        P("pipe", dp, "t"),
        P("pipe", dp, "t"),
        P("pipe", dp),
    )
    return jax.shard_map(section_step, mesh=fine, in_specs=in_specs, out_specs=out_specs, check_vma=False)
```

profile of v0, /device:TPU:4, one launch (start us, length us, event | category | flops | bytes accessed | tf_op | source)
XLA Modules:
  0.0 189.6 jit_solution(3426093155461955946)
XLA Ops:
  4.8 4.4 %shard_map.120 = (bf16[256,3584]{1,0:T(8,128)(2,1)}, bf16[256,896]{1,0:T(8,128)(2,1)}) custom-call(bf16[256,3584]{1,0:T(8,128)(2,1)} %bitcast.32, f32[1,3584]{1,0:T(1,128)} %gain_ref.5, bf16[3584,128]{1,0:T(8,128)(2,1)} %bitcast.35, bf16[4,7,64,64]{3,2,1,0:T(8,128)(2,1)} %bitcast.41), custom_call_target="tpu_custom_call" | custom-call | tf_op jit(solution)/shard_map/pallas_call | solution.py:233
  13.0 2.0 %shard_map.121.own_ref.values_ref = bf16[256,128]{1,0:T(8,128)(2,1)} custom-call(s32[1]{0:T(128)} %bitcast.active_ref.upper_ref, bf16[256,3584]{1,0:T(8,128)(2,1)} %bitcast_select_fusion.dy_ref, bf16[896,3584]{1,0:T(8,128)(2,1)} %bitcast.30, bf16[4,7,64,64]{3,2,1,0:T(8,128)(2,1)} %bitcast.42), custom_call_target="tpu_custom_call" | custom-call | tf_op jit(solution)/shard_map/pallas_call | solution.py:247
  16.6 3.5 %shard_map.122 = bf16[256,3584]{1,0:T(8,128)(2,1)} custom-call(s32[1]{0:T(128)} %bitcast.active_ref.upper_ref, s32[1]{0:T(128)} %bitcast.1.tensor_ref, bf16[256,128]{1,0:T(8,128)(2,1)} %shard_map.121.own_ref.values_ref, bf16[256,128]{1,0:T(8,128)(2,1)} %copy-done.18, bf16[3584,128]{1,0:T(8,128)(2,1)} %bitcast.36, bf16[3584,128]{1,0:T(8,128)(2,1)} %copy-done.4, ...), custom_call_target="tpu_custom_call" | custom-call | tf_op jit(solution)/shard_map/pallas_call | solution.py:272
  22.1 3.5 %collective-permute-start = (s32[8,128]{1,0:T(8,128)S(1)}, s32[8,128]{1,0:T(8,128)S(1)}, u32[]{:S(2)}, u32[]{:S(2)}) collective-permute-start(s32[8,128]{1,0:T(8,128)S(1)} %broadcast_in_dim.16), channel_id=1, source_target_pairs={{0,4},{4,0},{8,12},{12,8},{1,5},{5,1},{9,13},{13,9},{2,6},{6,2},{1... | collective-permute-start | bytes 12296 | tf_op jit(solution)/shard_map/ppermute | solution.py:22
  25.6 2.0 %collective-permute-done = s32[8,128]{1,0:T(8,128)S(1)} collective-permute-done((s32[8,128]{1,0:T(8,128)S(1)}, s32[8,128]{1,0:T(8,128)S(1)}, u32[]{:S(2)}, u32[]{:S(2)}) %collective-permute-start) | collective-permute-done | bytes 4128 | tf_op jit(solution)/shard_map/ppermute | solution.py:22
  27.6 5.1 %collective-permute-start.1 = (s32[8,128]{1,0:T(8,128)S(1)}, s32[8,128]{1,0:T(8,128)S(1)}, u32[]{:S(2)}, u32[]{:S(2)}) collective-permute-start(s32[8,128]{1,0:T(8,128)S(1)} %add.51), channel_id=1, source_target_pairs={{0,8},{4,12},{8,0},{12,4},{1,9},{5,13},{9,1},{13,5},{2,10},{6,14},... | collective-permute-start | bytes 12296 | tf_op jit(solution)/shard_map/ppermute | solution.py:22
  32.7 1.9 collective-permute-done.1
  34.6 3.1 %collective-permute-start.2 = (s32[8,128]{1,0:T(8,128)S(1)}, s32[8,128]{1,0:T(8,128)S(1)}, u32[]{:S(2)}, u32[]{:S(2)}) collective-permute-start(s32[8,128]{1,0:T(8,128)S(1)} %add.52), channel_id=1, source_target_pairs={{0,2},{2,0},{1,3},{3,1},{4,6},{6,4},{5,7},{7,5},{8,10},{10,8},{9,1... | collective-permute-start | bytes 12296 | tf_op jit(solution)/shard_map/ppermute | solution.py:22
  37.7 2.4 %collective-permute-done.2 = s32[8,128]{1,0:T(8,128)S(1)} collective-permute-done((s32[8,128]{1,0:T(8,128)S(1)}, s32[8,128]{1,0:T(8,128)S(1)}, u32[]{:S(2)}, u32[]{:S(2)}) %collective-permute-start.2) | collective-permute-done | bytes 4128 | tf_op jit(solution)/shard_map/ppermute | solution.py:22
  40.1 3.8 %collective-permute-start.3 = (s32[8,128]{1,0:T(8,128)S(1)}, s32[8,128]{1,0:T(8,128)S(1)}, u32[]{:S(2)}, u32[]{:S(2)}) collective-permute-start(s32[8,128]{1,0:T(8,128)S(1)} %add.53), channel_id=1, source_target_pairs={{0,16},{16,0},{32,48},{48,32},{64,80},{80,64},{96,112},{112,96},{1... | collective-permute-start | bytes 12296 | tf_op jit(solution)/shard_map/ppermute | solution.py:22
  45.6 5.2 %collective-permute-start.4 = (s32[8,128]{1,0:T(8,128)S(1)}, s32[8,128]{1,0:T(8,128)S(1)}, u32[]{:S(2)}, u32[]{:S(2)}) collective-permute-start(s32[8,128]{1,0:T(8,128)S(1)} %add.54), channel_id=1, source_target_pairs={{0,32},{16,48},{32,0},{48,16},{64,96},{80,112},{96,64},{112,80},{1... | collective-permute-start | bytes 12296 | tf_op jit(solution)/shard_map/ppermute | solution.py:22
  52.4 8.7 %collective-permute-start.5 = (s32[8,128]{1,0:T(8,128)S(1)}, s32[8,128]{1,0:T(8,128)S(1)}, u32[]{:S(2)}, u32[]{:S(2)}) collective-permute-start(s32[8,128]{1,0:T(8,128)S(1)} %add.55), channel_id=1, source_target_pairs={{0,64},{16,80},{32,96},{48,112},{64,0},{80,16},{96,32},{112,48},{1... | collective-permute-start | bytes 12296 | tf_op jit(solution)/shard_map/ppermute | solution.py:22
  68.3 8.4 %shard_map.123.own_ref.values_ref = bf16[256,128]{1,0:T(8,128)(2,1)} custom-call(s32[1]{0:T(128)S(6)} %sub.39.active_ref, bf16[256,3584]{1,0:T(8,128)(2,1)} %copy-done, bf16[896,3584]{1,0:T(8,128)(2,1)} %bitcast.31, bf16[4,7,64,64]{3,2,1,0:T(8,128)(2,1)} %bitcast.43), custom_call_target="tpu_custom_call" | custom-call | tf_op jit(solution)/shard_map/pallas_call | solution.py:247
  76.7 5.2 %shard_map.126 = (bf16[896,384]{1,0:T(8,128)(2,1)}, bf16[896,384]{1,0:T(8,128)(2,1)}, bf16[896,384]{1,0:T(8,128)(2,1)}, bf16[896,384]{1,0:T(8,128)(2,1)}) custom-call(s32[1]{0:T(128)S(6)} %sub.39.active_ref, s32[1]{0:T(128)} %bitcast.17.y_ref, bf16[256,3584]{1,0:T(8,128)(2,1)} %copy-done, f32[256,1]{1,0:T(8,128)} %reshape.138.weight_ref, ...), custom_call_target="tpu_custom_call" | custom-call | tf_op jit(solution)/shard_map/pallas_call | solution.py:292
  81.8 3.5 %collective-permute-start.16 = (bf16[896,384]{1,0:T(8,128)(2,1)}, bf16[896,384]{1,0:T(8,128)(2,1)S(1)}, u32[]{:S(2)}, u32[]{:S(2)}) collective-permute-start(bf16[896,384]{1,0:T(8,128)(2,1)} %get-tuple-element.44), channel_id=1, source_target_pairs={{0,4},{4,8},{8,12},{12,0},{1,5},{5,9},{9,13},{13,1},{2,6},{6,10},{... | collective-permute-start | bytes 2064392 | tf_op jit(solution)/shard_map/ppermute | solution.py:309
  88.5 3.9 %collective-permute-start.17 = (bf16[896,384]{1,0:T(8,128)(2,1)}, bf16[896,384]{1,0:T(8,128)(2,1)S(1)}, u32[]{:S(2)}, u32[]{:S(2)}) collective-permute-start(bf16[896,384]{1,0:T(8,128)(2,1)} %get-tuple-element.45), channel_id=1, source_target_pairs={{0,8},{4,12},{8,0},{12,4},{1,9},{5,13},{9,1},{13,5},{2,10},{6,14},... | collective-permute-start | bytes 2064392 | tf_op jit(solution)/shard_map/ppermute | solution.py:309
  92.4 3.7 %collective-permute-start.18 = (bf16[896,384]{1,0:T(8,128)(2,1)}, bf16[896,384]{1,0:T(8,128)(2,1)S(1)}, u32[]{:S(2)}, u32[]{:S(2)}) collective-permute-start(bf16[896,384]{1,0:T(8,128)(2,1)} %get-tuple-element.46), channel_id=1, source_target_pairs={{0,12},{4,0},{8,4},{12,8},{1,13},{5,1},{9,5},{13,9},{2,14},{6,2},{... | collective-permute-start | bytes 2064392 | tf_op jit(solution)/shard_map/ppermute | solution.py:309
  96.1 15.8 %collective-permute-done.19.refs_9_ = bf16[256,896]{1,0:T(8,128)(2,1)S(1)} collective-permute-done((bf16[256,896]{1,0:T(8,128)(2,1)S(1)}, bf16[256,896]{1,0:T(8,128)(2,1)S(1)}, u32[]{:S(2)}, u32[]{:S(2)}) %collective-permute-start.19) | collective-permute-done | bytes 458784 | tf_op jit(solution)/shard_map/ppermute | solution.py:241
  112.8 1.9 %collective-permute-start.11 = (bf16[256,128]{1,0:T(8,128)(2,1)S(1)}, bf16[256,128]{1,0:T(8,128)(2,1)}, u32[]{:S(2)}, u32[]{:S(2)}) collective-permute-start(bf16[256,128]{1,0:T(8,128)(2,1)S(1)} %copy-done.9), channel_id=1, source_target_pairs={{0,1},{1,0},{2,3},{3,2},{4,5},{5,4},{6,7},{7,6},{8,9},{9,8},{10,11... | collective-permute-start | bytes 196616 | tf_op jit(solution)/shard_map/ppermute | solution.py:302
  114.7 3.7 %shard_map.125 = (bf16[896,384]{1,0:T(8,128)(2,1)}, bf16[896,384]{1,0:T(8,128)(2,1)}, bf16[896,384]{1,0:T(8,128)(2,1)}, bf16[896,384]{1,0:T(8,128)(2,1)}) custom-call(s32[1]{0:T(128)} %bitcast.active_ref.upper_ref, s32[1]{0:T(128)} %bitcast.17.y_ref, bf16[256,3584]{1,0:T(8,128)(2,1)} %bitcast_select_fusion.dy_ref, f32[256,1]{1,0:T(8,128)} %reshape.138.weight_ref, ...), custom_call_target="tpu_custom_call" | custom-call | tf_op jit(solution)/shard_map/pallas_call | solution.py:292
  123.6 4.9 %collective-permute-done.17.refs_6_ = bf16[896,384]{1,0:T(8,128)(2,1)S(1)} collective-permute-done((bf16[896,384]{1,0:T(8,128)(2,1)}, bf16[896,384]{1,0:T(8,128)(2,1)S(1)}, u32[]{:S(2)}, u32[]{:S(2)}) %collective-permute-start.17) | collective-permute-done | bytes 688160 | tf_op jit(solution)/shard_map/ppermute | solution.py:309
  128.5 2.6 %collective-permute-start.12 = (bf16[3584,128]{1,0:T(8,128)(2,1)S(1)}, bf16[3584,128]{1,0:T(8,128)(2,1)}, u32[]{:S(2)}, u32[]{:S(2)}) collective-permute-start(bf16[3584,128]{1,0:T(8,128)(2,1)S(1)} %bitcast.39), channel_id=1, source_target_pairs={{0,3},{3,0},{1,2},{2,1},{4,7},{7,4},{5,6},{6,5},{8,11},{11,8},{9,1... | collective-permute-start | bytes 2752520 | tf_op jit(solution)/shard_map/ppermute | solution.py:227
  131.1 5.9 %collective-permute-done.21.refs_11_ = bf16[256,896]{1,0:T(8,128)(2,1)} collective-permute-done((bf16[256,896]{1,0:T(8,128)(2,1)S(1)}, bf16[256,896]{1,0:T(8,128)(2,1)}, u32[]{:S(2)}, u32[]{:S(2)}) %collective-permute-start.21) | collective-permute-done | bytes 458784 | tf_op jit(solution)/shard_map/ppermute | solution.py:241
  137.1 6.5 %shard_map.127 = (bf16[4,56,1024]{2,1,0:T(8,128)(2,1)}, bf16[4,56,1024]{2,1,0:T(8,128)(2,1)}, bf16[4,56,1024]{2,1,0:T(8,128)(2,1)}, bf16[4,56,1024]{2,1,0:T(8,128)(2,1)}) custom-call(s32[1]{0:T(128)} %bitcast.active_ref.upper_ref, s32[1]{0:T(128)} %bitcast.16.own_ref, bf16[896,384]{1,0:T(8,128)(2,1)} %get-tuple-element.39.refs_0_, ...), custom_call_target="tpu_custom_call" | custom-call | tf_op jit(solution)/shard_map/pallas_call | solution.py:354
  147.2 8.6 %collective-permute-done.22.b_ref = bf16[4,56,1024]{2,1,0:T(8,128)(2,1)S(1)} collective-permute-done((bf16[4,56,1024]{2,1,0:T(8,128)(2,1)}, bf16[4,56,1024]{2,1,0:T(8,128)(2,1)S(1)}, u32[]{:S(2)}, u32[]{:S(2)}) %collective-permute-start.22) | collective-permute-done | bytes 458784 | tf_op jit(solution)/shard_map/ppermute | solution.py:29
  155.8 6.1 %collective-permute-done.24.d_ref = bf16[4,56,1024]{2,1,0:T(8,128)(2,1)S(1)} collective-permute-done((bf16[4,56,1024]{2,1,0:T(8,128)(2,1)}, bf16[4,56,1024]{2,1,0:T(8,128)(2,1)S(1)}, u32[]{:S(2)}, u32[]{:S(2)}) %collective-permute-start.24) | collective-permute-done | bytes 458784 | tf_op jit(solution)/shard_map/ppermute | solution.py:29
  162.7 2.4 %shard_map.128 = (f32[56,1024]{1,0:T(8,128)}, bf16[56,1024]{1,0:T(8,128)(2,1)}, bf16[56,1024]{1,0:T(8,128)(2,1)}, bf16[56,1024]{1,0:T(8,128)(2,1)}) custom-call(s32[1]{0:T(128)} %bitcast.15.own_ref, bf16[4,56,1024]{2,1,0:T(8,128)(2,1)} %get-tuple-element.51.a_ref, bf16[4,56,1024]{2,1,0:T(8,128)(2,1)} %copy-done.12, bf16[4,56,1024]{2,1,0:T(8,128)(2,1)} %copy-done.13, ...), custom_call_target="tpu_custom_call" | custom-call | tf_op jit(solution)/shard_map/pallas_call | solution.py:368
  165.1 2.2 %collective-permute-start.25 = (bf16[56,1024]{1,0:T(8,128)(2,1)}, bf16[56,1024]{1,0:T(8,128)(2,1)S(1)}, u32[]{:S(2)}, u32[]{:S(2)}) collective-permute-start(bf16[56,1024]{1,0:T(8,128)(2,1)} %get-tuple-element.56), channel_id=1, source_target_pairs={{0,32},{2,34},{16,48},{18,50},{32,0},{34,2},{48,16},{50,18},{64,96... | collective-permute-start | bytes 344072 | tf_op jit(solution)/shard_map/ppermute | solution.py:29
  167.2 6.1 %collective-permute-start.26 = (bf16[56,1024]{1,0:T(8,128)(2,1)}, bf16[56,1024]{1,0:T(8,128)(2,1)S(1)}, u32[]{:S(2)}, u32[]{:S(2)}) collective-permute-start(bf16[56,1024]{1,0:T(8,128)(2,1)} %get-tuple-element.57), channel_id=1, source_target_pairs={{0,64},{2,66},{16,80},{18,82},{32,96},{34,98},{48,112},{50,114},{6... | collective-permute-start | bytes 344072 | tf_op jit(solution)/shard_map/ppermute | solution.py:29
  175.6 4.8 %shard_map.124 = bf16[128,3584]{1,0:T(8,128)(2,1)} custom-call(s32[1]{0:T(128)S(6)} %sub.39.active_ref, s32[1]{0:T(128)} %bitcast.1.tensor_ref, bf16[256,128]{1,0:T(8,128)(2,1)} %shard_map.123.own_ref.values_ref, bf16[256,128]{1,0:T(8,128)(2,1)} %collective-permute-done.11.other_ref, bf16[3584,128]{1,0:T(8,128)(2,1)} %bitcast.37, ...), custom_call_target="tpu_custom_call" | custom-call | tf_op jit(solution)/shard_map/pallas_call | solution.py:272
  181.2 1.9 shard_map.129
  184.8 2.4 %multiply_convert_fusion = bf16[1,2,1,64,3584]{4,3,2,1,0:T(8,128)(2,1)} fusion(bf16[1,2,1,64,3584]{4,3,2,1,0:T(8,128)(2,1)} %bitcast.44, bf16[2,2,64,3584]{3,2,1,0:T(8,128)(2,1)S(1)} %bitcast.40, s32[]{:T(128)S(6)} %select_n.67, f32[2]{0:T(128)S(1)} %dynamic-slice_reduce_fusion, pred[]{:T(512)S(6)} %eq.8), kind=kLoop, calls=%fused_computation.2 | loop fusion | flops 1835008 | bytes 2752525 | tf_op jit(solution)/shard_map/convert_element_type | solution.py:381
  (105 shorter events, 41.9 us)
Async XLA Ops:
  0.6 8.6 %collective-permute-start.6 = (bf16[2,64,3584]{2,1,0:T(8,128)(2,1)}, bf16[2,64,3584]{2,1,0:T(8,128)(2,1)S(1)}, u32[]{:S(2)}, u32[]{:S(2)}) collective-permute-start(bf16[2,64,3584]{2,1,0:T(8,128)(2,1)} %bitcast.45), channel_id=1, source_target_pairs={{128,129},{129,128},{130,131},{131,130},{132,133},{133,132},{134,1... | collective-permute-start | bytes 2752520 | tf_op jit(solution)/shard_map/ppermute | solution.py:201
  10.7 5.0 %collective-permute-start.8 = (bf16[3584,128]{1,0:T(8,128)(2,1)S(1)}, bf16[3584,128]{1,0:T(8,128)(2,1)S(1)}, u32[]{:S(2)}, u32[]{:S(2)}) collective-permute-start(bf16[3584,128]{1,0:T(8,128)(2,1)S(1)} %bitcast.38), channel_id=1, source_target_pairs={{128,131},{131,128},{129,130},{130,129},{132,135},{135,132},{133,1... | collective-permute-start | bytes 2752520 | tf_op jit(solution)/shard_map/ppermute | solution.py:227
  15.0 0.7 collective-permute-start.7
  16.6 49.3 %copy-start.19 = (f32[2,2]{1,0:T(2,128)S(1)}, f32[2,2]{1,0:T(2,128)}, u32[]{:S(2)}) copy-start(f32[2,2]{1,0:T(2,128)} %param.16) | copy-start | bytes 52
  20.1 46.9 %collective-permute-start.10 = (bf16[256,3584]{1,0:T(8,128)(2,1)}, bf16[256,3584]{1,0:T(8,128)(2,1)S(1)}, u32[]{:S(2)}, u32[]{:S(2)}) collective-permute-start(bf16[256,3584]{1,0:T(8,128)(2,1)} %shard_map.122), channel_id=1, source_target_pairs={{128,0},{129,1},{130,2},{131,3},{132,4},{133,5},{134,6},{135,7},{1... | collective-permute-start | bytes 5505032 | tf_op jit(solution)/shard_map/ppermute | solution.py:326
  22.1 5.5 %collective-permute-start = (s32[8,128]{1,0:T(8,128)S(1)}, s32[8,128]{1,0:T(8,128)S(1)}, u32[]{:S(2)}, u32[]{:S(2)}) collective-permute-start(s32[8,128]{1,0:T(8,128)S(1)} %broadcast_in_dim.16), channel_id=1, source_target_pairs={{0,4},{4,0},{8,12},{12,8},{1,5},{5,1},{9,13},{13,9},{2,6},{6,2},{1... | collective-permute-start | bytes 12296 | tf_op jit(solution)/shard_map/ppermute | solution.py:22
  27.6 7.0 %collective-permute-start.1 = (s32[8,128]{1,0:T(8,128)S(1)}, s32[8,128]{1,0:T(8,128)S(1)}, u32[]{:S(2)}, u32[]{:S(2)}) collective-permute-start(s32[8,128]{1,0:T(8,128)S(1)} %add.51), channel_id=1, source_target_pairs={{0,8},{4,12},{8,0},{12,4},{1,9},{5,13},{9,1},{13,5},{2,10},{6,14},... | collective-permute-start | bytes 12296 | tf_op jit(solution)/shard_map/ppermute | solution.py:22
  34.6 5.5 %collective-permute-start.2 = (s32[8,128]{1,0:T(8,128)S(1)}, s32[8,128]{1,0:T(8,128)S(1)}, u32[]{:S(2)}, u32[]{:S(2)}) collective-permute-start(s32[8,128]{1,0:T(8,128)S(1)} %add.52), channel_id=1, source_target_pairs={{0,2},{2,0},{1,3},{3,1},{4,6},{6,4},{5,7},{7,5},{8,10},{10,8},{9,1... | collective-permute-start | bytes 12296 | tf_op jit(solution)/shard_map/ppermute | solution.py:22
  40.1 5.5 %collective-permute-start.3 = (s32[8,128]{1,0:T(8,128)S(1)}, s32[8,128]{1,0:T(8,128)S(1)}, u32[]{:S(2)}, u32[]{:S(2)}) collective-permute-start(s32[8,128]{1,0:T(8,128)S(1)} %add.53), channel_id=1, source_target_pairs={{0,16},{16,0},{32,48},{48,32},{64,80},{80,64},{96,112},{112,96},{1... | collective-permute-start | bytes 12296 | tf_op jit(solution)/shard_map/ppermute | solution.py:22
  45.6 6.7 %collective-permute-start.4 = (s32[8,128]{1,0:T(8,128)S(1)}, s32[8,128]{1,0:T(8,128)S(1)}, u32[]{:S(2)}, u32[]{:S(2)}) collective-permute-start(s32[8,128]{1,0:T(8,128)S(1)} %add.54), channel_id=1, source_target_pairs={{0,32},{16,48},{32,0},{48,16},{64,96},{80,112},{96,64},{112,80},{1... | collective-permute-start | bytes 12296 | tf_op jit(solution)/shard_map/ppermute | solution.py:22
  52.4 10.3 %collective-permute-start.5 = (s32[8,128]{1,0:T(8,128)S(1)}, s32[8,128]{1,0:T(8,128)S(1)}, u32[]{:S(2)}, u32[]{:S(2)}) collective-permute-start(s32[8,128]{1,0:T(8,128)S(1)} %add.55), channel_id=1, source_target_pairs={{0,64},{16,80},{32,96},{48,112},{64,0},{80,16},{96,32},{112,48},{1... | collective-permute-start | bytes 12296 | tf_op jit(solution)/shard_map/ppermute | solution.py:22
  62.7 2.1 %collective-permute-start.9 = (s32[8,128]{1,0:T(8,128)S(1)}, s32[8,128]{1,0:T(8,128)S(1)}, u32[]{:S(2)}, u32[]{:S(2)}) collective-permute-start(s32[8,128]{1,0:T(8,128)S(1)} %add.56), channel_id=1, source_target_pairs={{0,128},{1,129},{2,130},{3,131},{4,132},{5,133},{6,134},{7,135},{8... | collective-permute-start | bytes 12296 | tf_op jit(solution)/shard_map/ppermute | solution.py:329
  76.7 36.1 %copy-start.9 = (bf16[256,128]{1,0:T(8,128)(2,1)S(1)}, bf16[256,128]{1,0:T(8,128)(2,1)}, u32[]{:S(2)}) copy-start(bf16[256,128]{1,0:T(8,128)(2,1)} %shard_map.123.own_ref.values_ref) | copy-start | bytes 196612
  81.8 40.2 %collective-permute-start.16 = (bf16[896,384]{1,0:T(8,128)(2,1)}, bf16[896,384]{1,0:T(8,128)(2,1)S(1)}, u32[]{:S(2)}, u32[]{:S(2)}) collective-permute-start(bf16[896,384]{1,0:T(8,128)(2,1)} %get-tuple-element.44), channel_id=1, source_target_pairs={{0,4},{4,8},{8,12},{12,0},{1,5},{5,9},{9,13},{13,1},{2,6},{6,10},{... | collective-permute-start | bytes 2064392 | tf_op jit(solution)/shard_map/ppermute | solution.py:309
  85.3 26.7 %collective-permute-start.19 = (bf16[256,896]{1,0:T(8,128)(2,1)S(1)}, bf16[256,896]{1,0:T(8,128)(2,1)S(1)}, u32[]{:S(2)}, u32[]{:S(2)}) collective-permute-start(bf16[256,896]{1,0:T(8,128)(2,1)S(1)} %copy-done.10), channel_id=1, source_target_pairs={{0,4},{4,8},{8,12},{12,0},{1,5},{5,9},{9,13},{13,1},{2,6},{6,10},{... | collective-permute-start | bytes 1376264 | tf_op jit(solution)/shard_map/ppermute | solution.py:241
  87.0 31.4 %collective-permute-start.20 = (bf16[256,896]{1,0:T(8,128)(2,1)S(1)}, bf16[256,896]{1,0:T(8,128)(2,1)}, u32[]{:S(2)}, u32[]{:S(2)}) collective-permute-start(bf16[256,896]{1,0:T(8,128)(2,1)S(1)} %copy-done.10), channel_id=1, source_target_pairs={{0,8},{4,12},{8,0},{12,4},{1,9},{5,13},{9,1},{13,5},{2,10},{6,14},... | collective-permute-start | bytes 1376264 | tf_op jit(solution)/shard_map/ppermute | solution.py:241
  88.5 39.9 %collective-permute-start.17 = (bf16[896,384]{1,0:T(8,128)(2,1)}, bf16[896,384]{1,0:T(8,128)(2,1)S(1)}, u32[]{:S(2)}, u32[]{:S(2)}) collective-permute-start(bf16[896,384]{1,0:T(8,128)(2,1)} %get-tuple-element.45), channel_id=1, source_target_pairs={{0,8},{4,12},{8,0},{12,4},{1,9},{5,13},{9,1},{13,5},{2,10},{6,14},... | collective-permute-start | bytes 2064392 | tf_op jit(solution)/shard_map/ppermute | solution.py:309
  92.4 36.1 %copy-start.2 = (bf16[1,3584,128]{2,1,0:T(8,128)(2,1)S(1)}, bf16[1,3584,128]{2,1,0:T(8,128)(2,1)}, u32[]{:S(2)}) copy-start(bf16[1,3584,128]{2,1,0:T(8,128)(2,1)} %param.12) | copy-start | bytes 2752516
  92.4 36.0 %collective-permute-start.18 = (bf16[896,384]{1,0:T(8,128)(2,1)}, bf16[896,384]{1,0:T(8,128)(2,1)S(1)}, u32[]{:S(2)}, u32[]{:S(2)}) collective-permute-start(bf16[896,384]{1,0:T(8,128)(2,1)} %get-tuple-element.46), channel_id=1, source_target_pairs={{0,12},{4,0},{8,4},{12,8},{1,13},{5,1},{9,5},{13,9},{2,14},{6,2},{... | collective-permute-start | bytes 2064392 | tf_op jit(solution)/shard_map/ppermute | solution.py:309
  112.8 7.8 %collective-permute-start.11 = (bf16[256,128]{1,0:T(8,128)(2,1)S(1)}, bf16[256,128]{1,0:T(8,128)(2,1)}, u32[]{:S(2)}, u32[]{:S(2)}) collective-permute-start(bf16[256,128]{1,0:T(8,128)(2,1)S(1)} %copy-done.9), channel_id=1, source_target_pairs={{0,1},{1,0},{2,3},{3,2},{4,5},{5,4},{6,7},{7,6},{8,9},{9,8},{10,11... | collective-permute-start | bytes 196616 | tf_op jit(solution)/shard_map/ppermute | solution.py:302
  118.4 18.7 %collective-permute-start.13 = (bf16[896,384]{1,0:T(8,128)(2,1)}, bf16[896,384]{1,0:T(8,128)(2,1)}, u32[]{:S(2)}, u32[]{:S(2)}) collective-permute-start(bf16[896,384]{1,0:T(8,128)(2,1)} %get-tuple-element.40), channel_id=1, source_target_pairs={{128,132},{132,136},{136,140},{140,128},{129,133},{133,137},{137,1... | collective-permute-start | bytes 2064392 | tf_op jit(solution)/shard_map/ppermute | solution.py:309
  120.5 16.5 %collective-permute-start.14 = (bf16[896,384]{1,0:T(8,128)(2,1)}, bf16[896,384]{1,0:T(8,128)(2,1)}, u32[]{:S(2)}, u32[]{:S(2)}) collective-permute-start(bf16[896,384]{1,0:T(8,128)(2,1)} %get-tuple-element.41), channel_id=1, source_target_pairs={{128,136},{132,140},{136,128},{140,132},{129,137},{133,141},{137,1... | collective-permute-start | bytes 2064392 | tf_op jit(solution)/shard_map/ppermute | solution.py:309
  122.0 15.0 %collective-permute-start.15 = (bf16[896,384]{1,0:T(8,128)(2,1)}, bf16[896,384]{1,0:T(8,128)(2,1)}, u32[]{:S(2)}, u32[]{:S(2)}) collective-permute-start(bf16[896,384]{1,0:T(8,128)(2,1)} %get-tuple-element.42), channel_id=1, source_target_pairs={{128,140},{132,128},{136,132},{140,136},{129,141},{133,129},{137,1... | collective-permute-start | bytes 2064392 | tf_op jit(solution)/shard_map/ppermute | solution.py:309
  128.5 8.6 %collective-permute-start.21 = (bf16[256,896]{1,0:T(8,128)(2,1)S(1)}, bf16[256,896]{1,0:T(8,128)(2,1)}, u32[]{:S(2)}, u32[]{:S(2)}) collective-permute-start(bf16[256,896]{1,0:T(8,128)(2,1)S(1)} %copy-done.10), channel_id=1, source_target_pairs={{0,12},{4,0},{8,4},{12,8},{1,13},{5,1},{9,5},{13,9},{2,14},{6,2},{... | collective-permute-start | bytes 1376264 | tf_op jit(solution)/shard_map/ppermute | solution.py:241
  128.5 47.1 %collective-permute-start.12 = (bf16[3584,128]{1,0:T(8,128)(2,1)S(1)}, bf16[3584,128]{1,0:T(8,128)(2,1)}, u32[]{:S(2)}, u32[]{:S(2)}) collective-permute-start(bf16[3584,128]{1,0:T(8,128)(2,1)S(1)} %bitcast.39), channel_id=1, source_target_pairs={{0,3},{3,0},{1,2},{2,1},{4,7},{7,4},{5,6},{6,5},{8,11},{11,8},{9,1... | collective-permute-start | bytes 2752520 | tf_op jit(solution)/shard_map/ppermute | solution.py:227
  143.6 12.2 %collective-permute-start.22 = (bf16[4,56,1024]{2,1,0:T(8,128)(2,1)}, bf16[4,56,1024]{2,1,0:T(8,128)(2,1)S(1)}, u32[]{:S(2)}, u32[]{:S(2)}) collective-permute-start(bf16[4,56,1024]{2,1,0:T(8,128)(2,1)} %get-tuple-element.52), channel_id=1, source_target_pairs={{0,2},{2,0},{16,18},{18,16},{32,34},{34,32},{48,50},{50,48},{64,66... | collective-permute-start | bytes 1376264 | tf_op jit(solution)/shard_map/ppermute | solution.py:29
  144.9 10.9 %collective-permute-start.23 = (bf16[4,56,1024]{2,1,0:T(8,128)(2,1)}, bf16[4,56,1024]{2,1,0:T(8,128)(2,1)S(1)}, u32[]{:S(2)}, u32[]{:S(2)}) collective-permute-start(bf16[4,56,1024]{2,1,0:T(8,128)(2,1)} %get-tuple-element.53), channel_id=1, source_target_pairs={{0,16},{2,18},{16,0},{18,2},{32,48},{34,50},{48,32},{50,34},{64,80... | collective-permute-start | bytes 1376264 | tf_op jit(solution)/shard_map/ppermute | solution.py:29
  146.2 15.7 %collective-permute-start.24 = (bf16[4,56,1024]{2,1,0:T(8,128)(2,1)}, bf16[4,56,1024]{2,1,0:T(8,128)(2,1)S(1)}, u32[]{:S(2)}, u32[]{:S(2)}) collective-permute-start(bf16[4,56,1024]{2,1,0:T(8,128)(2,1)} %get-tuple-element.54), channel_id=1, source_target_pairs={{0,18},{2,16},{16,2},{18,0},{32,50},{34,48},{48,34},{50,32},{64,82... | collective-permute-start | bytes 1376264 | tf_op jit(solution)/shard_map/ppermute | solution.py:29
  165.1 15.4 %collective-permute-start.25 = (bf16[56,1024]{1,0:T(8,128)(2,1)}, bf16[56,1024]{1,0:T(8,128)(2,1)S(1)}, u32[]{:S(2)}, u32[]{:S(2)}) collective-permute-start(bf16[56,1024]{1,0:T(8,128)(2,1)} %get-tuple-element.56), channel_id=1, source_target_pairs={{0,32},{2,34},{16,48},{18,50},{32,0},{34,2},{48,16},{50,18},{64,96... | collective-permute-start | bytes 344072 | tf_op jit(solution)/shard_map/ppermute | solution.py:29
  167.2 13.2 %collective-permute-start.26 = (bf16[56,1024]{1,0:T(8,128)(2,1)}, bf16[56,1024]{1,0:T(8,128)(2,1)S(1)}, u32[]{:S(2)}, u32[]{:S(2)}) collective-permute-start(bf16[56,1024]{1,0:T(8,128)(2,1)} %get-tuple-element.57), channel_id=1, source_target_pairs={{0,64},{2,66},{16,80},{18,82},{32,96},{34,98},{48,112},{50,114},{6... | collective-permute-start | bytes 344072 | tf_op jit(solution)/shard_map/ppermute | solution.py:29
  173.4 7.1 %collective-permute-start.27 = (bf16[56,1024]{1,0:T(8,128)(2,1)}, bf16[56,1024]{1,0:T(8,128)(2,1)S(1)}, u32[]{:S(2)}, u32[]{:S(2)}) collective-permute-start(bf16[56,1024]{1,0:T(8,128)(2,1)} %get-tuple-element.58), channel_id=1, source_target_pairs={{0,96},{2,98},{16,112},{18,114},{32,64},{34,66},{48,80},{50,82},{6... | collective-permute-start | bytes 344072 | tf_op jit(solution)/shard_map/ppermute | solution.py:29
  183.9 5.2 %collective-permute-start.28 = (f32[1,56]{1,0:T(1,128)S(1)}, f32[1,56]{1,0:T(1,128)S(1)}, u32[]{:S(2)}, u32[]{:S(2)}) collective-permute-start(f32[1,56]{1,0:T(1,128)S(1)} %bitcast.48), channel_id=1, source_target_pairs={{0,1},{1,0},{2,3},{3,2},{4,5},{5,4},{6,7},{7,6},{8,9},{9,8},{10,11... | collective-permute-start | bytes 680 | tf_op jit(solution)/shard_map/ppermute | solution.py:19
  (17 other events, 78.5 us)
where the time goes:
time: 192 us; the launch traced here: 190 us
  starting transfers between devices  70.4 us (37%)
  waiting for transfers between devices  55.8 us (29%)
  Pallas kernels  42.6 us (22%)
  other arithmetic  9.7 us (5%)
  local copies, waits for them, and re-layouts  9.42 us (5%)
    ppermute x6, starting transfers between devices, paired(): return lax.ppermute(block, ('pipe', axis), route)  29.4 us
    ppermute x3, waiting for transfers between devices, around(): return lax.ppermute(block, 'y', [(i, (i + shift) % NY) for i in range(NY)])  21.8 us
    ppermute x6, starting transfers between devices, sent(): got.append(lax.ppermute(blocks[s], ('pipe', 'y'), route))  15.6 us
    ppermute x6, waiting for transfers between devices, over_xz(): return lax.ppermute(block, ('z', 'x'), route)  14.8 us
    ppermute x6, starting transfers between devices, over_xz(): return lax.ppermute(block, ('z', 'x'), route)  11.9 us
    ppermute x6, waiting for transfers between devices, paired(): return lax.ppermute(block, ('pipe', axis), route)  11.1 us
    pallas_call x2, Pallas kernels, values_of(): pl.pallas_call(values_kernel, out_shape=shaped(tokens, HEAD_DIM), grid_sp...  10.4 us
    pallas_call x2, Pallas kernels, owners_of(): pl.pallas_call(owners_kernel, out_shape=(shaped(width // NY, tokens + HEA...  8.85 us
  transfers between devices with their start and end apart: 29, of which 14 were waited for; matrix products, arithmetic and copies ran while one was open for 6% of the time, Pallas kernels for 13%

commit v1 on v0

v1 whole, which is shorter than its diff:
```python
import jax
import jax.numpy as jnp
from jax import lax
from jax.experimental import pallas as pl
from jax.experimental.pallas import tpu as pltpu
from jax.sharding import Mesh, PartitionSpec as P


HEAD_DIM = 128
EPSILON = 1e-06
DPO_BETA = 0.25
LIKELIHOOD_COEF = 0.2
NZ, NY, NX, NT = 8, 4, 2, 2
F32, BF16 = jnp.float32, jnp.bfloat16


def paired(block, axis, size, distance, section=None):
    if section is None:
        return lax.ppermute(block, axis, [(i, i ^ distance) for i in range(size)])
    base = section * size
    route = [(base + i, base + (i ^ distance)) for i in range(size)]
    return lax.ppermute(block, ("pipe", axis), route)


def over_xz(block, k):
    route = [
        (z * NX + x, (z ^ (k >> 1)) * NX + (x ^ (k & 1))) for z in range(NZ) for x in range(NX)
    ]
    return lax.ppermute(block, ("z", "x"), route)


VMEM = pl.BlockSpec(memory_space=pltpu.VMEM)
SMEM = pl.BlockSpec(memory_space=pltpu.SMEM)
ANY = pl.BlockSpec(memory_space=pl.ANY)


def dot(a, b, contract):
    return lax.dot_general(a, b, (contract, ((), ())), preferred_element_type=F32)


def rms_of(x):
    return lax.rsqrt(jnp.mean(x * x, axis=-1, keepdims=True) + EPSILON)


def forward_kernel(x_ref, gain_ref, wv_ref, pattern_ref, *refs):
    mixed_ref, turned_ref, normed_t_ref = refs[-3:]
    heads, seq = pattern_ref.shape[1:3]
    x = x_ref[...].astype(F32)
    normed = (x * rms_of(x) * gain_ref[...]).astype(BF16)
    normed_t_ref[...] = normed.T
    values = dot(normed, wv_ref[...], ((1,), (0,))).astype(BF16)
    for part in range(2):
        at = slice(part * seq, (part + 1) * seq)
        pattern = pattern_ref[part].reshape(heads * seq, seq)
        turned_ref[part] = pattern.T
        mixed = dot(pattern, values[at], ((1,), (0,))).astype(BF16)
        for h in range(heads):
            mixed_ref[at, h * HEAD_DIM : (h + 1) * HEAD_DIM] = mixed[h * seq : (h + 1) * seq]


def add_values(step, dy, wo_ref, turned_refs, values_ref, mixed_ref):
    part = dot(dy, wo_ref[...], ((1,), (1,)))

    @pl.when(step == 0)
    def _():
        mixed_ref[...] = part

    @pl.when(step > 0)
    def _():
        mixed_ref[...] += part

    @pl.when(step == pl.num_programs(0) - 1)
    def _():
        per_pair, seq, depth = turned_refs[0].shape
        for n in range(per_pair * len(turned_refs)):
            at = slice(n * seq, (n + 1) * seq)
            mixed = mixed_ref[at].astype(BF16)
            stacked = jnp.concatenate(
                [mixed[:, h * HEAD_DIM : (h + 1) * HEAD_DIM] for h in range(depth // seq)], axis=0
            )
            turned = turned_refs[n // per_pair][n % per_pair]
            values_ref[at] = dot(turned, stacked, ((1,), (0,))).astype(BF16)


def upper_values_kernel(
    active_ref, tensor_ref, own_ref, other_ref, mask_ref, wo_ref, a_ref, b_ref,
    values_ref, raw_ref, mixed_ref,
):
    @pl.when(active_ref[0] == 1)
    def _():
        first = tensor_ref[0] == 0
        seq = own_ref.shape[1]
        for p in range(own_ref.shape[0]):
            own, other = own_ref[p].astype(F32), other_ref[p].astype(F32)
            for c, head in enumerate((jnp.where(first, own, other), jnp.where(first, other, own))):
                at = slice((2 * p + c) * seq, (2 * p + c + 1) * seq)
                raw_ref[at] = (mask_ref[at] * head).astype(BF16)
        step = pl.program_id(0)
        add_values(step, raw_ref[...], wo_ref, (a_ref, b_ref), values_ref, mixed_ref)


def lower_values_kernel(active_ref, dy_ref, wo_ref, a_ref, b_ref, values_ref, mixed_ref):
    @pl.when(active_ref[0] == 1)
    def _():
        step = pl.program_id(0)
        add_values(step, dy_ref[...], wo_ref, (a_ref, b_ref), values_ref, mixed_ref)


def rows_of_sequence(own_ref, other_ref, own_wv_ref, other_wv_ref, x_ref, gain_ref, dy_ref):
    first = dot(own_ref[...], own_wv_ref[...], ((1,), (1,))).astype(BF16)
    second = dot(other_ref[...], other_wv_ref[...], ((1,), (1,))).astype(BF16)
    scaled = (first.astype(F32) + second.astype(F32)) * gain_ref[...]
    x = x_ref[...].astype(F32)
    inverse = rms_of(x)
    pull = (inverse * inverse * inverse) * jnp.mean(x * scaled, axis=-1, keepdims=True)
    return dy_ref[...].astype(F32) + (inverse * scaled - x * pull)


def rows_kernel(active_ref, *refs):
    @pl.when(active_ref[0] == 1)
    def _():
        refs[-1][...] = rows_of_sequence(*refs[:-1]).astype(BF16)


def own_rows_kernel(active_ref, tensor_ref, weight_ref, done_ref, *refs):
    @pl.when(active_ref[0] == 1)
    def _():
        refs[-1][0] = (weight_ref[...] * rows_of_sequence(*refs[:-1])).astype(BF16)

    @pl.when(active_ref[0] == 0)
    def _():
        refs[-1][0] = (weight_ref[...] * done_ref[...].astype(F32)).astype(BF16)


def owners_kernel(upper_ref, y_ref, *refs):
    (upper_dy, upper_values, lower_dy, lower_values, weight_ref, a_ref, b_ref), refs = (
        refs[:7],
        refs[7:],
    )
    out_refs, turned_ref, dy_buffer, sems = refs[:NY], refs[NY], refs[NY + 1], refs[NY + 2]
    block = 896

    def turn(dy_hbm, values_ref):
        tokens, width = dy_hbm.shape
        copies = [
            pltpu.make_async_copy(
                dy_hbm.at[:, start : start + block], dy_buffer.at[n], sems.at[n]
            )
            for n, start in enumerate(range(0, width, block))
        ]
        for copy in copies:
            copy.start()
        weight = weight_ref[...]
        values = (weight * values_ref[...].astype(F32)).astype(BF16)
        half = tokens // 2
        turned_ref[:, tokens:] = (
            dot(a_ref[...], values[:half], ((1,), (0,)))
            + dot(b_ref[...], values[half:], ((1,), (0,)))
        ).astype(BF16)
        for n, copy in enumerate(copies):
            copy.wait()
            dy = (weight * dy_buffer[n].astype(F32)).astype(BF16)
            turned_ref[n * block : (n + 1) * block, :tokens] = dy.T

    @pl.when(upper_ref[0] == 1)
    def _():
        turn(upper_dy, upper_values)

    @pl.when(upper_ref[0] == 0)
    def _():
        turn(lower_dy, lower_values)

    size = out_refs[0].shape[0] // NZ
    for s, out_ref in enumerate(out_refs):
        owner = (y_ref[0] + s) % NY
        for z in range(NZ):
            start = pl.multiple_of((z * NY + owner) * size, 16)
            out_ref[z * size : (z + 1) * size] = turned_ref[pl.ds(start, size)]


def products_kernel(own_ref, *refs):
    blocks, mixed_refs, out_refs, total_ref = refs[:NY], refs[NY : 2 * NY], refs[2 * NY : -1], refs[-1]
    tokens = mixed_refs[0].shape[0]
    total_ref[:, :HEAD_DIM] = sum(b[:, tokens:].astype(F32) for b in blocks)
    total_ref[:, HEAD_DIM:] = sum(
        dot(b[:, :tokens], m[...], ((1,), (0,))) for b, m in zip(blocks, mixed_refs)
    )
    count, size = out_refs[0].shape[:2]
    for k, out_ref in enumerate(out_refs):
        for n in range(count):
            start = pl.multiple_of((n * 4 + (own_ref[0] ^ k)) * size, 8)
            out_ref[n] = total_ref[pl.ds(start, size)].astype(BF16)


def stage_kernel(own_ref, a_ref, b_ref, c_ref, d_ref, *out_refs):
    for k, out_ref in enumerate(out_refs):
        j = own_ref[0] ^ k
        total = sum(r[j].astype(F32) for r in (a_ref, b_ref, c_ref, d_ref))
        out_ref[...] = total.astype(out_ref.dtype)


def last_kernel(a_ref, b_ref, c_ref, d_ref, wv_ref, gain_ref, value_ref, output_ref, part_ref):
    total = a_ref[...] + sum(r[...].astype(F32) for r in (b_ref, c_ref, d_ref))
    value = total[:, :HEAD_DIM]
    value_ref[0] = value
    output_ref[0] = total[:, HEAD_DIM:]
    row = lax.dot_general(
        jnp.ones((8, HEAD_DIM), F32),
        wv_ref[...] * value,
        (((1,), (1,)), ((), ())),
        precision=lax.Precision.HIGHEST,
        preferred_element_type=F32,
    )
    part_ref[...] = row[:1] / gain_ref[...]


def shaped(*dims):
    return jax.ShapeDtypeStruct(dims, BF16)


def after(block, *others):
    return lax.optimization_barrier((block, *others))[0]


def section_step(
    hidden_in,
    attention_probs,
    norm_gain,
    value_weight,
    output_weight,
    head_grad,
    policy_logprob,
    reference_logprob,
    sequence_bounds,
):
    section = lax.axis_index("pipe")
    zi, yi, xi, ti = (lax.axis_index(a) for a in ("z", "y", "x", "t"))
    pairs, _, seq, width = hidden_in.shape[1:]
    heads = attention_probs.shape[3]
    tokens = pairs * 2 * seq
    gain = norm_gain[0]
    wv = value_weight[0]
    wo = output_weight[0]
    inputs = hidden_in[0]
    pattern = attention_probs[0]
    own_head = head_grad[:, 0]

    other_head = lax.ppermute(own_head, ("pipe", "t"), [(2, 3), (3, 2)])

    positions = jnp.arange(seq, dtype=jnp.int32)
    response_bool = (positions[None, None, :] >= sequence_bounds[:, 0:1, None]) & (
        positions[None, None, :] < sequence_bounds[:, 1:3, None]
    )
    ends = jnp.clip(sequence_bounds[:, :2], 0, seq)
    count = jnp.sum(jnp.maximum(ends[:, 1] - ends[:, 0], 0)).reshape(1, 1)
    count = lax.optimization_barrier(jnp.broadcast_to(count, (8, 128)))

    def exchanged(block, z, y, x):
        base = NZ * NY * NX
        route = []
        for device in range(base):
            zz, yy, xx = device // (NY * NX), device // NX % NY, device % NX
            route.append((device, ((zz ^ z) * NY + (yy ^ y)) * NX + (xx ^ x)))
        return lax.ppermute(block, ("pipe", "z", "y", "x"), route)

    for steps in (
        ((0, 0, 1), (0, 1, 0), (0, 1, 1)),
        ((1, 0, 0), (0, 2, 0), (1, 2, 0)),
        ((2, 0, 0),),
        ((4, 0, 0),),
    ):
        got = [exchanged(count, *at) for at in steps]
        count = count + sum(got)
    mask = response_bool.astype(F32)
    sequence_logprob = jnp.sum(mask * policy_logprob, axis=-1)
    margin = DPO_BETA * (
        sequence_logprob[:, 0]
        - reference_logprob[:, 0]
        - (sequence_logprob[:, 1] - reference_logprob[:, 1])
    )
    weight_pair = jax.nn.sigmoid(-margin)

    def across(block, section_id):
        pairs_xt = ((0, 3), (3, 0), (1, 2), (2, 1))
        base = section_id * 4
        route = [(base + a, base + b) for a, b in pairs_xt]
        return lax.ppermute(block, ("pipe", "x", "t"), route)

    other_wv_1 = across(wv, 1)

    x = inputs.reshape(tokens, width)
    patterns = pattern.reshape(pairs * 2, heads, seq, seq)
    half = tokens // pairs

    def forward(p, *earlier):
        return pl.pallas_call(
            forward_kernel,
            out_shape=(
                shaped(tokens, heads * HEAD_DIM),
                shaped(2, seq, heads * seq),
                shaped(width, half),
            ),
            grid=(1,),
            in_specs=[
                pl.BlockSpec((half, width), lambda i: (p, 0)),
                pl.BlockSpec((1, width), lambda i: (0, 0)),
                pl.BlockSpec((width, HEAD_DIM), lambda i: (0, 0)),
                pl.BlockSpec((2, heads, seq, seq), lambda i: (p, 0, 0, 0)),
            ]
            + [ANY] * len(earlier),
            out_specs=(
                pl.BlockSpec((half, heads * HEAD_DIM), lambda i: (p, 0)),
                pl.BlockSpec((2, seq, heads * seq), lambda i: (0, 0, 0)),
                pl.BlockSpec((width, half), lambda i: (0, 0)),
            ),
            input_output_aliases={4: 0} if earlier else {},
        )(x, norm_gain, wv, patterns, *earlier)

    mixed, turned_0, normed_0 = forward(0)
    mixed, turned_1, normed_1 = forward(1, mixed)

    def around(shift):
        return lax.ppermute(mixed, "y", [(i, (i + shift) % NY) for i in range(NY)])

    mixed_all = [mixed] + [around(s) for s in range(1, NY)]

    upper = section == 1
    is_upper = upper.astype(jnp.int32).reshape(1)
    is_lower = 1 - is_upper
    tensor = ti.astype(jnp.int32).reshape(1)
    block = width // 2

    def values_of(kernel, scalars, blocks, more):
        def along(*shape):
            rank = len(shape)
            return pl.BlockSpec(shape, lambda i, on, *_: (0,) * (rank - 1) + (i * on[0],))

        def whole(*shape):
            return pl.BlockSpec(shape, lambda i, *_: (0,) * len(shape))

        out_shape = [shaped(tokens, HEAD_DIM)] + [shaped(tokens, width)] * more
        out_specs = [whole(tokens, HEAD_DIM)] + [along(tokens, block)] * more
        in_specs = [
            along(*b.shape[:-1], block) if b.shape[-1] == width else whole(*b.shape)
            for b in blocks
        ]
        return pl.pallas_call(
            kernel,
            out_shape=out_shape,
            grid_spec=pltpu.PrefetchScalarGridSpec(
                num_scalar_prefetch=len(scalars),
                grid=(width // block,),
                in_specs=in_specs,
                out_specs=out_specs,
                scratch_shapes=[pltpu.VMEM((tokens, heads * HEAD_DIM), F32)],
            ),
        )(*scalars, *blocks)

    def whole_of(*shape):
        return pl.BlockSpec(shape, lambda n, *_: (0,) * len(shape))

    def rows_of(active, own, other, other_wv, dy):
        def pick(n, on):
            return (n * on[0], 0)

        return pl.pallas_call(
            rows_kernel,
            out_shape=shaped(tokens, width),
            grid_spec=pltpu.PrefetchScalarGridSpec(
                num_scalar_prefetch=1,
                grid=(pairs * 2,),
                in_specs=[
                    pl.BlockSpec((seq, HEAD_DIM), pick),
                    pl.BlockSpec((seq, HEAD_DIM), pick),
                    whole_of(width, HEAD_DIM),
                    whole_of(width, HEAD_DIM),
                    pl.BlockSpec((seq, width), pick),
                    whole_of(1, width),
                    pl.BlockSpec((seq, width), pick),
                ],
                out_specs=pl.BlockSpec((seq, width), pick),
            ),
        )(active, own, other, wv, other_wv, x, norm_gain, dy)

    def own_rows_of(active, weight, done, own, other, other_wv, dy):
        def pick(n, on, t):
            return ((n * 2 + t[0]) * on[0], 0)

        def mine(n, on, t):
            return (n * 2 + t[0], 0)

        return pl.pallas_call(
            own_rows_kernel,
            out_shape=shaped(1, pairs * seq, width),
            grid_spec=pltpu.PrefetchScalarGridSpec(
                num_scalar_prefetch=2,
                grid=(pairs,),
                in_specs=[
                    pl.BlockSpec((seq, 1), mine),
                    pl.BlockSpec((seq, width), lambda n, on, t: ((n * 2 + t[0]) * (1 - on[0]), 0)),
                    pl.BlockSpec((seq, HEAD_DIM), pick),
                    pl.BlockSpec((seq, HEAD_DIM), pick),
                    whole_of(width, HEAD_DIM),
                    whole_of(width, HEAD_DIM),
                    pl.BlockSpec((seq, width), pick),
                    whole_of(1, width),
                    pl.BlockSpec((seq, width), pick),
                ],
                out_specs=pl.BlockSpec((1, seq, width), lambda n, on, t: (0, n, 0)),
            ),
        )(active, tensor, weight, done, own, other, wv, other_wv, x, norm_gain, dy)

    def swapped(values, section_id):
        route = [(section_id * 2, section_id * 2 + 1), (section_id * 2 + 1, section_id * 2)]
        return lax.ppermute(values, ("pipe", "t"), route)

    columns = HEAD_DIM * (heads + 1)
    share_rows = width // (NZ * NY * NX)

    mask_column = mask.reshape(tokens, 1)
    own_1, raw = values_of(
        upper_values_kernel,
        (is_upper, tensor),
        (own_head, other_head, mask_column, wo, turned_0, turned_1),
        1,
    )
    other_1 = swapped(own_1, 1)
    rows_1 = rows_of(is_upper, own_1, other_1, other_wv_1, raw)
    incoming = lax.ppermute(rows_1, "pipe", [(1, 0)])

    count = after(count, rows_1)
    count_up = lax.ppermute(count, "pipe", [(0, 1)])
    chosen_total = jnp.where(upper, count_up, count)[0, 0]
    pair_total = pairs * NZ * NY * NX
    scale = LIKELIHOOD_COEF * jnp.asarray(pair_total, F32) / chosen_total.astype(F32)
    weights = jnp.stack([-DPO_BETA * weight_pair - scale, DPO_BETA * weight_pair], axis=1)
    weight = jnp.broadcast_to(weights[:, :, None], (pairs, 2, seq)).reshape(tokens, 1)

    (own_0,) = values_of(lower_values_kernel, (is_lower,), (incoming, wo, turned_0, turned_1), 0)
    other_0 = swapped(own_0, 0)
    other_wv_0 = across(after(wv, count), 0)

    turned = pl.pallas_call(
        owners_kernel,
        out_shape=(shaped(width // NY, tokens + HEAD_DIM),) * NY,
        in_specs=[SMEM, SMEM, ANY, VMEM, ANY, VMEM, VMEM, VMEM, VMEM],
        out_specs=(VMEM,) * NY,
        scratch_shapes=[
            pltpu.VMEM((width, tokens + HEAD_DIM), BF16),
            pltpu.VMEM((4, tokens, 896), BF16),
            pltpu.SemaphoreType.DMA((4,)),
        ],
    )(
        is_upper, yi.astype(jnp.int32).reshape(1), raw, own_1, incoming, own_0, weight,
        normed_0, normed_1,
    )
    blocks = [turned[0]]
    for s in range(1, NY):
        route = [(i, (i + s) % NY) for i in range(NY)]
        blocks.append(lax.ppermute(turned[s], "y", route))

    first_own = ((zi % 2) * NX + xi).astype(jnp.int32).reshape(1)
    group = width // NY // 2

    parts = pl.pallas_call(
        products_kernel,
        out_shape=(shaped(4, share_rows, columns),) * 4,
        grid_spec=pltpu.PrefetchScalarGridSpec(
            num_scalar_prefetch=1,
            grid=(2,),
            in_specs=[pl.BlockSpec((group, tokens + HEAD_DIM), lambda i, own: (i, 0))] * NY
            + [whole_of(tokens, heads * HEAD_DIM)] * NY,
            out_specs=(pl.BlockSpec((2, share_rows, columns), lambda i, own: (i, 0, 0)),) * 4,
            scratch_shapes=[pltpu.VMEM((group, columns), F32)],
        ),
    )(first_own, *after(tuple(blocks), other_0), *mixed_all)
    got = [parts[0]] + [over_xz(parts[k], k) for k in (1, 2, 3)]
    parts = pl.pallas_call(
        stage_kernel,
        out_shape=(jax.ShapeDtypeStruct((share_rows, columns), F32),)
        + (shaped(share_rows, columns),) * 3,
        in_specs=[SMEM] + [VMEM] * 4,
        out_specs=(VMEM,) * 4,
    )((zi // 2).astype(jnp.int32).reshape(1), *got)
    got = [parts[0]] + [over_xz(parts[k], k << 2) for k in (1, 2, 3)]

    own_rows = own_rows_of(is_lower, weight, rows_1, own_0, other_0, other_wv_0, incoming)
    start = ((zi * NY + yi) * NX + xi) * share_rows
    own_wv = lax.dynamic_slice_in_dim(wv, start, share_rows, 0).astype(F32)
    own_gain = lax.dynamic_slice_in_dim(gain, start, share_rows, 0).reshape(1, share_rows)
    value_share, output_share, gain_part = pl.pallas_call(
        last_kernel,
        out_shape=(
            jax.ShapeDtypeStruct((1, share_rows, HEAD_DIM), F32),
            jax.ShapeDtypeStruct((1, share_rows, columns - HEAD_DIM), F32),
            jax.ShapeDtypeStruct((1, share_rows), F32),
        ),
        in_specs=[VMEM] * 6,
        out_specs=(VMEM,) * 3,
    )(*got, own_wv, own_gain)
    gain_rows = gain_part + paired(gain_part, "t", NT, 1)
    return own_rows.reshape(1, pairs, 1, seq, width), value_share, output_share, gain_rows


def solution(mesh):
    fine = Mesh(
        mesh.devices.reshape(2, NZ, NY, NX, NT), ("pipe", "z", "y", "x", "t")
    )
    dp = ("z", "y", "x")
    in_specs = (
        P("pipe", dp, None, None, None),
        P("pipe", dp, None, "t", None, None),
        P("pipe", None),
        P("pipe", None, "t"),
        P("pipe", "t", None),
        P(dp, "t", None, None),
        P(dp, None, None),
        P(dp, None),
        P(dp, None),
    )
    out_specs = (
        P("pipe", dp, "t", None, None),
        P("pipe", dp, "t"),
        P("pipe", dp, "t"),
        P("pipe", dp),
    )
    return jax.shard_map(section_step, mesh=fine, in_specs=in_specs, out_specs=out_specs, check_vma=False)
```

time: 192 us -> 195 us (1.016)
  the two profiles are of different devices: /device:TPU:4 before, /device:TPU:56 now
where the time goes in v1:
time: 195 us; the launch traced here: 194 us
  waiting for transfers between devices  71.1 us (36%)
  starting transfers between devices  70.2 us (36%)
  Pallas kernels  37.9 us (19%)
  local copies, waits for them, and re-layouts  10.4 us (5%)
  other arithmetic  3.15 us (2%)
    ppermute x8, starting transfers between devices, exchanged(): return lax.ppermute(block, ('pipe', 'z', 'y', 'x'), route)  32.9 us
    ppermute x6, waiting for transfers between devices, over_xz(): return lax.ppermute(block, ('z', 'x'), route)  27.7 us
    ppermute x3, waiting for transfers between devices, section_step(): blocks.append(lax.ppermute(turned[s], 'y', route))  19.7 us
    ppermute x3, waiting for transfers between devices, around(): return lax.ppermute(mixed, 'y', [(i, (i + shift) % NY) for i in range(NY)])  14.9 us
    ppermute x6, starting transfers between devices, over_xz(): return lax.ppermute(block, ('z', 'x'), route)  11 us
    pallas_call x2, Pallas kernels, values_of(): pl.pallas_call(kernel, out_shape=out_shape, grid_spec=pltpu.PrefetchScala...  8.81 us
    ppermute x8, waiting for transfers between devices, exchanged(): return lax.ppermute(block, ('pipe', 'z', 'y', 'x'), route)  7.98 us
    pallas_call x2, Pallas kernels, forward(): pl.pallas_call(forward_kernel, out_shape=(shaped(tokens, heads * HEAD_DIM...  6.68 us
  transfers between devices with their start and end apart: 28, of which 15 were waited for; matrix products, arithmetic and copies ran while one was open for 4% of the time, Pallas kernels for 13%

profile of v1, /device:TPU:56, one launch (start us, length us, event | category | flops | bytes accessed | tf_op | source)
XLA Modules:
  0.0 194.4 jit_solution(13406232775933788244)
XLA Ops:
  4.7 3.3 %shard_map.120 = (bf16[256,896]{1,0:T(8,128)(2,1)}, bf16[2,64,448]{2,1,0:T(8,128)(2,1)}, bf16[3584,128]{1,0:T(8,128)(2,1)}) custom-call(bf16[256,3584]{1,0:T(8,128)(2,1)} %bitcast.17, f32[1,3584]{1,0:T(1,128)} %refs_5_.3, bf16[3584,128]{1,0:T(8,128)(2,1)} %bitcast.24, bf16[4,7,64,64]{3,2,1,0:T(8,128)(2,1)} %bitcast.29), custom_call_target="tpu_custom_call" | custom-call | tf_op jit(solution)/shard_map/pallas_call | solution.py:296
  8.0 3.3 %shard_map.121 = (bf16[256,896]{1,0:T(8,128)(2,1)}, bf16[2,64,448]{2,1,0:T(8,128)(2,1)}, bf16[3584,128]{1,0:T(8,128)(2,1)}) custom-call(bf16[256,3584]{1,0:T(8,128)(2,1)} %bitcast.18, f32[1,3584]{1,0:T(1,128)} %refs_5_.3, bf16[3584,128]{1,0:T(8,128)(2,1)} %bitcast.25, bf16[4,7,64,64]{3,2,1,0:T(8,128)(2,1)} %bitcast.30, ...), custom_call_target="tpu_custom_call", output_to_operand_aliasing={{0}: (4, {})} | custom-call | tf_op jit(solution)/shard_map/pallas_call | solution.py:296
  12.3 3.2 %shard_map.122 = (bf16[256,128]{1,0:T(8,128)(2,1)}, bf16[256,3584]{1,0:T(8,128)(2,1)}) custom-call(s32[1]{0:T(128)} %bitcast.active_ref.upper_ref, s32[1]{0:T(128)} %bitcast.1.tensor_ref, bf16[2,64,3584]{2,1,0:T(8,128)(2,1)} %bitcast.32, bf16[2,64,3584]{2,1,0:T(8,128)(2,1)} %copy-done.3, f32[256,1]{1,0:T(8,128)} %reshape.123.mask_ref, ...), custom_call_target="tpu_custom_call" | custom-call | tf_op jit(solution)/shard_map/pallas_call | solution.py:347
  17.1 2.6 %shard_map.123.done_ref = bf16[256,3584]{1,0:T(8,128)(2,1)} custom-call(s32[1]{0:T(128)} %bitcast.active_ref.upper_ref, bf16[256,128]{1,0:T(8,128)(2,1)} %get-tuple-element.36.refs_0_.refs_1_, bf16[256,128]{1,0:T(8,128)(2,1)} %copy-done.16, bf16[3584,128]{1,0:T(8,128)(2,1)} %bitcast.26, bf16[3584,128]{1,0:T(8,128)(2,1)} %copy-done.4, ...), custom_call_target="tpu_custom_call" | custom-call | tf_op jit(solution)/shard_map/pallas_call | solution.py:366
  22.3 3.6 %collective-permute-start.2 = (s32[8,128]{1,0:T(8,128)S(1)}, s32[8,128]{1,0:T(8,128)S(1)}, u32[]{:S(2)}, u32[]{:S(2)}) collective-permute-start(s32[8,128]{1,0:T(8,128)S(1)} %broadcast_in_dim.4), channel_id=1, source_target_pairs={{0,6},{2,4},{4,2},{6,0},{8,14},{10,12},{12,10},{14,8},{16,22},{18,... | collective-permute-start | bytes 12296 | tf_op jit(solution)/shard_map/ppermute | solution.py:264
  25.9 2.4 %collective-permute-start = (s32[8,128]{1,0:T(8,128)S(1)}, s32[8,128]{1,0:T(8,128)S(1)}, u32[]{:S(2)}, u32[]{:S(2)}) collective-permute-start(s32[8,128]{1,0:T(8,128)S(1)} %broadcast_in_dim.4), channel_id=1, source_target_pairs={{0,2},{2,0},{4,6},{6,4},{8,10},{10,8},{12,14},{14,12},{16,18},{18,... | collective-permute-start | bytes 12296 | tf_op jit(solution)/shard_map/ppermute | solution.py:264
  28.3 3.2 %collective-permute-start.1 = (s32[8,128]{1,0:T(8,128)S(1)}, s32[8,128]{1,0:T(8,128)S(1)}, u32[]{:S(2)}, u32[]{:S(2)}) collective-permute-start(s32[8,128]{1,0:T(8,128)S(1)} %broadcast_in_dim.4), channel_id=1, source_target_pairs={{0,4},{2,6},{4,0},{6,2},{8,12},{10,14},{12,8},{14,10},{16,20},{18,... | collective-permute-start | bytes 12296 | tf_op jit(solution)/shard_map/ppermute | solution.py:264
  33.9 4.1 %collective-permute-start.5 = (s32[8,128]{1,0:T(8,128)S(1)}, s32[8,128]{1,0:T(8,128)S(1)}, u32[]{:S(2)}, u32[]{:S(2)}) collective-permute-start(s32[8,128]{1,0:T(8,128)S(1)} %add_add_fusion.1), channel_id=1, source_target_pairs={{0,24},{2,26},{4,28},{6,30},{8,16},{10,18},{12,20},{14,22},{16,8},... | collective-permute-start | bytes 12296 | tf_op jit(solution)/shard_map/ppermute | solution.py:264
  40.1 4.5 %collective-permute-start.4 = (s32[8,128]{1,0:T(8,128)S(1)}, s32[8,128]{1,0:T(8,128)S(1)}, u32[]{:S(2)}, u32[]{:S(2)}) collective-permute-start(s32[8,128]{1,0:T(8,128)S(1)} %add_add_fusion.1), channel_id=1, source_target_pairs={{0,8},{2,10},{4,12},{6,14},{8,0},{10,2},{12,4},{14,6},{16,24},{18,... | collective-permute-start | bytes 12296 | tf_op jit(solution)/shard_map/ppermute | solution.py:264
  44.6 2.5 %collective-permute-done.4 = s32[8,128]{1,0:T(8,128)S(1)} collective-permute-done((s32[8,128]{1,0:T(8,128)S(1)}, s32[8,128]{1,0:T(8,128)S(1)}, u32[]{:S(2)}, u32[]{:S(2)}) %collective-permute-start.4) | collective-permute-done | bytes 4128 | tf_op jit(solution)/shard_map/ppermute | solution.py:264
  47.1 5.2 %collective-permute-start.6 = (s32[8,128]{1,0:T(8,128)S(1)}, s32[8,128]{1,0:T(8,128)S(1)}, u32[]{:S(2)}, u32[]{:S(2)}) collective-permute-start(s32[8,128]{1,0:T(8,128)S(1)} %add_add_fusion), channel_id=1, source_target_pairs={{0,32},{2,34},{4,36},{6,38},{8,40},{10,42},{12,44},{14,46},{16,48}... | collective-permute-start | bytes 12296 | tf_op jit(solution)/shard_map/ppermute | solution.py:264
  53.9 7.8 %collective-permute-start.7 = (s32[8,128]{1,0:T(8,128)S(1)}, s32[8,128]{1,0:T(8,128)S(1)}, u32[]{:S(2)}, u32[]{:S(2)}) collective-permute-start(s32[8,128]{1,0:T(8,128)S(1)} %add.57), channel_id=1, source_target_pairs={{0,64},{2,66},{4,68},{6,70},{8,72},{10,74},{12,76},{14,78},{16,80}... | collective-permute-start | bytes 12296 | tf_op jit(solution)/shard_map/ppermute | solution.py:264
  68.9 5.6 %shard_map.124.refs_0_.refs_3_ = bf16[256,128]{1,0:T(8,128)(2,1)} custom-call(s32[1]{0:T(128)S(6)} %sub.33.active_ref, bf16[256,3584]{1,0:T(8,128)(2,1)} %copy-done, bf16[896,3584]{1,0:T(8,128)(2,1)} %bitcast.22, bf16[2,64,448]{2,1,0:T(8,128)(2,1)} %get-tuple-element.33.a_ref, bf16[2,64,448]{2,1,0:T(8,128)(2,1)} %get-tuple-element.35.b_ref), custom_call_target="tpu_custom_call" | custom-call | tf_op jit(solution)/shard_map/pallas_call | solution.py:347
  74.5 5.3 %shard_map.126 = (bf16[896,384]{1,0:T(8,128)(2,1)}, bf16[896,384]{1,0:T(8,128)(2,1)}, bf16[896,384]{1,0:T(8,128)(2,1)}, bf16[896,384]{1,0:T(8,128)(2,1)}) custom-call(s32[1]{0:T(128)} %bitcast.active_ref.upper_ref, s32[1]{0:T(128)} %bitcast.12.y_ref, bf16[256,3584]{1,0:T(8,128)(2,1)} %get-tuple-element.37.refs_6_.refs_0_, ...), custom_call_target="tpu_custom_call" | custom-call | tf_op jit(solution)/shard_map/pallas_call | solution.py:443
  79.8 3.1 %collective-permute-start.15 = (bf16[896,384]{1,0:T(8,128)(2,1)}, bf16[896,384]{1,0:T(8,128)(2,1)S(1)}, u32[]{:S(2)}, u32[]{:S(2)}) collective-permute-start(bf16[896,384]{1,0:T(8,128)(2,1)} %get-tuple-element.43), channel_id=1, source_target_pairs={{0,4},{4,8},{8,12},{12,0},{1,5},{5,9},{9,13},{13,1},{2,6},{6,10},{... | collective-permute-start | bytes 2064392 | tf_op jit(solution)/shard_map/ppermute | solution.py:460
  83.9 4.9 %collective-permute-start.13 = (bf16[256,128]{1,0:T(8,128)(2,1)S(1)}, bf16[256,128]{1,0:T(8,128)(2,1)S(1)}, u32[]{:S(2)}, u32[]{:S(2)}) collective-permute-start(bf16[256,128]{1,0:T(8,128)(2,1)S(1)} %copy-done.7), channel_id=1, source_target_pairs={{0,1},{1,0},{2,3},{3,2},{4,5},{5,4},{6,7},{7,6},{8,9},{9,8},{10,11... | collective-permute-start | bytes 196616 | tf_op jit(solution)/shard_map/ppermute | solution.py:415
  88.8 2.5 %collective-permute-start.18 = (bf16[256,896]{1,0:T(8,128)(2,1)S(1)}, bf16[256,896]{1,0:T(8,128)(2,1)S(1)}, u32[]{:S(2)}, u32[]{:S(2)}) collective-permute-start(bf16[256,896]{1,0:T(8,128)(2,1)S(1)} %copy-done.2), channel_id=1, source_target_pairs={{0,4},{4,8},{8,12},{12,0},{1,5},{5,9},{9,13},{13,1},{2,6},{6,10},{... | collective-permute-start | bytes 1376264 | tf_op jit(solution)/shard_map/ppermute | solution.py:323
  91.6 2.5 %collective-permute-start.19 = (bf16[256,896]{1,0:T(8,128)(2,1)S(1)}, bf16[256,896]{1,0:T(8,128)(2,1)}, u32[]{:S(2)}, u32[]{:S(2)}) collective-permute-start(bf16[256,896]{1,0:T(8,128)(2,1)S(1)} %copy-done.2), channel_id=1, source_target_pairs={{0,8},{4,12},{8,0},{12,4},{1,9},{5,13},{9,1},{13,5},{2,10},{6,14},... | collective-permute-start | bytes 1376264 | tf_op jit(solution)/shard_map/ppermute | solution.py:323
  94.1 19.7 %collective-permute-done.15.refs_1_ = bf16[896,384]{1,0:T(8,128)(2,1)S(1)} collective-permute-done((bf16[896,384]{1,0:T(8,128)(2,1)}, bf16[896,384]{1,0:T(8,128)(2,1)S(1)}, u32[]{:S(2)}, u32[]{:S(2)}) %collective-permute-start.15) | collective-permute-done | bytes 688160 | tf_op jit(solution)/shard_map/ppermute | solution.py:460
  113.8 4.7 %collective-permute-start.14 = (bf16[3584,128]{1,0:T(8,128)(2,1)S(1)}, bf16[3584,128]{1,0:T(8,128)(2,1)S(1)}, u32[]{:S(2)}, u32[]{:S(2)}) collective-permute-start(bf16[3584,128]{1,0:T(8,128)(2,1)S(1)} %bitcast.28), channel_id=1, source_target_pairs={{0,3},{3,0},{1,2},{2,1},{4,7},{7,4},{5,6},{6,5},{8,11},{11,8},{9,1... | collective-permute-start | bytes 2752520 | tf_op jit(solution)/shard_map/ppermute | solution.py:287
  118.5 11.4 %collective-permute-done.18.refs_5_ = bf16[256,896]{1,0:T(8,128)(2,1)S(1)} collective-permute-done((bf16[256,896]{1,0:T(8,128)(2,1)S(1)}, bf16[256,896]{1,0:T(8,128)(2,1)S(1)}, u32[]{:S(2)}, u32[]{:S(2)}) %collective-permute-start.18) | collective-permute-done | bytes 458784 | tf_op jit(solution)/shard_map/ppermute | solution.py:323
  129.9 3.5 %collective-permute-done.20.refs_7_ = bf16[256,896]{1,0:T(8,128)(2,1)} collective-permute-done((bf16[256,896]{1,0:T(8,128)(2,1)S(1)}, bf16[256,896]{1,0:T(8,128)(2,1)}, u32[]{:S(2)}, u32[]{:S(2)}) %collective-permute-start.20) | collective-permute-done | bytes 458784 | tf_op jit(solution)/shard_map/ppermute | solution.py:323
  133.5 5.4 %shard_map.127 = (bf16[4,56,1024]{2,1,0:T(8,128)(2,1)}, bf16[4,56,1024]{2,1,0:T(8,128)(2,1)}, bf16[4,56,1024]{2,1,0:T(8,128)(2,1)}, bf16[4,56,1024]{2,1,0:T(8,128)(2,1)}) custom-call(s32[1]{0:T(128)} %bitcast.11.own_ref, bf16[896,384]{1,0:T(8,128)(2,1)} %get-tuple-element.46.refs_0_, bf16[896,384]{1,0:T(8,128)(2,1)} %copy-done.6, ...), custom_call_target="tpu_custom_call" | custom-call | tf_op jit(solution)/shard_map/pallas_call | solution.py:465
  142.4 9.2 %collective-permute-done.21.b_ref = bf16[4,56,1024]{2,1,0:T(8,128)(2,1)S(1)} collective-permute-done((bf16[4,56,1024]{2,1,0:T(8,128)(2,1)}, bf16[4,56,1024]{2,1,0:T(8,128)(2,1)S(1)}, u32[]{:S(2)}, u32[]{:S(2)}) %collective-permute-start.21) | collective-permute-done | bytes 458784 | tf_op jit(solution)/shard_map/ppermute | solution.py:29
  151.6 2.4 %collective-permute-done.22.c_ref = bf16[4,56,1024]{2,1,0:T(8,128)(2,1)S(1)} collective-permute-done((bf16[4,56,1024]{2,1,0:T(8,128)(2,1)}, bf16[4,56,1024]{2,1,0:T(8,128)(2,1)S(1)}, u32[]{:S(2)}, u32[]{:S(2)}) %collective-permute-start.22) | collective-permute-done | bytes 458784 | tf_op jit(solution)/shard_map/ppermute | solution.py:29
  154.0 8.2 %collective-permute-done.23.d_ref = bf16[4,56,1024]{2,1,0:T(8,128)(2,1)S(1)} collective-permute-done((bf16[4,56,1024]{2,1,0:T(8,128)(2,1)}, bf16[4,56,1024]{2,1,0:T(8,128)(2,1)S(1)}, u32[]{:S(2)}, u32[]{:S(2)}) %collective-permute-start.23) | collective-permute-done | bytes 458784 | tf_op jit(solution)/shard_map/ppermute | solution.py:29
  163.0 2.3 %shard_map.128 = (f32[56,1024]{1,0:T(8,128)}, bf16[56,1024]{1,0:T(8,128)(2,1)}, bf16[56,1024]{1,0:T(8,128)(2,1)}, bf16[56,1024]{1,0:T(8,128)(2,1)}) custom-call(s32[1]{0:T(128)} %bitcast.10.own_ref, bf16[4,56,1024]{2,1,0:T(8,128)(2,1)} %get-tuple-element.51.a_ref, bf16[4,56,1024]{2,1,0:T(8,128)(2,1)} %copy-done.9, bf16[4,56,1024]{2,1,0:T(8,128)(2,1)} %copy-done.10, ...), custom_call_target="tpu_custom_call" | custom-call | tf_op jit(solution)/shard_map/pallas_call | solution.py:478
  165.3 2.9 %collective-permute-start.24 = (bf16[56,1024]{1,0:T(8,128)(2,1)}, bf16[56,1024]{1,0:T(8,128)(2,1)S(1)}, u32[]{:S(2)}, u32[]{:S(2)}) collective-permute-start(bf16[56,1024]{1,0:T(8,128)(2,1)} %get-tuple-element.56), channel_id=1, source_target_pairs={{0,32},{2,34},{16,48},{18,50},{32,0},{34,2},{48,16},{50,18},{64,96... | collective-permute-start | bytes 344072 | tf_op jit(solution)/shard_map/ppermute | solution.py:29
  168.2 4.5 %collective-permute-start.25 = (bf16[56,1024]{1,0:T(8,128)(2,1)}, bf16[56,1024]{1,0:T(8,128)(2,1)S(1)}, u32[]{:S(2)}, u32[]{:S(2)}) collective-permute-start(bf16[56,1024]{1,0:T(8,128)(2,1)} %get-tuple-element.57), channel_id=1, source_target_pairs={{0,64},{2,66},{16,80},{18,82},{32,96},{34,98},{48,112},{50,114},{6... | collective-permute-start | bytes 344072 | tf_op jit(solution)/shard_map/ppermute | solution.py:29
  178.4 4.1 %collective-permute-done.26.d_ref = bf16[56,1024]{1,0:T(8,128)(2,1)S(1)} collective-permute-done((bf16[56,1024]{1,0:T(8,128)(2,1)}, bf16[56,1024]{1,0:T(8,128)(2,1)S(1)}, u32[]{:S(2)}, u32[]{:S(2)}) %collective-permute-start.26) | collective-permute-done | bytes 114720 | tf_op jit(solution)/shard_map/ppermute | solution.py:29
  185.0 3.0 %collective-permute-start.27 = (f32[1,56]{1,0:T(1,128)}, f32[1,56]{1,0:T(1,128)S(1)}, u32[]{:S(2)}, u32[]{:S(2)}) collective-permute-start(f32[1,56]{1,0:T(1,128)} %get-tuple-element.61), channel_id=1, source_target_pairs={{0,1},{1,0},{2,3},{3,2},{4,5},{5,4},{6,7},{7,6},{8,9},{9,8},{10,11... | collective-permute-start | bytes 680 | tf_op jit(solution)/shard_map/ppermute | solution.py:19
  188.9 4.9 %shard_map.125 = bf16[1,128,3584]{2,1,0:T(8,128)(2,1)} custom-call(s32[1]{0:T(128)S(6)} %sub.33.active_ref, s32[1]{0:T(128)} %bitcast.1.tensor_ref, f32[256,1]{1,0:T(8,128)} %reshape.124.weight_ref.refs_4_, bf16[256,3584]{1,0:T(8,128)(2,1)} %shard_map.123.done_ref, bf16[256,128]{1,0:T(8,128)(2,1)} %shard_map.124.refs_0_.refs_3_, ...), custom_call_target="tpu_custom_call" | custom-call | tf_op jit(solution)/shard_map/pallas_call | solution.py:392
  (96 shorter events, 36.8 us)
Async XLA Ops:
  0.6 10.7 %collective-permute-start.8 = (bf16[2,64,3584]{2,1,0:T(8,128)(2,1)}, bf16[2,64,3584]{2,1,0:T(8,128)(2,1)S(1)}, u32[]{:S(2)}, u32[]{:S(2)}) collective-permute-start(bf16[2,64,3584]{2,1,0:T(8,128)(2,1)} %bitcast.31), channel_id=1, source_target_pairs={{128,129},{129,128},{130,131},{131,130},{132,133},{133,132},{134,1... | collective-permute-start | bytes 2752520 | tf_op jit(solution)/shard_map/ppermute | solution.py:248
  1.4 14.8 %collective-permute-start.10 = (bf16[3584,128]{1,0:T(8,128)(2,1)}, bf16[3584,128]{1,0:T(8,128)(2,1)S(1)}, u32[]{:S(2)}, u32[]{:S(2)}) collective-permute-start(bf16[3584,128]{1,0:T(8,128)(2,1)} %bitcast.23), channel_id=1, source_target_pairs={{128,131},{131,128},{129,130},{130,129},{132,135},{135,132},{133,1... | collective-permute-start | bytes 2752520 | tf_op jit(solution)/shard_map/ppermute | solution.py:287
  15.5 0.7 collective-permute-start.9
  17.1 47.5 %copy-start.18 = (f32[2,2,64]{2,1,0:T(2,128)S(1)}, f32[2,2,64]{2,1,0:T(2,128)}, u32[]{:S(2)}) copy-start(f32[2,2,64]{2,1,0:T(2,128)} %param.15) | copy-start | bytes 3076
  17.1 49.5 %copy-start.17 = (f32[2,2]{1,0:T(2,128)S(1)}, f32[2,2]{1,0:T(2,128)}, u32[]{:S(2)}) copy-start(f32[2,2]{1,0:T(2,128)} %param.16) | copy-start | bytes 52
  19.7 48.0 %collective-permute-start.12 = (bf16[256,3584]{1,0:T(8,128)(2,1)}, bf16[256,3584]{1,0:T(8,128)(2,1)S(1)}, u32[]{:S(2)}, u32[]{:S(2)}) collective-permute-start(bf16[256,3584]{1,0:T(8,128)(2,1)} %shard_map.123.done_ref), channel_id=1, source_target_pairs={{128,0},{129,1},{130,2},{131,3},{132,4},{133,5},{134,6},{135,7},{1... | collective-permute-start | bytes 5505032 | tf_op jit(solution)/shard_map/ppermute | solution.py:429
  22.3 9.2 %collective-permute-start.2 = (s32[8,128]{1,0:T(8,128)S(1)}, s32[8,128]{1,0:T(8,128)S(1)}, u32[]{:S(2)}, u32[]{:S(2)}) collective-permute-start(s32[8,128]{1,0:T(8,128)S(1)} %broadcast_in_dim.4), channel_id=1, source_target_pairs={{0,6},{2,4},{4,2},{6,0},{8,14},{10,12},{12,10},{14,8},{16,22},{18,... | collective-permute-start | bytes 12296 | tf_op jit(solution)/shard_map/ppermute | solution.py:264
  25.9 5.7 %collective-permute-start = (s32[8,128]{1,0:T(8,128)S(1)}, s32[8,128]{1,0:T(8,128)S(1)}, u32[]{:S(2)}, u32[]{:S(2)}) collective-permute-start(s32[8,128]{1,0:T(8,128)S(1)} %broadcast_in_dim.4), channel_id=1, source_target_pairs={{0,2},{2,0},{4,6},{6,4},{8,10},{10,8},{12,14},{14,12},{16,18},{18,... | collective-permute-start | bytes 12296 | tf_op jit(solution)/shard_map/ppermute | solution.py:264
  28.3 5.5 %collective-permute-start.1 = (s32[8,128]{1,0:T(8,128)S(1)}, s32[8,128]{1,0:T(8,128)S(1)}, u32[]{:S(2)}, u32[]{:S(2)}) collective-permute-start(s32[8,128]{1,0:T(8,128)S(1)} %broadcast_in_dim.4), channel_id=1, source_target_pairs={{0,4},{2,6},{4,0},{6,2},{8,12},{10,14},{12,8},{14,10},{16,20},{18,... | collective-permute-start | bytes 12296 | tf_op jit(solution)/shard_map/ppermute | solution.py:264
  33.9 10.7 %collective-permute-start.5 = (s32[8,128]{1,0:T(8,128)S(1)}, s32[8,128]{1,0:T(8,128)S(1)}, u32[]{:S(2)}, u32[]{:S(2)}) collective-permute-start(s32[8,128]{1,0:T(8,128)S(1)} %add_add_fusion.1), channel_id=1, source_target_pairs={{0,24},{2,26},{4,28},{6,30},{8,16},{10,18},{12,20},{14,22},{16,8},... | collective-permute-start | bytes 12296 | tf_op jit(solution)/shard_map/ppermute | solution.py:264
  38.0 6.6 %collective-permute-start.3 = (s32[8,128]{1,0:T(8,128)S(1)}, s32[8,128]{1,0:T(8,128)S(1)}, u32[]{:S(2)}, u32[]{:S(2)}) collective-permute-start(s32[8,128]{1,0:T(8,128)S(1)} %add_add_fusion.1), channel_id=1, source_target_pairs={{0,16},{2,18},{4,20},{6,22},{8,24},{10,26},{12,28},{14,30},{16,0},... | collective-permute-start | bytes 12296 | tf_op jit(solution)/shard_map/ppermute | solution.py:264
  40.1 7.0 %collective-permute-start.4 = (s32[8,128]{1,0:T(8,128)S(1)}, s32[8,128]{1,0:T(8,128)S(1)}, u32[]{:S(2)}, u32[]{:S(2)}) collective-permute-start(s32[8,128]{1,0:T(8,128)S(1)} %add_add_fusion.1), channel_id=1, source_target_pairs={{0,8},{2,10},{4,12},{6,14},{8,0},{10,2},{12,4},{14,6},{16,24},{18,... | collective-permute-start | bytes 12296 | tf_op jit(solution)/shard_map/ppermute | solution.py:264
  47.1 6.8 %collective-permute-start.6 = (s32[8,128]{1,0:T(8,128)S(1)}, s32[8,128]{1,0:T(8,128)S(1)}, u32[]{:S(2)}, u32[]{:S(2)}) collective-permute-start(s32[8,128]{1,0:T(8,128)S(1)} %add_add_fusion), channel_id=1, source_target_pairs={{0,32},{2,34},{4,36},{6,38},{8,40},{10,42},{12,44},{14,46},{16,48}... | collective-permute-start | bytes 12296 | tf_op jit(solution)/shard_map/ppermute | solution.py:264
  53.9 9.4 %collective-permute-start.7 = (s32[8,128]{1,0:T(8,128)S(1)}, s32[8,128]{1,0:T(8,128)S(1)}, u32[]{:S(2)}, u32[]{:S(2)}) collective-permute-start(s32[8,128]{1,0:T(8,128)S(1)} %add.57), channel_id=1, source_target_pairs={{0,64},{2,66},{4,68},{6,70},{8,72},{10,74},{12,76},{14,78},{16,80}... | collective-permute-start | bytes 12296 | tf_op jit(solution)/shard_map/ppermute | solution.py:264
  63.3 2.1 %collective-permute-start.11 = (s32[8,128]{1,0:T(8,128)S(1)}, s32[8,128]{1,0:T(8,128)S(1)}, u32[]{:S(2)}, u32[]{:S(2)}) collective-permute-start(s32[8,128]{1,0:T(8,128)S(1)} %add.58), channel_id=1, source_target_pairs={{0,128},{1,129},{2,130},{3,131},{4,132},{5,133},{6,134},{7,135},{8... | collective-permute-start | bytes 12296 | tf_op jit(solution)/shard_map/ppermute | solution.py:432
  74.5 39.3 %copy-start.1 = (bf16[1,3584,128]{2,1,0:T(8,128)(2,1)S(1)}, bf16[1,3584,128]{2,1,0:T(8,128)(2,1)}, u32[]{:S(2)}) copy-start(bf16[1,3584,128]{2,1,0:T(8,128)(2,1)} %param.12) | copy-start | bytes 2752516
  79.8 33.9 %collective-permute-start.15 = (bf16[896,384]{1,0:T(8,128)(2,1)}, bf16[896,384]{1,0:T(8,128)(2,1)S(1)}, u32[]{:S(2)}, u32[]{:S(2)}) collective-permute-start(bf16[896,384]{1,0:T(8,128)(2,1)} %get-tuple-element.43), channel_id=1, source_target_pairs={{0,4},{4,8},{8,12},{12,0},{1,5},{5,9},{9,13},{13,1},{2,6},{6,10},{... | collective-permute-start | bytes 2064392 | tf_op jit(solution)/shard_map/ppermute | solution.py:460
  82.9 30.9 %collective-permute-start.16 = (bf16[896,384]{1,0:T(8,128)(2,1)}, bf16[896,384]{1,0:T(8,128)(2,1)}, u32[]{:S(2)}, u32[]{:S(2)}) collective-permute-start(bf16[896,384]{1,0:T(8,128)(2,1)} %get-tuple-element.44), channel_id=1, source_target_pairs={{0,8},{4,12},{8,0},{12,4},{1,9},{5,13},{9,1},{13,5},{2,10},{6,14},... | collective-permute-start | bytes 2064392 | tf_op jit(solution)/shard_map/ppermute | solution.py:460
  82.9 35.6 %collective-permute-start.17 = (bf16[896,384]{1,0:T(8,128)(2,1)}, bf16[896,384]{1,0:T(8,128)(2,1)}, u32[]{:S(2)}, u32[]{:S(2)}) collective-permute-start(bf16[896,384]{1,0:T(8,128)(2,1)} %get-tuple-element.45), channel_id=1, source_target_pairs={{0,12},{4,0},{8,4},{12,8},{1,13},{5,1},{9,5},{13,9},{2,14},{6,2},{... | collective-permute-start | bytes 2064392 | tf_op jit(solution)/shard_map/ppermute | solution.py:460
  83.9 7.7 %collective-permute-start.13 = (bf16[256,128]{1,0:T(8,128)(2,1)S(1)}, bf16[256,128]{1,0:T(8,128)(2,1)S(1)}, u32[]{:S(2)}, u32[]{:S(2)}) collective-permute-start(bf16[256,128]{1,0:T(8,128)(2,1)S(1)} %copy-done.7), channel_id=1, source_target_pairs={{0,1},{1,0},{2,3},{3,2},{4,5},{5,4},{6,7},{7,6},{8,9},{9,8},{10,11... | collective-permute-start | bytes 196616 | tf_op jit(solution)/shard_map/ppermute | solution.py:415
  88.8 41.1 %collective-permute-start.18 = (bf16[256,896]{1,0:T(8,128)(2,1)S(1)}, bf16[256,896]{1,0:T(8,128)(2,1)S(1)}, u32[]{:S(2)}, u32[]{:S(2)}) collective-permute-start(bf16[256,896]{1,0:T(8,128)(2,1)S(1)} %copy-done.2), channel_id=1, source_target_pairs={{0,4},{4,8},{8,12},{12,0},{1,5},{5,9},{9,13},{13,1},{2,6},{6,10},{... | collective-permute-start | bytes 1376264 | tf_op jit(solution)/shard_map/ppermute | solution.py:323
  91.6 22.2 %copy-start.15 = (bf16[256,128]{1,0:T(8,128)(2,1)}, bf16[256,128]{1,0:T(8,128)(2,1)S(1)}, u32[]{:S(2)}) copy-start(bf16[256,128]{1,0:T(8,128)(2,1)S(1)} %collective-permute-done.13.refs_1_) | copy-start | bytes 196612
  91.6 38.4 %collective-permute-start.19 = (bf16[256,896]{1,0:T(8,128)(2,1)S(1)}, bf16[256,896]{1,0:T(8,128)(2,1)}, u32[]{:S(2)}, u32[]{:S(2)}) collective-permute-start(bf16[256,896]{1,0:T(8,128)(2,1)S(1)} %copy-done.2), channel_id=1, source_target_pairs={{0,8},{4,12},{8,0},{12,4},{1,9},{5,13},{9,1},{13,5},{2,10},{6,14},... | collective-permute-start | bytes 1376264 | tf_op jit(solution)/shard_map/ppermute | solution.py:323
  113.8 19.7 %collective-permute-start.20 = (bf16[256,896]{1,0:T(8,128)(2,1)S(1)}, bf16[256,896]{1,0:T(8,128)(2,1)}, u32[]{:S(2)}, u32[]{:S(2)}) collective-permute-start(bf16[256,896]{1,0:T(8,128)(2,1)S(1)} %copy-done.2), channel_id=1, source_target_pairs={{0,12},{4,0},{8,4},{12,8},{1,13},{5,1},{9,5},{13,9},{2,14},{6,2},{... | collective-permute-start | bytes 1376264 | tf_op jit(solution)/shard_map/ppermute | solution.py:323
  113.8 74.2 %collective-permute-start.14 = (bf16[3584,128]{1,0:T(8,128)(2,1)S(1)}, bf16[3584,128]{1,0:T(8,128)(2,1)S(1)}, u32[]{:S(2)}, u32[]{:S(2)}) collective-permute-start(bf16[3584,128]{1,0:T(8,128)(2,1)S(1)} %bitcast.28), channel_id=1, source_target_pairs={{0,3},{3,0},{1,2},{2,1},{4,7},{7,4},{5,6},{6,5},{8,11},{11,8},{9,1... | collective-permute-start | bytes 2752520 | tf_op jit(solution)/shard_map/ppermute | solution.py:287
  138.8 12.8 %collective-permute-start.21 = (bf16[4,56,1024]{2,1,0:T(8,128)(2,1)}, bf16[4,56,1024]{2,1,0:T(8,128)(2,1)S(1)}, u32[]{:S(2)}, u32[]{:S(2)}) collective-permute-start(bf16[4,56,1024]{2,1,0:T(8,128)(2,1)} %get-tuple-element.52), channel_id=1, source_target_pairs={{0,2},{2,0},{16,18},{18,16},{32,34},{34,32},{48,50},{50,48},{64,66... | collective-permute-start | bytes 1376264 | tf_op jit(solution)/shard_map/ppermute | solution.py:29
  140.4 13.6 %collective-permute-start.22 = (bf16[4,56,1024]{2,1,0:T(8,128)(2,1)}, bf16[4,56,1024]{2,1,0:T(8,128)(2,1)S(1)}, u32[]{:S(2)}, u32[]{:S(2)}) collective-permute-start(bf16[4,56,1024]{2,1,0:T(8,128)(2,1)} %get-tuple-element.53), channel_id=1, source_target_pairs={{0,16},{2,18},{16,0},{18,2},{32,48},{34,50},{48,32},{50,34},{64,80... | collective-permute-start | bytes 1376264 | tf_op jit(solution)/shard_map/ppermute | solution.py:29
  141.4 20.8 %collective-permute-start.23 = (bf16[4,56,1024]{2,1,0:T(8,128)(2,1)}, bf16[4,56,1024]{2,1,0:T(8,128)(2,1)S(1)}, u32[]{:S(2)}, u32[]{:S(2)}) collective-permute-start(bf16[4,56,1024]{2,1,0:T(8,128)(2,1)} %get-tuple-element.54), channel_id=1, source_target_pairs={{0,18},{2,16},{16,2},{18,0},{32,50},{34,48},{48,34},{50,32},{64,82... | collective-permute-start | bytes 1376264 | tf_op jit(solution)/shard_map/ppermute | solution.py:29
  165.3 10.9 %collective-permute-start.24 = (bf16[56,1024]{1,0:T(8,128)(2,1)}, bf16[56,1024]{1,0:T(8,128)(2,1)S(1)}, u32[]{:S(2)}, u32[]{:S(2)}) collective-permute-start(bf16[56,1024]{1,0:T(8,128)(2,1)} %get-tuple-element.56), channel_id=1, source_target_pairs={{0,32},{2,34},{16,48},{18,50},{32,0},{34,2},{48,16},{50,18},{64,96... | collective-permute-start | bytes 344072 | tf_op jit(solution)/shard_map/ppermute | solution.py:29
  168.2 10.1 %collective-permute-start.25 = (bf16[56,1024]{1,0:T(8,128)(2,1)}, bf16[56,1024]{1,0:T(8,128)(2,1)S(1)}, u32[]{:S(2)}, u32[]{:S(2)}) collective-permute-start(bf16[56,1024]{1,0:T(8,128)(2,1)} %get-tuple-element.57), channel_id=1, source_target_pairs={{0,64},{2,66},{16,80},{18,82},{32,96},{34,98},{48,112},{50,114},{6... | collective-permute-start | bytes 344072 | tf_op jit(solution)/shard_map/ppermute | solution.py:29
  172.7 9.7 %collective-permute-start.26 = (bf16[56,1024]{1,0:T(8,128)(2,1)}, bf16[56,1024]{1,0:T(8,128)(2,1)S(1)}, u32[]{:S(2)}, u32[]{:S(2)}) collective-permute-start(bf16[56,1024]{1,0:T(8,128)(2,1)} %get-tuple-element.58), channel_id=1, source_target_pairs={{0,96},{2,98},{16,112},{18,114},{32,64},{34,66},{48,80},{50,82},{6... | collective-permute-start | bytes 344072 | tf_op jit(solution)/shard_map/ppermute | solution.py:29
  185.0 8.9 %collective-permute-start.27 = (f32[1,56]{1,0:T(1,128)}, f32[1,56]{1,0:T(1,128)S(1)}, u32[]{:S(2)}, u32[]{:S(2)}) collective-permute-start(f32[1,56]{1,0:T(1,128)} %get-tuple-element.61), channel_id=1, source_target_pairs={{0,1},{1,0},{2,3},{3,2},{4,5},{5,4},{6,7},{7,6},{8,9},{9,8},{10,11... | collective-permute-start | bytes 680 | tf_op jit(solution)/shard_map/ppermute | solution.py:19
  (16 other events, 91.3 us)

commit v2 on v1

--- a/solution.py
+++ b/solution.py
@@ -42,12 +42,22 @@
     return lax.rsqrt(jnp.mean(x * x, axis=-1, keepdims=True) + EPSILON)
 
 
-def forward_kernel(x_ref, gain_ref, wv_ref, pattern_ref, *refs):
-    mixed_ref, turned_ref, normed_t_ref = refs[-3:]
+def deal(out_refs, source_ref, first_owner):
+    size = source_ref.shape[0] // (NZ * NY)
+    for s, out_ref in enumerate(out_refs):
+        owner = (first_owner + s) % NY
+        for z in range(NZ):
+            start = pl.multiple_of((z * NY + owner) * size, 16)
+            out_ref[z * size : (z + 1) * size] = source_ref[pl.ds(start, size)]
+
+
+def forward_kernel(y_ref, x_ref, gain_ref, wv_ref, pattern_ref, *refs):
+    mixed_ref, turned_ref, normed_refs, normed_t_ref = refs[-7], refs[-6], refs[-5:-1], refs[-1]
     heads, seq = pattern_ref.shape[1:3]
     x = x_ref[...].astype(F32)
     normed = (x * rms_of(x) * gain_ref[...]).astype(BF16)
     normed_t_ref[...] = normed.T
+    deal(normed_refs, normed_t_ref, y_ref[0])
     values = dot(normed, wv_ref[...], ((1,), (0,))).astype(BF16)
     for part in range(2):
         at = slice(part * seq, (part + 1) * seq)
@@ -132,13 +142,13 @@
         refs[-1][0] = (weight_ref[...] * done_ref[...].astype(F32)).astype(BF16)
 
 
+EXTRA = 16
+
+
 def owners_kernel(upper_ref, y_ref, *refs):
-    (upper_dy, upper_values, lower_dy, lower_values, weight_ref, a_ref, b_ref), refs = (
-        refs[:7],
-        refs[7:],
-    )
+    (upper_dy, upper_values, lower_dy, lower_values, weight_ref), refs = refs[:5], refs[5:]
     out_refs, turned_ref, dy_buffer, sems = refs[:NY], refs[NY], refs[NY + 1], refs[NY + 2]
-    block = 896
+    block = dy_buffer.shape[2]
 
     def turn(dy_hbm, values_ref):
         tokens, width = dy_hbm.shape
@@ -151,16 +161,17 @@
         for copy in copies:
             copy.start()
         weight = weight_ref[...]
-        values = (weight * values_ref[...].astype(F32)).astype(BF16)
-        half = tokens // 2
-        turned_ref[:, tokens:] = (
-            dot(a_ref[...], values[:half], ((1,), (0,)))
-            + dot(b_ref[...], values[half:], ((1,), (0,)))
-        ).astype(BF16)
+        high = weight.astype(BF16).astype(F32)
+        rest = jnp.zeros((EXTRA - 2, tokens), F32)
+        below = jnp.concatenate([high, weight - high, rest], axis=0).astype(BF16)
+        values_t = values_ref[...].T
+        for out_ref in out_refs:
+            rows = out_ref.shape[0]
+            out_ref[rows - EXTRA - HEAD_DIM : rows - EXTRA] = values_t
+            out_ref[rows - EXTRA :] = below
         for n, copy in enumerate(copies):
             copy.wait()
-            dy = (weight * dy_buffer[n].astype(F32)).astype(BF16)
-            turned_ref[n * block : (n + 1) * block, :tokens] = dy.T
+            turned_ref[n * block : (n + 1) * block] = dy_buffer[n].T
 
     @pl.when(upper_ref[0] == 1)
     def _():
@@ -170,21 +181,25 @@
     def _():
         turn(lower_dy, lower_values)
 
-    size = out_refs[0].shape[0] // NZ
-    for s, out_ref in enumerate(out_refs):
-        owner = (y_ref[0] + s) % NY
-        for z in range(NZ):
-            start = pl.multiple_of((z * NY + owner) * size, 16)
-            out_ref[z * size : (z + 1) * size] = turned_ref[pl.ds(start, size)]
-
-
-def products_kernel(own_ref, *refs):
-    blocks, mixed_refs, out_refs, total_ref = refs[:NY], refs[NY : 2 * NY], refs[2 * NY : -1], refs[-1]
-    tokens = mixed_refs[0].shape[0]
-    total_ref[:, :HEAD_DIM] = sum(b[:, tokens:].astype(F32) for b in blocks)
-    total_ref[:, HEAD_DIM:] = sum(
-        dot(b[:, :tokens], m[...], ((1,), (0,))) for b, m in zip(blocks, mixed_refs)
-    )
+    deal(out_refs, turned_ref, y_ref[0])
+
+
+def products_kernel(own_ref, scale_ref, *refs):
+    groups, refs = [refs[n * NY : (n + 1) * NY] for n in range(5)], refs[5 * NY :]
+    out_refs, total_ref = refs[:-1], refs[-1]
+    tokens = groups[0][0].shape[1]
+    lane = lax.broadcasted_iota(jnp.int32, (1, tokens), 1)
+    chosen = jnp.where(lane // 64 % 2 == 0, scale_ref[0], 0.0)
+    value, output = 0.0, 0.0
+    for dy_ref, values_ref, weight_ref, normed_ref, mixed_ref in zip(*groups):
+        rows = weight_ref[...].astype(F32)
+        weight = rows[0:1] + rows[1:2] - chosen
+        dy = (weight * dy_ref[...].astype(F32)).astype(BF16)
+        values_t = (weight * values_ref[...].astype(F32)).astype(BF16)
+        output = output + dot(dy, mixed_ref[...], ((1,), (0,)))
+        value = value + dot(normed_ref[...], values_t, ((1,), (1,)))
+    total_ref[:, :HEAD_DIM] = value
+    total_ref[:, HEAD_DIM:] = output
     count, size = out_refs[0].shape[:2]
     for k, out_ref in enumerate(out_refs):
         for n in range(count):
@@ -255,21 +270,17 @@
     count = jnp.sum(jnp.maximum(ends[:, 1] - ends[:, 0], 0)).reshape(1, 1)
     count = lax.optimization_barrier(jnp.broadcast_to(count, (8, 128)))
 
-    def exchanged(block, z, y, x):
+    def exchanged(block, z, y, x, section_id):
         base = NZ * NY * NX
         route = []
         for device in range(base):
             zz, yy, xx = device // (NY * NX), device // NX % NY, device % NX
-            route.append((device, ((zz ^ z) * NY + (yy ^ y)) * NX + (xx ^ x)))
+            other = ((zz ^ z) * NY + (yy ^ y)) * NX + (xx ^ x)
+            route.append((section_id * base + device, section_id * base + other))
         return lax.ppermute(block, ("pipe", "z", "y", "x"), route)
 
-    for steps in (
-        ((0, 0, 1), (0, 1, 0), (0, 1, 1)),
-        ((1, 0, 0), (0, 2, 0), (1, 2, 0)),
-        ((2, 0, 0),),
-        ((4, 0, 0),),
-    ):
-        got = [exchanged(count, *at) for at in steps]
+    for steps in (((0, 0, 1), (0, 1, 0), (0, 1, 1)), ((1, 0, 0), (0, 2, 0), (1, 2, 0))):
+        got = [exchanged(count, *at, 0) for at in steps]
         count = count + sum(got)
     mask = response_bool.astype(F32)
     sequence_logprob = jnp.sum(mask * policy_logprob, axis=-1)
@@ -292,37 +303,41 @@
     patterns = pattern.reshape(pairs * 2, heads, seq, seq)
     half = tokens // pairs
 
+    y_index = yi.astype(jnp.int32).reshape(1)
+
     def forward(p, *earlier):
         return pl.pallas_call(
             forward_kernel,
-            out_shape=(
-                shaped(tokens, heads * HEAD_DIM),
-                shaped(2, seq, heads * seq),
-                shaped(width, half),
+            out_shape=(shaped(tokens, heads * HEAD_DIM), shaped(2, seq, heads * seq))
+            + (shaped(width // NY, tokens),) * NY,
+            grid_spec=pltpu.PrefetchScalarGridSpec(
+                num_scalar_prefetch=1,
+                grid=(1,),
+                in_specs=[
+                    pl.BlockSpec((half, width), lambda i, y: (p, 0)),
+                    pl.BlockSpec((1, width), lambda i, y: (0, 0)),
+                    pl.BlockSpec((width, HEAD_DIM), lambda i, y: (0, 0)),
+                    pl.BlockSpec((2, heads, seq, seq), lambda i, y: (p, 0, 0, 0)),
+                ]
+                + [ANY] * len(earlier),
+                out_specs=(
+                    pl.BlockSpec((half, heads * HEAD_DIM), lambda i, y: (p, 0)),
+                    pl.BlockSpec((2, seq, heads * seq), lambda i, y: (0, 0, 0)),
+                )
+                + (pl.BlockSpec((width // NY, half), lambda i, y: (0, p)),) * NY,
+                scratch_shapes=[pltpu.VMEM((width, half), BF16)],
             ),
-            grid=(1,),
-            in_specs=[
-                pl.BlockSpec((half, width), lambda i: (p, 0)),
-                pl.BlockSpec((1, width), lambda i: (0, 0)),
-                pl.BlockSpec((width, HEAD_DIM), lambda i: (0, 0)),
-                pl.BlockSpec((2, heads, seq, seq), lambda i: (p, 0, 0, 0)),
-            ]
-            + [ANY] * len(earlier),
-            out_specs=(
-                pl.BlockSpec((half, heads * HEAD_DIM), lambda i: (p, 0)),
-                pl.BlockSpec((2, seq, heads * seq), lambda i: (0, 0, 0)),
-                pl.BlockSpec((width, half), lambda i: (0, 0)),
-            ),
-            input_output_aliases={4: 0} if earlier else {},
-        )(x, norm_gain, wv, patterns, *earlier)
-
-    mixed, turned_0, normed_0 = forward(0)
-    mixed, turned_1, normed_1 = forward(1, mixed)
-
-    def around(shift):
-        return lax.ppermute(mixed, "y", [(i, (i + shift) % NY) for i in range(NY)])
-
-    mixed_all = [mixed] + [around(s) for s in range(1, NY)]
+            input_output_aliases={5: 0, 6: 2, 7: 3, 8: 4, 9: 5} if earlier else {},
+        )(y_index, x, norm_gain, wv, patterns, *earlier)
+
+    mixed, turned_0, *normed = forward(0)
+    mixed, turned_1, *normed = forward(1, mixed, *normed)
+
+    def around(block, shift):
+        return lax.ppermute(block, "y", [(i, (i + shift) % NY) for i in range(NY)])
+
+    mixed_all = [mixed] + [around(mixed, s) for s in range(1, NY)]
+    normed_all = [normed[0]] + [around(normed[s], s) for s in range(1, NY)]
 
     upper = section == 1
     is_upper = upper.astype(jnp.int32).reshape(1)
@@ -428,36 +443,37 @@
     rows_1 = rows_of(is_upper, own_1, other_1, other_wv_1, raw)
     incoming = lax.ppermute(rows_1, "pipe", [(1, 0)])
 
-    count = after(count, rows_1)
-    count_up = lax.ppermute(count, "pipe", [(0, 1)])
-    chosen_total = jnp.where(upper, count_up, count)[0, 0]
+    partial_count = lax.ppermute(count, "pipe", [(0, 1)])
+    full_count = partial_count + exchanged(partial_count, 2, 0, 0, 1)
+    full_count = full_count + exchanged(full_count, 4, 0, 0, 1)
+    count_down = lax.ppermute(full_count, "pipe", [(1, 0)])
+    chosen_total = jnp.where(upper, full_count, count_down)[0, 0]
     pair_total = pairs * NZ * NY * NX
     scale = LIKELIHOOD_COEF * jnp.asarray(pair_total, F32) / chosen_total.astype(F32)
-    weights = jnp.stack([-DPO_BETA * weight_pair - scale, DPO_BETA * weight_pair], axis=1)
-    weight = jnp.broadcast_to(weights[:, :, None], (pairs, 2, seq)).reshape(tokens, 1)
+    bare = jnp.stack([-DPO_BETA * weight_pair, DPO_BETA * weight_pair], axis=1)
+    bare_row = jnp.broadcast_to(bare[:, :, None], (pairs, 2, seq)).reshape(1, tokens)
+    bare_row = lax.optimization_barrier(bare_row)
+    lane = lax.broadcasted_iota(jnp.int32, (1, tokens), 1)
+    weight = bare_row - jnp.where(lane // seq % 2 == 0, scale, 0.0)
+    weight = weight.reshape(tokens, 1)
 
     (own_0,) = values_of(lower_values_kernel, (is_lower,), (incoming, wo, turned_0, turned_1), 0)
     other_0 = swapped(own_0, 0)
-    other_wv_0 = across(after(wv, count), 0)
-
+    other_wv_0 = across(wv, 0)
+
+    below = HEAD_DIM + EXTRA
     turned = pl.pallas_call(
         owners_kernel,
-        out_shape=(shaped(width // NY, tokens + HEAD_DIM),) * NY,
-        in_specs=[SMEM, SMEM, ANY, VMEM, ANY, VMEM, VMEM, VMEM, VMEM],
+        out_shape=(shaped(width // NY + below, tokens),) * NY,
+        in_specs=[SMEM, SMEM, ANY, VMEM, ANY, VMEM, VMEM],
         out_specs=(VMEM,) * NY,
         scratch_shapes=[
-            pltpu.VMEM((width, tokens + HEAD_DIM), BF16),
+            pltpu.VMEM((width, tokens), BF16),
             pltpu.VMEM((4, tokens, 896), BF16),
             pltpu.SemaphoreType.DMA((4,)),
         ],
-    )(
-        is_upper, yi.astype(jnp.int32).reshape(1), raw, own_1, incoming, own_0, weight,
-        normed_0, normed_1,
-    )
-    blocks = [turned[0]]
-    for s in range(1, NY):
-        route = [(i, (i + s) % NY) for i in range(NY)]
-        blocks.append(lax.ppermute(turned[s], "y", route))
+    )(is_upper, y_index, raw, own_1, incoming, own_0, bare_row)
+    blocks = [turned[0]] + [around(turned[s], s) for s in range(1, NY)]
 
     first_own = ((zi % 2) * NX + xi).astype(jnp.int32).reshape(1)
     group = width // NY // 2
@@ -468,12 +484,20 @@
         grid_spec=pltpu.PrefetchScalarGridSpec(
             num_scalar_prefetch=1,
             grid=(2,),
-            in_specs=[pl.BlockSpec((group, tokens + HEAD_DIM), lambda i, own: (i, 0))] * NY
+            in_specs=[SMEM]
+            + [pl.BlockSpec((group, tokens), lambda i, own: (i, 0))] * NY
+            + [pl.BlockSpec((HEAD_DIM, tokens), lambda i, own: (2 * group // HEAD_DIM, 0))] * NY
+            + [pl.BlockSpec((EXTRA, tokens), lambda i, own: ((2 * group + HEAD_DIM) // EXTRA, 0))]
+            * NY
+            + [pl.BlockSpec((group, tokens), lambda i, own: (i, 0))] * NY
             + [whole_of(tokens, heads * HEAD_DIM)] * NY,
             out_specs=(pl.BlockSpec((2, share_rows, columns), lambda i, own: (i, 0, 0)),) * 4,
             scratch_shapes=[pltpu.VMEM((group, columns), F32)],
         ),
-    )(first_own, *after(tuple(blocks), other_0), *mixed_all)
+    )(
+        first_own, scale.reshape(1), *after(tuple(blocks), other_0), *blocks, *blocks,
+        *normed_all, *mixed_all,
+    )
     got = [parts[0]] + [over_xz(parts[k], k) for k in (1, 2, 3)]
     parts = pl.pallas_call(
         stage_kernel,

time: 195 us -> 186 us (0.954)
  the two profiles are of different devices: /device:TPU:56 before, /device:TPU:4 now
where the time goes in v2:
time: 186 us; the launch traced here: 183 us
  waiting for transfers between devices  74.5 us (40%)
  starting transfers between devices  57.1 us (31%)
  Pallas kernels  37.9 us (20%)
  local copies, waits for them, and re-layouts  8.92 us (5%)
  other arithmetic  3.17 us (2%)
    ppermute x6, waiting for transfers between devices, over_xz(): return lax.ppermute(block, ('z', 'x'), route)  26.4 us
    ppermute x9, waiting for transfers between devices, around(): return lax.ppermute(block, 'y', [(i, (i + shift) % NY) for i in range(NY)])  26.2 us
    ppermute x8, starting transfers between devices, exchanged(): return lax.ppermute(block, ('pipe', 'z', 'y', 'x'), route)  21.2 us
    ppermute x1, waiting for transfers between devices, section_step(): count_down = lax.ppermute(full_count, 'pipe', [(1, 0)])  14.9 us
    ppermute x9, starting transfers between devices, around(): return lax.ppermute(block, 'y', [(i, (i + shift) % NY) for i in range(NY)])  13.8 us
    ppermute x6, starting transfers between devices, over_xz(): return lax.ppermute(block, ('z', 'x'), route)  10.7 us
    pallas_call x2, Pallas kernels, values_of(): pl.pallas_call(kernel, out_shape=out_shape, grid_spec=pltpu.PrefetchScala...  8.92 us
    pallas_call x2, Pallas kernels, forward(): pl.pallas_call(forward_kernel, out_shape=(shaped(tokens, heads * HEAD_DIM...  6.77 us
  transfers between devices with their start and end apart: 32, of which 12 were waited for; matrix products, arithmetic and copies ran while one was open for 5% of the time, Pallas kernels for 19%

profile of v2, /device:TPU:4, one launch (start us, length us, event | category | flops | bytes accessed | tf_op | source)
XLA Modules:
  0.0 183.2 jit_solution(133540480737037187)
XLA Ops:
  4.7 3.3 %shard_map.120 = (bf16[256,896]{1,0:T(8,128)(2,1)}, bf16[2,64,448]{2,1,0:T(8,128)(2,1)}, bf16[896,256]{1,0:T(8,128)(2,1)}, bf16[896,256]{1,0:T(8,128)(2,1)}, bf1...) custom-call(s32[1]{0:T(128)} %bitcast.6.y_ref, bf16[256,3584]{1,0:T(8,128)(2,1)} %bitcast.20, f32[1,3584]{1,0:T(1,128)} %refs_5_.3, ...), custom_call_target="tpu_custom_call" | custom-call | tf_op jit(solution)/shard_map/pallas_call | solution.py:309
  8.0 3.4 %shard_map.121 = (bf16[256,896]{1,0:T(8,128)(2,1)}, bf16[2,64,448]{2,1,0:T(8,128)(2,1)}, bf16[896,256]{1,0:T(8,128)(2,1)}, bf16[896,256]{1,0:T(8,128)(2,1)}, bf1...) custom-call(s32[1]{0:T(128)} %bitcast.6.y_ref, ...), custom_call_target="tpu_custom_call", output_to_operand_aliasing={{0}: (5, {}), {2}: (6, {}), {3}: (7, {}), {4}: (8, {}), {5}... | custom-call | tf_op jit(solution)/shard_map/pallas_call | solution.py:309
  12.4 3.3 %shard_map.122 = (bf16[256,128]{1,0:T(8,128)(2,1)}, bf16[256,3584]{1,0:T(8,128)(2,1)}) custom-call(s32[1]{0:T(128)} %bitcast.active_ref.upper_ref, s32[1]{0:T(128)} %bitcast.1.tensor_ref, bf16[2,64,3584]{2,1,0:T(8,128)(2,1)} %bitcast.35, bf16[2,64,3584]{2,1,0:T(8,128)(2,1)} %copy-done.6, f32[256,1]{1,0:T(8,128)} %reshape.237.mask_ref, ...), custom_call_target="tpu_custom_call" | custom-call | tf_op jit(solution)/shard_map/pallas_call | solution.py:362
  17.3 2.6 %shard_map.123.done_ref = bf16[256,3584]{1,0:T(8,128)(2,1)} custom-call(s32[1]{0:T(128)} %bitcast.active_ref.upper_ref, bf16[256,128]{1,0:T(8,128)(2,1)} %get-tuple-element.44.refs_0_.refs_1_, bf16[256,128]{1,0:T(8,128)(2,1)} %copy-done.18, bf16[3584,128]{1,0:T(8,128)(2,1)} %bitcast.29, bf16[3584,128]{1,0:T(8,128)(2,1)} %copy-done.7, ...), custom_call_target="tpu_custom_call" | custom-call | tf_op jit(solution)/shard_map/pallas_call | solution.py:381
  22.5 4.1 %collective-permute-start.2 = (s32[8,128]{1,0:T(8,128)S(1)}, s32[8,128]{1,0:T(8,128)S(1)}, u32[]{:S(2)}, u32[]{:S(2)}) collective-permute-start(s32[8,128]{1,0:T(8,128)S(1)} %broadcast_in_dim.11), channel_id=1, source_target_pairs={{0,6},{2,4},{4,2},{6,0},{8,14},{10,12},{12,10},{14,8},{16,22},{18,... | collective-permute-start | bytes 12296 | tf_op jit(solution)/shard_map/ppermute | solution.py:280
  26.7 2.7 %collective-permute-start = (s32[8,128]{1,0:T(8,128)S(1)}, s32[8,128]{1,0:T(8,128)S(1)}, u32[]{:S(2)}, u32[]{:S(2)}) collective-permute-start(s32[8,128]{1,0:T(8,128)S(1)} %broadcast_in_dim.11), channel_id=1, source_target_pairs={{0,2},{2,0},{4,6},{6,4},{8,10},{10,8},{12,14},{14,12},{16,18},{18,... | collective-permute-start | bytes 12296 | tf_op jit(solution)/shard_map/ppermute | solution.py:280
  29.4 2.4 %collective-permute-start.1 = (s32[8,128]{1,0:T(8,128)S(1)}, s32[8,128]{1,0:T(8,128)S(1)}, u32[]{:S(2)}, u32[]{:S(2)}) collective-permute-start(s32[8,128]{1,0:T(8,128)S(1)} %broadcast_in_dim.11), channel_id=1, source_target_pairs={{0,4},{2,6},{4,0},{6,2},{8,12},{10,14},{12,8},{14,10},{16,20},{18,... | collective-permute-start | bytes 12296 | tf_op jit(solution)/shard_map/ppermute | solution.py:280
  34.9 6.1 %collective-permute-start.5 = (s32[8,128]{1,0:T(8,128)S(1)}, s32[8,128]{1,0:T(8,128)S(1)}, u32[]{:S(2)}, u32[]{:S(2)}) collective-permute-start(s32[8,128]{1,0:T(8,128)S(1)} %add_add_fusion.1), channel_id=1, source_target_pairs={{0,24},{2,26},{4,28},{6,30},{8,16},{10,18},{12,20},{14,22},{16,8},... | collective-permute-start | bytes 12296 | tf_op jit(solution)/shard_map/ppermute | solution.py:280
  41.1 2.0 %collective-permute-start.3 = (s32[8,128]{1,0:T(8,128)S(1)}, s32[8,128]{1,0:T(8,128)S(1)}, u32[]{:S(2)}, u32[]{:S(2)}) collective-permute-start(s32[8,128]{1,0:T(8,128)S(1)} %add_add_fusion.1), channel_id=1, source_target_pairs={{0,16},{2,18},{4,20},{6,22},{8,24},{10,26},{12,28},{14,30},{16,0},... | collective-permute-start | bytes 12296 | tf_op jit(solution)/shard_map/ppermute | solution.py:280
  43.1 2.5 %collective-permute-start.4 = (s32[8,128]{1,0:T(8,128)S(1)}, s32[8,128]{1,0:T(8,128)S(1)}, u32[]{:S(2)}, u32[]{:S(2)}) collective-permute-start(s32[8,128]{1,0:T(8,128)S(1)} %add_add_fusion.1), channel_id=1, source_target_pairs={{0,8},{2,10},{4,12},{6,14},{8,0},{10,2},{12,4},{14,6},{16,24},{18,... | collective-permute-start | bytes 12296 | tf_op jit(solution)/shard_map/ppermute | solution.py:280
  46.5 2.9 %collective-permute-start.20 = (bf16[896,256]{1,0:T(8,128)(2,1)}, bf16[896,256]{1,0:T(8,128)(2,1)}, u32[]{:S(2)}, u32[]{:S(2)}) collective-permute-start(bf16[896,256]{1,0:T(8,128)(2,1)} %get-tuple-element.56), channel_id=1, source_target_pairs={{0,8},{4,12},{8,0},{12,4},{1,9},{5,13},{9,1},{13,5},{2,10},{6,14},... | collective-permute-start | bytes 1376264 | tf_op jit(solution)/shard_map/ppermute | solution.py:337
  49.4 5.6 %shard_map.124.refs_0_.refs_3_ = bf16[256,128]{1,0:T(8,128)(2,1)} custom-call(s32[1]{0:T(128)S(6)} %sub.35.active_ref, bf16[256,3584]{1,0:T(8,128)(2,1)} %copy-done, bf16[896,3584]{1,0:T(8,128)(2,1)} %bitcast.25, bf16[2,64,448]{2,1,0:T(8,128)(2,1)} %get-tuple-element.37.a_ref, bf16[2,64,448]{2,1,0:T(8,128)(2,1)} %get-tuple-element.43.b_ref), custom_call_target="tpu_custom_call" | custom-call | tf_op jit(solution)/shard_map/pallas_call | solution.py:362
  55.0 4.2 %shard_map.126 = (bf16[1040,256]{1,0:T(8,128)(2,1)}, bf16[1040,256]{1,0:T(8,128)(2,1)}, bf16[1040,256]{1,0:T(8,128)(2,1)}, bf16[1040,256]{1,0:T(8,128)(2,1)}) custom-call(s32[1]{0:T(128)} %bitcast.active_ref.upper_ref, s32[1]{0:T(128)} %bitcast.6.y_ref, bf16[256,3584]{1,0:T(8,128)(2,1)} %get-tuple-element.45.refs_6_.refs_0_, ...), custom_call_target="tpu_custom_call" | custom-call | tf_op jit(solution)/shard_map/pallas_call | solution.py:465
  66.1 14.9 %collective-permute-done.9 = s32[8,128]{1,0:T(8,128)S(1)} collective-permute-done((s32[8,128]{1,0:T(8,128)S(1)}, s32[8,128]{1,0:T(8,128)S(1)}, u32[]{:S(2)}, u32[]{:S(2)}) %collective-permute-start.9) | collective-permute-done | bytes 4128 | tf_op jit(solution)/shard_map/ppermute | solution.py:449
  81.0 1.9 %collective-permute-start.18 = (bf16[1040,256]{1,0:T(8,128)(2,1)}, bf16[1040,256]{1,0:T(8,128)(2,1)S(1)}, u32[]{:S(2)}, u32[]{:S(2)}) collective-permute-start(bf16[1040,256]{1,0:T(8,128)(2,1)} %get-tuple-element.49), channel_id=1, source_target_pairs={{0,12},{4,0},{8,4},{12,8},{1,13},{5,1},{9,5},{13,9},{2,14},{6,2},{... | collective-permute-start | bytes 1597448 | tf_op jit(solution)/shard_map/ppermute | solution.py:337
  82.9 2.4 %collective-permute-start.14 = (bf16[256,128]{1,0:T(8,128)(2,1)S(1)}, bf16[256,128]{1,0:T(8,128)(2,1)S(1)}, u32[]{:S(2)}, u32[]{:S(2)}) collective-permute-start(bf16[256,128]{1,0:T(8,128)(2,1)S(1)} %copy-done.8), channel_id=1, source_target_pairs={{0,1},{1,0},{2,3},{3,2},{4,5},{5,4},{6,7},{7,6},{8,9},{9,8},{10,11... | collective-permute-start | bytes 196616 | tf_op jit(solution)/shard_map/ppermute | solution.py:430
  85.7 4.9 %collective-permute-done.14.refs_1_ = bf16[256,128]{1,0:T(8,128)(2,1)S(1)} collective-permute-done((bf16[256,128]{1,0:T(8,128)(2,1)S(1)}, bf16[256,128]{1,0:T(8,128)(2,1)S(1)}, u32[]{:S(2)}, u32[]{:S(2)}) %collective-permute-start.14) | collective-permute-done | bytes 65568 | tf_op jit(solution)/shard_map/ppermute | solution.py:430
  90.8 2.2 %collective-permute-start.23 = (bf16[256,896]{1,0:T(8,128)(2,1)S(1)}, bf16[256,896]{1,0:T(8,128)(2,1)}, u32[]{:S(2)}, u32[]{:S(2)}) collective-permute-start(bf16[256,896]{1,0:T(8,128)(2,1)S(1)} %copy-done.5), channel_id=1, source_target_pairs={{0,8},{4,12},{8,0},{12,4},{1,9},{5,13},{9,1},{13,5},{2,10},{6,14},... | collective-permute-start | bytes 1376264 | tf_op jit(solution)/shard_map/ppermute | solution.py:337
  93.0 2.6 %collective-permute-start.24 = (bf16[256,896]{1,0:T(8,128)(2,1)S(1)}, bf16[256,896]{1,0:T(8,128)(2,1)}, u32[]{:S(2)}, u32[]{:S(2)}) collective-permute-start(bf16[256,896]{1,0:T(8,128)(2,1)S(1)} %copy-done.5), channel_id=1, source_target_pairs={{0,12},{4,0},{8,4},{12,8},{1,13},{5,1},{9,5},{13,9},{2,14},{6,2},{... | collective-permute-start | bytes 1376264 | tf_op jit(solution)/shard_map/ppermute | solution.py:337
  96.3 2.4 %collective-permute-start.15 = (bf16[3584,128]{1,0:T(8,128)(2,1)S(1)}, bf16[3584,128]{1,0:T(8,128)(2,1)}, u32[]{:S(2)}, u32[]{:S(2)}) collective-permute-start(bf16[3584,128]{1,0:T(8,128)(2,1)S(1)} %bitcast.31), channel_id=1, source_target_pairs={{0,3},{3,0},{1,2},{2,1},{4,7},{7,4},{5,6},{6,5},{8,11},{11,8},{9,1... | collective-permute-start | bytes 2752520 | tf_op jit(solution)/shard_map/ppermute | solution.py:298
  100.0 15.2 %collective-permute-done.21.refs_15_ = bf16[896,256]{1,0:T(8,128)(2,1)S(1)} collective-permute-done((bf16[896,256]{1,0:T(8,128)(2,1)}, bf16[896,256]{1,0:T(8,128)(2,1)S(1)}, u32[]{:S(2)}, u32[]{:S(2)}) %collective-permute-start.21) | collective-permute-done | bytes 458784 | tf_op jit(solution)/shard_map/ppermute | solution.py:337
  115.2 10.3 %collective-permute-done.24.refs_19_ = bf16[256,896]{1,0:T(8,128)(2,1)} collective-permute-done((bf16[256,896]{1,0:T(8,128)(2,1)S(1)}, bf16[256,896]{1,0:T(8,128)(2,1)}, u32[]{:S(2)}, u32[]{:S(2)}) %collective-permute-start.24) | collective-permute-done | bytes 458784 | tf_op jit(solution)/shard_map/ppermute | solution.py:337
  125.4 6.2 %shard_map.127 = (bf16[4,56,1024]{2,1,0:T(8,128)(2,1)}, bf16[4,56,1024]{2,1,0:T(8,128)(2,1)}, bf16[4,56,1024]{2,1,0:T(8,128)(2,1)}, bf16[4,56,1024]{2,1,0:T(8,128)(2,1)}) custom-call(s32[1]{0:T(128)} %bitcast.13.own_ref, f32[1]{0:T(128)} %bitcast.14.scale_ref, bf16[1040,256]{1,0:T(8,128)(2,1)} %get-tuple-element.50.refs_0_.refs_4_.refs_8_, ...), custom_call_target="tpu_custom_call" | custom-call | tf_op jit(solution)/shard_map/pallas_call | solution.py:481
  135.2 9.2 %collective-permute-done.25.b_ref = bf16[4,56,1024]{2,1,0:T(8,128)(2,1)S(1)} collective-permute-done((bf16[4,56,1024]{2,1,0:T(8,128)(2,1)}, bf16[4,56,1024]{2,1,0:T(8,128)(2,1)S(1)}, u32[]{:S(2)}, u32[]{:S(2)}) %collective-permute-start.25) | collective-permute-done | bytes 458784 | tf_op jit(solution)/shard_map/ppermute | solution.py:29
  144.4 2.1 %collective-permute-done.26.c_ref = bf16[4,56,1024]{2,1,0:T(8,128)(2,1)S(1)} collective-permute-done((bf16[4,56,1024]{2,1,0:T(8,128)(2,1)}, bf16[4,56,1024]{2,1,0:T(8,128)(2,1)S(1)}, u32[]{:S(2)}, u32[]{:S(2)}) %collective-permute-start.26) | collective-permute-done | bytes 458784 | tf_op jit(solution)/shard_map/ppermute | solution.py:29
  146.5 8.4 %collective-permute-done.27.d_ref = bf16[4,56,1024]{2,1,0:T(8,128)(2,1)S(1)} collective-permute-done((bf16[4,56,1024]{2,1,0:T(8,128)(2,1)}, bf16[4,56,1024]{2,1,0:T(8,128)(2,1)S(1)}, u32[]{:S(2)}, u32[]{:S(2)}) %collective-permute-start.27) | collective-permute-done | bytes 458784 | tf_op jit(solution)/shard_map/ppermute | solution.py:29
  155.7 2.3 %shard_map.128 = (f32[56,1024]{1,0:T(8,128)}, bf16[56,1024]{1,0:T(8,128)(2,1)}, bf16[56,1024]{1,0:T(8,128)(2,1)}, bf16[56,1024]{1,0:T(8,128)(2,1)}) custom-call(s32[1]{0:T(128)} %bitcast.12.own_ref, bf16[4,56,1024]{2,1,0:T(8,128)(2,1)} %get-tuple-element.59.a_ref, bf16[4,56,1024]{2,1,0:T(8,128)(2,1)} %copy-done.10, bf16[4,56,1024]{2,1,0:T(8,128)(2,1)} %copy-done.11, ...), custom_call_target="tpu_custom_call" | custom-call | tf_op jit(solution)/shard_map/pallas_call | solution.py:502
  158.1 1.9 %collective-permute-start.28 = (bf16[56,1024]{1,0:T(8,128)(2,1)}, bf16[56,1024]{1,0:T(8,128)(2,1)S(1)}, u32[]{:S(2)}, u32[]{:S(2)}) collective-permute-start(bf16[56,1024]{1,0:T(8,128)(2,1)} %get-tuple-element.64), channel_id=1, source_target_pairs={{0,32},{2,34},{16,48},{18,50},{32,0},{34,2},{48,16},{50,18},{64,96... | collective-permute-start | bytes 344072 | tf_op jit(solution)/shard_map/ppermute | solution.py:29
  160.0 5.2 %collective-permute-start.29 = (bf16[56,1024]{1,0:T(8,128)(2,1)}, bf16[56,1024]{1,0:T(8,128)(2,1)S(1)}, u32[]{:S(2)}, u32[]{:S(2)}) collective-permute-start(bf16[56,1024]{1,0:T(8,128)(2,1)} %get-tuple-element.65), channel_id=1, source_target_pairs={{0,64},{2,66},{16,80},{18,82},{32,96},{34,98},{48,112},{50,114},{6... | collective-permute-start | bytes 344072 | tf_op jit(solution)/shard_map/ppermute | solution.py:29
  167.1 4.2 %collective-permute-done.29.c_ref = bf16[56,1024]{1,0:T(8,128)(2,1)S(1)} collective-permute-done((bf16[56,1024]{1,0:T(8,128)(2,1)}, bf16[56,1024]{1,0:T(8,128)(2,1)S(1)}, u32[]{:S(2)}, u32[]{:S(2)}) %collective-permute-start.29) | collective-permute-done | bytes 114720 | tf_op jit(solution)/shard_map/ppermute | solution.py:29
  171.4 2.4 %collective-permute-done.30.d_ref = bf16[56,1024]{1,0:T(8,128)(2,1)S(1)} collective-permute-done((bf16[56,1024]{1,0:T(8,128)(2,1)}, bf16[56,1024]{1,0:T(8,128)(2,1)S(1)}, u32[]{:S(2)}, u32[]{:S(2)}) %collective-permute-start.30) | collective-permute-done | bytes 114720 | tf_op jit(solution)/shard_map/ppermute | solution.py:29
  177.7 4.9 %shard_map.125 = bf16[1,128,3584]{2,1,0:T(8,128)(2,1)} custom-call(s32[1]{0:T(128)S(6)} %sub.35.active_ref, s32[1]{0:T(128)} %bitcast.1.tensor_ref, f32[256,1]{1,0:T(8,128)} %copy.20.weight_ref, bf16[256,3584]{1,0:T(8,128)(2,1)} %shard_map.123.done_ref, bf16[256,128]{1,0:T(8,128)(2,1)} %shard_map.124.refs_0_.refs_3_, bf16[256,128]{1,0:T(8,128)(2,1)} %copy-done.17, ...), custom_call_target="tpu_custom_call" | custom-call | tf_op jit(solution)/shard_map/pallas_call | solution.py:407
  (112 shorter events, 32.4 us)
Async XLA Ops:
  0.6 10.8 %collective-permute-start.10 = (bf16[2,64,3584]{2,1,0:T(8,128)(2,1)}, bf16[2,64,3584]{2,1,0:T(8,128)(2,1)S(1)}, u32[]{:S(2)}, u32[]{:S(2)}) collective-permute-start(bf16[2,64,3584]{2,1,0:T(8,128)(2,1)} %bitcast.34), channel_id=1, source_target_pairs={{128,129},{129,128},{130,131},{131,130},{132,133},{133,132},{134,1... | collective-permute-start | bytes 2752520 | tf_op jit(solution)/shard_map/ppermute | solution.py:263
  1.4 15.0 %collective-permute-start.12 = (bf16[3584,128]{1,0:T(8,128)(2,1)}, bf16[3584,128]{1,0:T(8,128)(2,1)S(1)}, u32[]{:S(2)}, u32[]{:S(2)}) collective-permute-start(bf16[3584,128]{1,0:T(8,128)(2,1)} %bitcast.26), channel_id=1, source_target_pairs={{128,131},{131,128},{129,130},{130,129},{132,135},{135,132},{133,1... | collective-permute-start | bytes 2752520 | tf_op jit(solution)/shard_map/ppermute | solution.py:298
  15.7 0.7 collective-permute-start.11
  19.9 26.6 %collective-permute-start.13 = (bf16[256,3584]{1,0:T(8,128)(2,1)}, bf16[256,3584]{1,0:T(8,128)(2,1)S(1)}, u32[]{:S(2)}, u32[]{:S(2)}) collective-permute-start(bf16[256,3584]{1,0:T(8,128)(2,1)} %shard_map.123.done_ref), channel_id=1, source_target_pairs={{128,0},{129,1},{130,2},{131,3},{132,4},{133,5},{134,6},{135,7},{1... | collective-permute-start | bytes 5505032 | tf_op jit(solution)/shard_map/ppermute | solution.py:444
  22.5 11.2 %collective-permute-start.2 = (s32[8,128]{1,0:T(8,128)S(1)}, s32[8,128]{1,0:T(8,128)S(1)}, u32[]{:S(2)}, u32[]{:S(2)}) collective-permute-start(s32[8,128]{1,0:T(8,128)S(1)} %broadcast_in_dim.11), channel_id=1, source_target_pairs={{0,6},{2,4},{4,2},{6,0},{8,14},{10,12},{12,10},{14,8},{16,22},{18,... | collective-permute-start | bytes 12296 | tf_op jit(solution)/shard_map/ppermute | solution.py:280
  26.7 7.0 %collective-permute-start = (s32[8,128]{1,0:T(8,128)S(1)}, s32[8,128]{1,0:T(8,128)S(1)}, u32[]{:S(2)}, u32[]{:S(2)}) collective-permute-start(s32[8,128]{1,0:T(8,128)S(1)} %broadcast_in_dim.11), channel_id=1, source_target_pairs={{0,2},{2,0},{4,6},{6,4},{8,10},{10,8},{12,14},{14,12},{16,18},{18,... | collective-permute-start | bytes 12296 | tf_op jit(solution)/shard_map/ppermute | solution.py:280
  29.4 5.5 %collective-permute-start.1 = (s32[8,128]{1,0:T(8,128)S(1)}, s32[8,128]{1,0:T(8,128)S(1)}, u32[]{:S(2)}, u32[]{:S(2)}) collective-permute-start(s32[8,128]{1,0:T(8,128)S(1)} %broadcast_in_dim.11), channel_id=1, source_target_pairs={{0,4},{2,6},{4,0},{6,2},{8,12},{10,14},{12,8},{14,10},{16,20},{18,... | collective-permute-start | bytes 12296 | tf_op jit(solution)/shard_map/ppermute | solution.py:280
  31.8 51.1 %collective-permute-start.19 = (bf16[896,256]{1,0:T(8,128)(2,1)S(1)}, bf16[896,256]{1,0:T(8,128)(2,1)}, u32[]{:S(2)}, u32[]{:S(2)}) collective-permute-start(bf16[896,256]{1,0:T(8,128)(2,1)S(1)} %copy-done.9), channel_id=1, source_target_pairs={{0,4},{4,8},{8,12},{12,0},{1,5},{5,9},{9,13},{13,1},{2,6},{6,10},{... | collective-permute-start | bytes 1376264 | tf_op jit(solution)/shard_map/ppermute | solution.py:337
  34.9 24.3 %collective-permute-start.5 = (s32[8,128]{1,0:T(8,128)S(1)}, s32[8,128]{1,0:T(8,128)S(1)}, u32[]{:S(2)}, u32[]{:S(2)}) collective-permute-start(s32[8,128]{1,0:T(8,128)S(1)} %add_add_fusion.1), channel_id=1, source_target_pairs={{0,24},{2,26},{4,28},{6,30},{8,16},{10,18},{12,20},{14,22},{16,8},... | collective-permute-start | bytes 12296 | tf_op jit(solution)/shard_map/ppermute | solution.py:280
  41.1 18.4 %collective-permute-start.3 = (s32[8,128]{1,0:T(8,128)S(1)}, s32[8,128]{1,0:T(8,128)S(1)}, u32[]{:S(2)}, u32[]{:S(2)}) collective-permute-start(s32[8,128]{1,0:T(8,128)S(1)} %add_add_fusion.1), channel_id=1, source_target_pairs={{0,16},{2,18},{4,20},{6,22},{8,24},{10,26},{12,28},{14,30},{16,0},... | collective-permute-start | bytes 12296 | tf_op jit(solution)/shard_map/ppermute | solution.py:280
  43.1 18.2 %collective-permute-start.4 = (s32[8,128]{1,0:T(8,128)S(1)}, s32[8,128]{1,0:T(8,128)S(1)}, u32[]{:S(2)}, u32[]{:S(2)}) collective-permute-start(s32[8,128]{1,0:T(8,128)S(1)} %add_add_fusion.1), channel_id=1, source_target_pairs={{0,8},{2,10},{4,12},{6,14},{8,0},{10,2},{12,4},{14,6},{16,24},{18,... | collective-permute-start | bytes 12296 | tf_op jit(solution)/shard_map/ppermute | solution.py:280
  46.5 38.8 %collective-permute-start.20 = (bf16[896,256]{1,0:T(8,128)(2,1)}, bf16[896,256]{1,0:T(8,128)(2,1)}, u32[]{:S(2)}, u32[]{:S(2)}) collective-permute-start(bf16[896,256]{1,0:T(8,128)(2,1)} %get-tuple-element.56), channel_id=1, source_target_pairs={{0,8},{4,12},{8,0},{12,4},{1,9},{5,13},{9,1},{13,5},{2,10},{6,14},... | collective-permute-start | bytes 1376264 | tf_op jit(solution)/shard_map/ppermute | solution.py:337
  59.2 31.6 %collective-permute-start.16 = (bf16[1040,256]{1,0:T(8,128)(2,1)}, bf16[1040,256]{1,0:T(8,128)(2,1)S(1)}, u32[]{:S(2)}, u32[]{:S(2)}) collective-permute-start(bf16[1040,256]{1,0:T(8,128)(2,1)} %get-tuple-element.47), channel_id=1, source_target_pairs={{0,4},{4,8},{8,12},{12,0},{1,5},{5,9},{9,13},{13,1},{2,6},{6,10},{... | collective-permute-start | bytes 1597448 | tf_op jit(solution)/shard_map/ppermute | solution.py:337
  59.5 33.5 %collective-permute-start.17 = (bf16[1040,256]{1,0:T(8,128)(2,1)}, bf16[1040,256]{1,0:T(8,128)(2,1)S(1)}, u32[]{:S(2)}, u32[]{:S(2)}) collective-permute-start(bf16[1040,256]{1,0:T(8,128)(2,1)} %get-tuple-element.48), channel_id=1, source_target_pairs={{0,8},{4,12},{8,0},{12,4},{1,9},{5,13},{9,1},{13,5},{2,10},{6,14},... | collective-permute-start | bytes 1597448 | tf_op jit(solution)/shard_map/ppermute | solution.py:337
  61.3 2.1 %collective-permute-start.6 = (s32[8,128]{1,0:T(8,128)S(1)}, s32[8,128]{1,0:T(8,128)S(1)}, u32[]{:S(2)}, u32[]{:S(2)}) collective-permute-start(s32[8,128]{1,0:T(8,128)S(1)} %add_add_fusion), channel_id=1, source_target_pairs={{0,128},{1,129},{2,130},{3,131},{4,132},{5,133},{6,134},{7,135},{8... | collective-permute-start | bytes 12296 | tf_op jit(solution)/shard_map/ppermute | solution.py:446
  63.4 0.7 collective-permute-start.7
  64.1 0.7 collective-permute-start.8
  64.8 16.2 %collective-permute-start.9 = (s32[8,128]{1,0:T(8,128)S(1)}, s32[8,128]{1,0:T(8,128)S(1)}, u32[]{:S(2)}, u32[]{:S(2)}) collective-permute-start(s32[8,128]{1,0:T(8,128)S(1)} %add.82), channel_id=1, source_target_pairs={{128,0},{129,1},{130,2},{131,3},{132,4},{133,5},{134,6},{135,7},{1... | collective-permute-start | bytes 12296 | tf_op jit(solution)/shard_map/ppermute | solution.py:449
  81.0 15.3 %collective-permute-start.18 = (bf16[1040,256]{1,0:T(8,128)(2,1)}, bf16[1040,256]{1,0:T(8,128)(2,1)S(1)}, u32[]{:S(2)}, u32[]{:S(2)}) collective-permute-start(bf16[1040,256]{1,0:T(8,128)(2,1)} %get-tuple-element.49), channel_id=1, source_target_pairs={{0,12},{4,0},{8,4},{12,8},{1,13},{5,1},{9,5},{13,9},{2,14},{6,2},{... | collective-permute-start | bytes 1597448 | tf_op jit(solution)/shard_map/ppermute | solution.py:337
  82.9 7.7 %collective-permute-start.14 = (bf16[256,128]{1,0:T(8,128)(2,1)S(1)}, bf16[256,128]{1,0:T(8,128)(2,1)S(1)}, u32[]{:S(2)}, u32[]{:S(2)}) collective-permute-start(bf16[256,128]{1,0:T(8,128)(2,1)S(1)} %copy-done.8), channel_id=1, source_target_pairs={{0,1},{1,0},{2,3},{3,2},{4,5},{5,4},{6,7},{7,6},{8,9},{9,8},{10,11... | collective-permute-start | bytes 196616 | tf_op jit(solution)/shard_map/ppermute | solution.py:430
  85.3 29.8 %collective-permute-start.21 = (bf16[896,256]{1,0:T(8,128)(2,1)}, bf16[896,256]{1,0:T(8,128)(2,1)S(1)}, u32[]{:S(2)}, u32[]{:S(2)}) collective-permute-start(bf16[896,256]{1,0:T(8,128)(2,1)} %get-tuple-element.57), channel_id=1, source_target_pairs={{0,12},{4,0},{8,4},{12,8},{1,13},{5,1},{9,5},{13,9},{2,14},{6,2},{... | collective-permute-start | bytes 1376264 | tf_op jit(solution)/shard_map/ppermute | solution.py:337
  90.6 24.6 %collective-permute-start.22 = (bf16[256,896]{1,0:T(8,128)(2,1)S(1)}, bf16[256,896]{1,0:T(8,128)(2,1)}, u32[]{:S(2)}, u32[]{:S(2)}) collective-permute-start(bf16[256,896]{1,0:T(8,128)(2,1)S(1)} %copy-done.5), channel_id=1, source_target_pairs={{0,4},{4,8},{8,12},{12,0},{1,5},{5,9},{9,13},{13,1},{2,6},{6,10},{... | collective-permute-start | bytes 1376264 | tf_op jit(solution)/shard_map/ppermute | solution.py:337
  90.8 24.3 %collective-permute-start.23 = (bf16[256,896]{1,0:T(8,128)(2,1)S(1)}, bf16[256,896]{1,0:T(8,128)(2,1)}, u32[]{:S(2)}, u32[]{:S(2)}) collective-permute-start(bf16[256,896]{1,0:T(8,128)(2,1)S(1)} %copy-done.5), channel_id=1, source_target_pairs={{0,8},{4,12},{8,0},{12,4},{1,9},{5,13},{9,1},{13,5},{2,10},{6,14},... | collective-permute-start | bytes 1376264 | tf_op jit(solution)/shard_map/ppermute | solution.py:337
  93.0 32.4 %collective-permute-start.24 = (bf16[256,896]{1,0:T(8,128)(2,1)S(1)}, bf16[256,896]{1,0:T(8,128)(2,1)}, u32[]{:S(2)}, u32[]{:S(2)}) collective-permute-start(bf16[256,896]{1,0:T(8,128)(2,1)S(1)} %copy-done.5), channel_id=1, source_target_pairs={{0,12},{4,0},{8,4},{12,8},{1,13},{5,1},{9,5},{13,9},{2,14},{6,2},{... | collective-permute-start | bytes 1376264 | tf_op jit(solution)/shard_map/ppermute | solution.py:337
  96.3 81.4 %collective-permute-start.15 = (bf16[3584,128]{1,0:T(8,128)(2,1)S(1)}, bf16[3584,128]{1,0:T(8,128)(2,1)}, u32[]{:S(2)}, u32[]{:S(2)}) collective-permute-start(bf16[3584,128]{1,0:T(8,128)(2,1)S(1)} %bitcast.31), channel_id=1, source_target_pairs={{0,3},{3,0},{1,2},{2,1},{4,7},{7,4},{5,6},{6,5},{8,11},{11,8},{9,1... | collective-permute-start | bytes 2752520 | tf_op jit(solution)/shard_map/ppermute | solution.py:298
  131.6 12.8 %collective-permute-start.25 = (bf16[4,56,1024]{2,1,0:T(8,128)(2,1)}, bf16[4,56,1024]{2,1,0:T(8,128)(2,1)S(1)}, u32[]{:S(2)}, u32[]{:S(2)}) collective-permute-start(bf16[4,56,1024]{2,1,0:T(8,128)(2,1)} %get-tuple-element.60), channel_id=1, source_target_pairs={{0,2},{2,0},{16,18},{18,16},{32,34},{34,32},{48,50},{50,48},{64,66... | collective-permute-start | bytes 1376264 | tf_op jit(solution)/shard_map/ppermute | solution.py:29
  132.9 13.6 %collective-permute-start.26 = (bf16[4,56,1024]{2,1,0:T(8,128)(2,1)}, bf16[4,56,1024]{2,1,0:T(8,128)(2,1)S(1)}, u32[]{:S(2)}, u32[]{:S(2)}) collective-permute-start(bf16[4,56,1024]{2,1,0:T(8,128)(2,1)} %get-tuple-element.61), channel_id=1, source_target_pairs={{0,16},{2,18},{16,0},{18,2},{32,48},{34,50},{48,32},{50,34},{64,80... | collective-permute-start | bytes 1376264 | tf_op jit(solution)/shard_map/ppermute | solution.py:29
  133.9 21.0 %collective-permute-start.27 = (bf16[4,56,1024]{2,1,0:T(8,128)(2,1)}, bf16[4,56,1024]{2,1,0:T(8,128)(2,1)S(1)}, u32[]{:S(2)}, u32[]{:S(2)}) collective-permute-start(bf16[4,56,1024]{2,1,0:T(8,128)(2,1)} %get-tuple-element.62), channel_id=1, source_target_pairs={{0,18},{2,16},{16,2},{18,0},{32,50},{34,48},{48,34},{50,32},{64,82... | collective-permute-start | bytes 1376264 | tf_op jit(solution)/shard_map/ppermute | solution.py:29
  158.1 9.1 %collective-permute-start.28 = (bf16[56,1024]{1,0:T(8,128)(2,1)}, bf16[56,1024]{1,0:T(8,128)(2,1)S(1)}, u32[]{:S(2)}, u32[]{:S(2)}) collective-permute-start(bf16[56,1024]{1,0:T(8,128)(2,1)} %get-tuple-element.64), channel_id=1, source_target_pairs={{0,32},{2,34},{16,48},{18,50},{32,0},{34,2},{48,16},{50,18},{64,96... | collective-permute-start | bytes 344072 | tf_op jit(solution)/shard_map/ppermute | solution.py:29
  160.0 11.4 %collective-permute-start.29 = (bf16[56,1024]{1,0:T(8,128)(2,1)}, bf16[56,1024]{1,0:T(8,128)(2,1)S(1)}, u32[]{:S(2)}, u32[]{:S(2)}) collective-permute-start(bf16[56,1024]{1,0:T(8,128)(2,1)} %get-tuple-element.65), channel_id=1, source_target_pairs={{0,64},{2,66},{16,80},{18,82},{32,96},{34,98},{48,112},{50,114},{6... | collective-permute-start | bytes 344072 | tf_op jit(solution)/shard_map/ppermute | solution.py:29
  165.2 8.6 %collective-permute-start.30 = (bf16[56,1024]{1,0:T(8,128)(2,1)}, bf16[56,1024]{1,0:T(8,128)(2,1)S(1)}, u32[]{:S(2)}, u32[]{:S(2)}) collective-permute-start(bf16[56,1024]{1,0:T(8,128)(2,1)} %get-tuple-element.66), channel_id=1, source_target_pairs={{0,96},{2,98},{16,112},{18,114},{32,64},{34,66},{48,80},{50,82},{6... | collective-permute-start | bytes 344072 | tf_op jit(solution)/shard_map/ppermute | solution.py:29
  176.3 6.3 %collective-permute-start.31 = (f32[1,56]{1,0:T(1,128)}, f32[1,56]{1,0:T(1,128)S(1)}, u32[]{:S(2)}, u32[]{:S(2)}) collective-permute-start(f32[1,56]{1,0:T(1,128)} %get-tuple-element.69), channel_id=1, source_target_pairs={{0,1},{1,0},{2,3},{3,2},{4,5},{5,4},{6,7},{7,6},{8,9},{9,8},{10,11... | collective-permute-start | bytes 680 | tf_op jit(solution)/shard_map/ppermute | solution.py:19
  (23 other events, 346.1 us)

commit v3 on v2

--- a/solution.py
+++ b/solution.py
@@ -214,11 +214,9 @@
         out_ref[...] = total.astype(out_ref.dtype)
 
 
-def last_kernel(a_ref, b_ref, c_ref, d_ref, wv_ref, gain_ref, value_ref, output_ref, part_ref):
-    total = a_ref[...] + sum(r[...].astype(F32) for r in (b_ref, c_ref, d_ref))
-    value = total[:, :HEAD_DIM]
+def gain_kernel(a_ref, b_ref, c_ref, d_ref, wv_ref, gain_ref, value_ref, part_ref):
+    value = a_ref[...] + sum(r[...].astype(F32) for r in (b_ref, c_ref, d_ref))
     value_ref[0] = value
-    output_ref[0] = total[:, HEAD_DIM:]
     row = lax.dot_general(
         jnp.ones((8, HEAD_DIM), F32),
         wv_ref[...] * value,
@@ -227,6 +225,11 @@
         preferred_element_type=F32,
     )
     part_ref[...] = row[:1] / gain_ref[...]
+
+
+def last_kernel(a_ref, b_ref, c_ref, d_ref, output_ref):
+    total = a_ref[:, HEAD_DIM:]
+    output_ref[0] = total + sum(r[:, HEAD_DIM:].astype(F32) for r in (b_ref, c_ref, d_ref))
 
 
 def shaped(*dims):
@@ -343,7 +346,7 @@
     is_upper = upper.astype(jnp.int32).reshape(1)
     is_lower = 1 - is_upper
     tensor = ti.astype(jnp.int32).reshape(1)
-    block = width // 2
+    block = width // 4
 
     def values_of(kernel, scalars, blocks, more):
         def along(*shape):
@@ -512,17 +515,28 @@
     start = ((zi * NY + yi) * NX + xi) * share_rows
     own_wv = lax.dynamic_slice_in_dim(wv, start, share_rows, 0).astype(F32)
     own_gain = lax.dynamic_slice_in_dim(gain, start, share_rows, 0).reshape(1, share_rows)
-    value_share, output_share, gain_part = pl.pallas_call(
-        last_kernel,
+    first_columns = [pl.BlockSpec((share_rows, HEAD_DIM), lambda i: (0, 0))] * 5
+    value_share, gain_part = pl.pallas_call(
+        gain_kernel,
         out_shape=(
             jax.ShapeDtypeStruct((1, share_rows, HEAD_DIM), F32),
-            jax.ShapeDtypeStruct((1, share_rows, columns - HEAD_DIM), F32),
             jax.ShapeDtypeStruct((1, share_rows), F32),
         ),
-        in_specs=[VMEM] * 6,
-        out_specs=(VMEM,) * 3,
+        grid=(1,),
+        in_specs=first_columns + [pl.BlockSpec((1, share_rows), lambda i: (0, 0))],
+        out_specs=(
+            pl.BlockSpec((1, share_rows, HEAD_DIM), lambda i: (0, 0, 0)),
+            pl.BlockSpec((1, share_rows), lambda i: (0, 0)),
+        ),
     )(*got, own_wv, own_gain)
-    gain_rows = gain_part + paired(gain_part, "t", NT, 1)
+    other_part = paired(gain_part, "t", NT, 1)
+    output_share = pl.pallas_call(
+        last_kernel,
+        out_shape=jax.ShapeDtypeStruct((1, share_rows, columns - HEAD_DIM), F32),
+        in_specs=[VMEM] * 4,
+        out_specs=VMEM,
+    )(*got)
+    gain_rows = gain_part + other_part
     return own_rows.reshape(1, pairs, 1, seq, width), value_share, output_share, gain_rows
 
 

time: 186 us -> 188 us (1.011)
  transfers between devices with their start and end apart: 32 -> 32, of which waited for: 12 -> 12; matrix products, arithmetic and copies ran while one was open for 5% -> 4% of each run, Pallas kernels for 19% -> 20%
where the time goes in v3:
time: 188 us; the launch traced here: 185 us
  waiting for transfers between devices  74.7 us (40%)
  starting transfers between devices  56.8 us (30%)
  Pallas kernels  39.6 us (21%)
  local copies, waits for them, and re-layouts  8.82 us (5%)
  other arithmetic  3.16 us (2%)
    ppermute x6, waiting for transfers between devices, over_xz(): return lax.ppermute(block, ('z', 'x'), route)  26.4 us
    ppermute x9, waiting for transfers between devices, around(): return lax.ppermute(block, 'y', [(i, (i + shift) % NY) for i in range(NY)])  26.2 us
    ppermute x8, starting transfers between devices, exchanged(): return lax.ppermute(block, ('pipe', 'z', 'y', 'x'), route)  21.2 us
    ppermute x1, waiting for transfers between devices, section_step(): count_down = lax.ppermute(full_count, 'pipe', [(1, 0)])  14.9 us
    ppermute x9, starting transfers between devices, around(): return lax.ppermute(block, 'y', [(i, (i + shift) % NY) for i in range(NY)])  13.6 us
    ppermute x6, starting transfers between devices, over_xz(): return lax.ppermute(block, ('z', 'x'), route)  10.7 us
    pallas_call x2, Pallas kernels, values_of(): pl.pallas_call(kernel, out_shape=out_shape, grid_spec=pltpu.PrefetchScala...  9.17 us
    pallas_call x2, Pallas kernels, forward(): pl.pallas_call(forward_kernel, out_shape=(shaped(tokens, heads * HEAD_DIM...  6.77 us
  transfers between devices with their start and end apart: 32, of which 12 were waited for; matrix products, arithmetic and copies ran while one was open for 4% of the time, Pallas kernels for 20%

profile of v3, /device:TPU:4, one launch (start us, length us, event | category | flops | bytes accessed | tf_op | source)
XLA Modules:
  0.0 184.8 jit_solution(12750540966650148361)
XLA Ops:
  4.7 3.4 %shard_map.120 = (bf16[256,896]{1,0:T(8,128)(2,1)}, bf16[2,64,448]{2,1,0:T(8,128)(2,1)}, bf16[896,256]{1,0:T(8,128)(2,1)}, bf16[896,256]{1,0:T(8,128)(2,1)}, bf1...) custom-call(s32[1]{0:T(128)} %bitcast.6.y_ref, bf16[256,3584]{1,0:T(8,128)(2,1)} %bitcast.20, f32[1,3584]{1,0:T(1,128)} %refs_5_.3, ...), custom_call_target="tpu_custom_call" | custom-call | tf_op jit(solution)/shard_map/pallas_call | solution.py:312
  8.0 3.4 %shard_map.121 = (bf16[256,896]{1,0:T(8,128)(2,1)}, bf16[2,64,448]{2,1,0:T(8,128)(2,1)}, bf16[896,256]{1,0:T(8,128)(2,1)}, bf16[896,256]{1,0:T(8,128)(2,1)}, bf1...) custom-call(s32[1]{0:T(128)} %bitcast.6.y_ref, ...), custom_call_target="tpu_custom_call", output_to_operand_aliasing={{0}: (5, {}), {2}: (6, {}), {3}: (7, {}), {4}: (8, {}), {5}... | custom-call | tf_op jit(solution)/shard_map/pallas_call | solution.py:312
  12.4 2.5 %shard_map.122 = (bf16[256,128]{1,0:T(8,128)(2,1)}, bf16[256,3584]{1,0:T(8,128)(2,1)}) custom-call(s32[1]{0:T(128)} %bitcast.active_ref.upper_ref, s32[1]{0:T(128)} %bitcast.1.tensor_ref, bf16[2,64,3584]{2,1,0:T(8,128)(2,1)} %bitcast.35, bf16[2,64,3584]{2,1,0:T(8,128)(2,1)} %copy-done.6, f32[256,1]{1,0:T(8,128)} %reshape.237.mask_ref, ...), custom_call_target="tpu_custom_call" | custom-call | tf_op jit(solution)/shard_map/pallas_call | solution.py:365
  16.5 2.6 %shard_map.123.done_ref = bf16[256,3584]{1,0:T(8,128)(2,1)} custom-call(s32[1]{0:T(128)} %bitcast.active_ref.upper_ref, bf16[256,128]{1,0:T(8,128)(2,1)} %get-tuple-element.43.refs_0_.refs_1_, bf16[256,128]{1,0:T(8,128)(2,1)} %copy-done.18, bf16[3584,128]{1,0:T(8,128)(2,1)} %bitcast.29, bf16[3584,128]{1,0:T(8,128)(2,1)} %copy-done.7, ...), custom_call_target="tpu_custom_call" | custom-call | tf_op jit(solution)/shard_map/pallas_call | solution.py:384
  21.8 4.1 %collective-permute-start.2 = (s32[8,128]{1,0:T(8,128)S(1)}, s32[8,128]{1,0:T(8,128)S(1)}, u32[]{:S(2)}, u32[]{:S(2)}) collective-permute-start(s32[8,128]{1,0:T(8,128)S(1)} %broadcast_in_dim.11), channel_id=1, source_target_pairs={{0,6},{2,4},{4,2},{6,0},{8,14},{10,12},{12,10},{14,8},{16,22},{18,... | collective-permute-start | bytes 12296 | tf_op jit(solution)/shard_map/ppermute | solution.py:283
  25.9 2.7 %collective-permute-start = (s32[8,128]{1,0:T(8,128)S(1)}, s32[8,128]{1,0:T(8,128)S(1)}, u32[]{:S(2)}, u32[]{:S(2)}) collective-permute-start(s32[8,128]{1,0:T(8,128)S(1)} %broadcast_in_dim.11), channel_id=1, source_target_pairs={{0,2},{2,0},{4,6},{6,4},{8,10},{10,8},{12,14},{14,12},{16,18},{18,... | collective-permute-start | bytes 12296 | tf_op jit(solution)/shard_map/ppermute | solution.py:283
  28.7 2.4 %collective-permute-start.1 = (s32[8,128]{1,0:T(8,128)S(1)}, s32[8,128]{1,0:T(8,128)S(1)}, u32[]{:S(2)}, u32[]{:S(2)}) collective-permute-start(s32[8,128]{1,0:T(8,128)S(1)} %broadcast_in_dim.11), channel_id=1, source_target_pairs={{0,4},{2,6},{4,0},{6,2},{8,12},{10,14},{12,8},{14,10},{16,20},{18,... | collective-permute-start | bytes 12296 | tf_op jit(solution)/shard_map/ppermute | solution.py:283
  34.2 6.2 %collective-permute-start.5 = (s32[8,128]{1,0:T(8,128)S(1)}, s32[8,128]{1,0:T(8,128)S(1)}, u32[]{:S(2)}, u32[]{:S(2)}) collective-permute-start(s32[8,128]{1,0:T(8,128)S(1)} %add_add_fusion.1), channel_id=1, source_target_pairs={{0,24},{2,26},{4,28},{6,30},{8,16},{10,18},{12,20},{14,22},{16,8},... | collective-permute-start | bytes 12296 | tf_op jit(solution)/shard_map/ppermute | solution.py:283
  40.3 2.0 %collective-permute-start.3 = (s32[8,128]{1,0:T(8,128)S(1)}, s32[8,128]{1,0:T(8,128)S(1)}, u32[]{:S(2)}, u32[]{:S(2)}) collective-permute-start(s32[8,128]{1,0:T(8,128)S(1)} %add_add_fusion.1), channel_id=1, source_target_pairs={{0,16},{2,18},{4,20},{6,22},{8,24},{10,26},{12,28},{14,30},{16,0},... | collective-permute-start | bytes 12296 | tf_op jit(solution)/shard_map/ppermute | solution.py:283
  42.3 2.5 %collective-permute-start.4 = (s32[8,128]{1,0:T(8,128)S(1)}, s32[8,128]{1,0:T(8,128)S(1)}, u32[]{:S(2)}, u32[]{:S(2)}) collective-permute-start(s32[8,128]{1,0:T(8,128)S(1)} %add_add_fusion.1), channel_id=1, source_target_pairs={{0,8},{2,10},{4,12},{6,14},{8,0},{10,2},{12,4},{14,6},{16,24},{18,... | collective-permute-start | bytes 12296 | tf_op jit(solution)/shard_map/ppermute | solution.py:283
  45.7 2.9 %collective-permute-start.20 = (bf16[896,256]{1,0:T(8,128)(2,1)}, bf16[896,256]{1,0:T(8,128)(2,1)}, u32[]{:S(2)}, u32[]{:S(2)}) collective-permute-start(bf16[896,256]{1,0:T(8,128)(2,1)} %get-tuple-element.55), channel_id=1, source_target_pairs={{0,8},{4,12},{8,0},{12,4},{1,9},{5,13},{9,1},{13,5},{2,10},{6,14},... | collective-permute-start | bytes 1376264 | tf_op jit(solution)/shard_map/ppermute | solution.py:340
  48.6 6.6 %shard_map.124.refs_0_.refs_3_ = bf16[256,128]{1,0:T(8,128)(2,1)} custom-call(s32[1]{0:T(128)S(6)} %sub.35.active_ref, bf16[256,3584]{1,0:T(8,128)(2,1)} %copy-done, bf16[896,3584]{1,0:T(8,128)(2,1)} %bitcast.25, bf16[2,64,448]{2,1,0:T(8,128)(2,1)} %get-tuple-element.36.a_ref, bf16[2,64,448]{2,1,0:T(8,128)(2,1)} %get-tuple-element.42.b_ref), custom_call_target="tpu_custom_call" | custom-call | tf_op jit(solution)/shard_map/pallas_call | solution.py:365
  55.2 4.2 %shard_map.126 = (bf16[1040,256]{1,0:T(8,128)(2,1)}, bf16[1040,256]{1,0:T(8,128)(2,1)}, bf16[1040,256]{1,0:T(8,128)(2,1)}, bf16[1040,256]{1,0:T(8,128)(2,1)}) custom-call(s32[1]{0:T(128)} %bitcast.active_ref.upper_ref, s32[1]{0:T(128)} %bitcast.6.y_ref, bf16[256,3584]{1,0:T(8,128)(2,1)} %get-tuple-element.44.refs_6_.refs_0_, ...), custom_call_target="tpu_custom_call" | custom-call | tf_op jit(solution)/shard_map/pallas_call | solution.py:468
  66.3 14.9 %collective-permute-done.9 = s32[8,128]{1,0:T(8,128)S(1)} collective-permute-done((s32[8,128]{1,0:T(8,128)S(1)}, s32[8,128]{1,0:T(8,128)S(1)}, u32[]{:S(2)}, u32[]{:S(2)}) %collective-permute-start.9) | collective-permute-done | bytes 4128 | tf_op jit(solution)/shard_map/ppermute | solution.py:452
  81.2 1.9 %collective-permute-start.18 = (bf16[1040,256]{1,0:T(8,128)(2,1)}, bf16[1040,256]{1,0:T(8,128)(2,1)S(1)}, u32[]{:S(2)}, u32[]{:S(2)}) collective-permute-start(bf16[1040,256]{1,0:T(8,128)(2,1)} %get-tuple-element.48), channel_id=1, source_target_pairs={{0,12},{4,0},{8,4},{12,8},{1,13},{5,1},{9,5},{13,9},{2,14},{6,2},{... | collective-permute-start | bytes 1597448 | tf_op jit(solution)/shard_map/ppermute | solution.py:340
  83.1 2.4 %collective-permute-start.14 = (bf16[256,128]{1,0:T(8,128)(2,1)S(1)}, bf16[256,128]{1,0:T(8,128)(2,1)S(1)}, u32[]{:S(2)}, u32[]{:S(2)}) collective-permute-start(bf16[256,128]{1,0:T(8,128)(2,1)S(1)} %copy-done.8), channel_id=1, source_target_pairs={{0,1},{1,0},{2,3},{3,2},{4,5},{5,4},{6,7},{7,6},{8,9},{9,8},{10,11... | collective-permute-start | bytes 196616 | tf_op jit(solution)/shard_map/ppermute | solution.py:433
  85.7 5.0 %collective-permute-done.14.refs_1_ = bf16[256,128]{1,0:T(8,128)(2,1)S(1)} collective-permute-done((bf16[256,128]{1,0:T(8,128)(2,1)S(1)}, bf16[256,128]{1,0:T(8,128)(2,1)S(1)}, u32[]{:S(2)}, u32[]{:S(2)}) %collective-permute-start.14) | collective-permute-done | bytes 65568 | tf_op jit(solution)/shard_map/ppermute | solution.py:433
  91.0 2.2 %collective-permute-start.23 = (bf16[256,896]{1,0:T(8,128)(2,1)S(1)}, bf16[256,896]{1,0:T(8,128)(2,1)}, u32[]{:S(2)}, u32[]{:S(2)}) collective-permute-start(bf16[256,896]{1,0:T(8,128)(2,1)S(1)} %copy-done.5), channel_id=1, source_target_pairs={{0,8},{4,12},{8,0},{12,4},{1,9},{5,13},{9,1},{13,5},{2,10},{6,14},... | collective-permute-start | bytes 1376264 | tf_op jit(solution)/shard_map/ppermute | solution.py:340
  93.2 2.5 %collective-permute-start.24 = (bf16[256,896]{1,0:T(8,128)(2,1)S(1)}, bf16[256,896]{1,0:T(8,128)(2,1)}, u32[]{:S(2)}, u32[]{:S(2)}) collective-permute-start(bf16[256,896]{1,0:T(8,128)(2,1)S(1)} %copy-done.5), channel_id=1, source_target_pairs={{0,12},{4,0},{8,4},{12,8},{1,13},{5,1},{9,5},{13,9},{2,14},{6,2},{... | collective-permute-start | bytes 1376264 | tf_op jit(solution)/shard_map/ppermute | solution.py:340
  96.5 2.4 %collective-permute-start.15 = (bf16[3584,128]{1,0:T(8,128)(2,1)S(1)}, bf16[3584,128]{1,0:T(8,128)(2,1)}, u32[]{:S(2)}, u32[]{:S(2)}) collective-permute-start(bf16[3584,128]{1,0:T(8,128)(2,1)S(1)} %bitcast.31), channel_id=1, source_target_pairs={{0,3},{3,0},{1,2},{2,1},{4,7},{7,4},{5,6},{6,5},{8,11},{11,8},{9,1... | collective-permute-start | bytes 2752520 | tf_op jit(solution)/shard_map/ppermute | solution.py:301
  100.2 15.2 %collective-permute-done.21.refs_15_ = bf16[896,256]{1,0:T(8,128)(2,1)S(1)} collective-permute-done((bf16[896,256]{1,0:T(8,128)(2,1)}, bf16[896,256]{1,0:T(8,128)(2,1)S(1)}, u32[]{:S(2)}, u32[]{:S(2)}) %collective-permute-start.21) | collective-permute-done | bytes 458784 | tf_op jit(solution)/shard_map/ppermute | solution.py:340
  115.4 10.3 %collective-permute-done.24.refs_19_ = bf16[256,896]{1,0:T(8,128)(2,1)} collective-permute-done((bf16[256,896]{1,0:T(8,128)(2,1)S(1)}, bf16[256,896]{1,0:T(8,128)(2,1)}, u32[]{:S(2)}, u32[]{:S(2)}) %collective-permute-start.24) | collective-permute-done | bytes 458784 | tf_op jit(solution)/shard_map/ppermute | solution.py:340
  125.6 6.2 %shard_map.127 = (bf16[4,56,1024]{2,1,0:T(8,128)(2,1)}, bf16[4,56,1024]{2,1,0:T(8,128)(2,1)}, bf16[4,56,1024]{2,1,0:T(8,128)(2,1)}, bf16[4,56,1024]{2,1,0:T(8,128)(2,1)}) custom-call(s32[1]{0:T(128)} %bitcast.13.own_ref, f32[1]{0:T(128)} %bitcast.14.scale_ref, bf16[1040,256]{1,0:T(8,128)(2,1)} %get-tuple-element.49.refs_0_.refs_4_.refs_8_, ...), custom_call_target="tpu_custom_call" | custom-call | tf_op jit(solution)/shard_map/pallas_call | solution.py:484
  137.3 7.3 %collective-permute-done.25.b_ref = bf16[4,56,1024]{2,1,0:T(8,128)(2,1)S(1)} collective-permute-done((bf16[4,56,1024]{2,1,0:T(8,128)(2,1)}, bf16[4,56,1024]{2,1,0:T(8,128)(2,1)S(1)}, u32[]{:S(2)}, u32[]{:S(2)}) %collective-permute-start.25) | collective-permute-done | bytes 458784 | tf_op jit(solution)/shard_map/ppermute | solution.py:29
  144.6 2.1 %collective-permute-done.26.c_ref = bf16[4,56,1024]{2,1,0:T(8,128)(2,1)S(1)} collective-permute-done((bf16[4,56,1024]{2,1,0:T(8,128)(2,1)}, bf16[4,56,1024]{2,1,0:T(8,128)(2,1)S(1)}, u32[]{:S(2)}, u32[]{:S(2)}) %collective-permute-start.26) | collective-permute-done | bytes 458784 | tf_op jit(solution)/shard_map/ppermute | solution.py:29
  146.8 8.4 %collective-permute-done.27.d_ref = bf16[4,56,1024]{2,1,0:T(8,128)(2,1)S(1)} collective-permute-done((bf16[4,56,1024]{2,1,0:T(8,128)(2,1)}, bf16[4,56,1024]{2,1,0:T(8,128)(2,1)S(1)}, u32[]{:S(2)}, u32[]{:S(2)}) %collective-permute-start.27) | collective-permute-done | bytes 458784 | tf_op jit(solution)/shard_map/ppermute | solution.py:29
  155.9 2.3 %shard_map.128 = (f32[56,1024]{1,0:T(8,128)}, bf16[56,1024]{1,0:T(8,128)(2,1)}, bf16[56,1024]{1,0:T(8,128)(2,1)}, bf16[56,1024]{1,0:T(8,128)(2,1)}) custom-call(s32[1]{0:T(128)} %bitcast.12.own_ref, bf16[4,56,1024]{2,1,0:T(8,128)(2,1)} %get-tuple-element.58.a_ref, bf16[4,56,1024]{2,1,0:T(8,128)(2,1)} %copy-done.10, bf16[4,56,1024]{2,1,0:T(8,128)(2,1)} %copy-done.11, ...), custom_call_target="tpu_custom_call" | custom-call | tf_op jit(solution)/shard_map/pallas_call | solution.py:505
  158.3 1.9 %collective-permute-start.28 = (bf16[56,1024]{1,0:T(8,128)(2,1)}, bf16[56,1024]{1,0:T(8,128)(2,1)S(1)}, u32[]{:S(2)}, u32[]{:S(2)}) collective-permute-start(bf16[56,1024]{1,0:T(8,128)(2,1)} %get-tuple-element.63), channel_id=1, source_target_pairs={{0,32},{2,34},{16,48},{18,50},{32,0},{34,2},{48,16},{50,18},{64,96... | collective-permute-start | bytes 344072 | tf_op jit(solution)/shard_map/ppermute | solution.py:29
  160.2 5.2 %collective-permute-start.29 = (bf16[56,1024]{1,0:T(8,128)(2,1)}, bf16[56,1024]{1,0:T(8,128)(2,1)S(1)}, u32[]{:S(2)}, u32[]{:S(2)}) collective-permute-start(bf16[56,1024]{1,0:T(8,128)(2,1)} %get-tuple-element.64), channel_id=1, source_target_pairs={{0,64},{2,66},{16,80},{18,82},{32,96},{34,98},{48,112},{50,114},{6... | collective-permute-start | bytes 344072 | tf_op jit(solution)/shard_map/ppermute | solution.py:29
  165.4 6.1 %collective-permute-done.29.c_ref = bf16[56,1024]{1,0:T(8,128)(2,1)S(1)} collective-permute-done((bf16[56,1024]{1,0:T(8,128)(2,1)}, bf16[56,1024]{1,0:T(8,128)(2,1)S(1)}, u32[]{:S(2)}, u32[]{:S(2)}) %collective-permute-start.29) | collective-permute-done | bytes 114720 | tf_op jit(solution)/shard_map/ppermute | solution.py:29
  171.6 2.4 %collective-permute-done.30.d_ref = bf16[56,1024]{1,0:T(8,128)(2,1)S(1)} collective-permute-done((bf16[56,1024]{1,0:T(8,128)(2,1)}, bf16[56,1024]{1,0:T(8,128)(2,1)S(1)}, u32[]{:S(2)}, u32[]{:S(2)}) %collective-permute-start.30) | collective-permute-done | bytes 114720 | tf_op jit(solution)/shard_map/ppermute | solution.py:29
  177.5 5.0 %shard_map.125 = bf16[1,128,3584]{2,1,0:T(8,128)(2,1)} custom-call(s32[1]{0:T(128)S(6)} %sub.35.active_ref, s32[1]{0:T(128)} %bitcast.1.tensor_ref, f32[256,1]{1,0:T(8,128)} %copy.20.weight_ref, bf16[256,3584]{1,0:T(8,128)(2,1)} %shard_map.123.done_ref, bf16[256,128]{1,0:T(8,128)(2,1)} %shard_map.124.refs_0_.refs_3_, bf16[256,128]{1,0:T(8,128)(2,1)} %copy-done.17, ...), custom_call_target="tpu_custom_call" | custom-call | tf_op jit(solution)/shard_map/pallas_call | solution.py:410
  (113 shorter events, 33.7 us)
Async XLA Ops:
  0.6 10.8 %collective-permute-start.10 = (bf16[2,64,3584]{2,1,0:T(8,128)(2,1)}, bf16[2,64,3584]{2,1,0:T(8,128)(2,1)S(1)}, u32[]{:S(2)}, u32[]{:S(2)}) collective-permute-start(bf16[2,64,3584]{2,1,0:T(8,128)(2,1)} %bitcast.34), channel_id=1, source_target_pairs={{128,129},{129,128},{130,131},{131,130},{132,133},{133,132},{134,1... | collective-permute-start | bytes 2752520 | tf_op jit(solution)/shard_map/ppermute | solution.py:266
  1.4 14.2 %collective-permute-start.12 = (bf16[3584,128]{1,0:T(8,128)(2,1)}, bf16[3584,128]{1,0:T(8,128)(2,1)S(1)}, u32[]{:S(2)}, u32[]{:S(2)}) collective-permute-start(bf16[3584,128]{1,0:T(8,128)(2,1)} %bitcast.26), channel_id=1, source_target_pairs={{128,131},{131,128},{129,130},{130,129},{132,135},{135,132},{133,1... | collective-permute-start | bytes 2752520 | tf_op jit(solution)/shard_map/ppermute | solution.py:301
  14.9 0.7 collective-permute-start.11
  19.1 26.5 %collective-permute-start.13 = (bf16[256,3584]{1,0:T(8,128)(2,1)}, bf16[256,3584]{1,0:T(8,128)(2,1)S(1)}, u32[]{:S(2)}, u32[]{:S(2)}) collective-permute-start(bf16[256,3584]{1,0:T(8,128)(2,1)} %shard_map.123.done_ref), channel_id=1, source_target_pairs={{128,0},{129,1},{130,2},{131,3},{132,4},{133,5},{134,6},{135,7},{1... | collective-permute-start | bytes 5505032 | tf_op jit(solution)/shard_map/ppermute | solution.py:447
  21.8 11.1 %collective-permute-start.2 = (s32[8,128]{1,0:T(8,128)S(1)}, s32[8,128]{1,0:T(8,128)S(1)}, u32[]{:S(2)}, u32[]{:S(2)}) collective-permute-start(s32[8,128]{1,0:T(8,128)S(1)} %broadcast_in_dim.11), channel_id=1, source_target_pairs={{0,6},{2,4},{4,2},{6,0},{8,14},{10,12},{12,10},{14,8},{16,22},{18,... | collective-permute-start | bytes 12296 | tf_op jit(solution)/shard_map/ppermute | solution.py:283
  25.9 7.0 %collective-permute-start = (s32[8,128]{1,0:T(8,128)S(1)}, s32[8,128]{1,0:T(8,128)S(1)}, u32[]{:S(2)}, u32[]{:S(2)}) collective-permute-start(s32[8,128]{1,0:T(8,128)S(1)} %broadcast_in_dim.11), channel_id=1, source_target_pairs={{0,2},{2,0},{4,6},{6,4},{8,10},{10,8},{12,14},{14,12},{16,18},{18,... | collective-permute-start | bytes 12296 | tf_op jit(solution)/shard_map/ppermute | solution.py:283
  28.7 5.5 %collective-permute-start.1 = (s32[8,128]{1,0:T(8,128)S(1)}, s32[8,128]{1,0:T(8,128)S(1)}, u32[]{:S(2)}, u32[]{:S(2)}) collective-permute-start(s32[8,128]{1,0:T(8,128)S(1)} %broadcast_in_dim.11), channel_id=1, source_target_pairs={{0,4},{2,6},{4,0},{6,2},{8,12},{10,14},{12,8},{14,10},{16,20},{18,... | collective-permute-start | bytes 12296 | tf_op jit(solution)/shard_map/ppermute | solution.py:283
  31.0 52.1 %collective-permute-start.19 = (bf16[896,256]{1,0:T(8,128)(2,1)S(1)}, bf16[896,256]{1,0:T(8,128)(2,1)}, u32[]{:S(2)}, u32[]{:S(2)}) collective-permute-start(bf16[896,256]{1,0:T(8,128)(2,1)S(1)} %copy-done.9), channel_id=1, source_target_pairs={{0,4},{4,8},{8,12},{12,0},{1,5},{5,9},{9,13},{13,1},{2,6},{6,10},{... | collective-permute-start | bytes 1376264 | tf_op jit(solution)/shard_map/ppermute | solution.py:340
  34.2 25.3 %collective-permute-start.5 = (s32[8,128]{1,0:T(8,128)S(1)}, s32[8,128]{1,0:T(8,128)S(1)}, u32[]{:S(2)}, u32[]{:S(2)}) collective-permute-start(s32[8,128]{1,0:T(8,128)S(1)} %add_add_fusion.1), channel_id=1, source_target_pairs={{0,24},{2,26},{4,28},{6,30},{8,16},{10,18},{12,20},{14,22},{16,8},... | collective-permute-start | bytes 12296 | tf_op jit(solution)/shard_map/ppermute | solution.py:283
  40.3 19.4 %collective-permute-start.3 = (s32[8,128]{1,0:T(8,128)S(1)}, s32[8,128]{1,0:T(8,128)S(1)}, u32[]{:S(2)}, u32[]{:S(2)}) collective-permute-start(s32[8,128]{1,0:T(8,128)S(1)} %add_add_fusion.1), channel_id=1, source_target_pairs={{0,16},{2,18},{4,20},{6,22},{8,24},{10,26},{12,28},{14,30},{16,0},... | collective-permute-start | bytes 12296 | tf_op jit(solution)/shard_map/ppermute | solution.py:283
  42.3 19.2 %collective-permute-start.4 = (s32[8,128]{1,0:T(8,128)S(1)}, s32[8,128]{1,0:T(8,128)S(1)}, u32[]{:S(2)}, u32[]{:S(2)}) collective-permute-start(s32[8,128]{1,0:T(8,128)S(1)} %add_add_fusion.1), channel_id=1, source_target_pairs={{0,8},{2,10},{4,12},{6,14},{8,0},{10,2},{12,4},{14,6},{16,24},{18,... | collective-permute-start | bytes 12296 | tf_op jit(solution)/shard_map/ppermute | solution.py:283
  45.7 39.8 %collective-permute-start.20 = (bf16[896,256]{1,0:T(8,128)(2,1)}, bf16[896,256]{1,0:T(8,128)(2,1)}, u32[]{:S(2)}, u32[]{:S(2)}) collective-permute-start(bf16[896,256]{1,0:T(8,128)(2,1)} %get-tuple-element.55), channel_id=1, source_target_pairs={{0,8},{4,12},{8,0},{12,4},{1,9},{5,13},{9,1},{13,5},{2,10},{6,14},... | collective-permute-start | bytes 1376264 | tf_op jit(solution)/shard_map/ppermute | solution.py:340
  59.4 31.6 %collective-permute-start.16 = (bf16[1040,256]{1,0:T(8,128)(2,1)}, bf16[1040,256]{1,0:T(8,128)(2,1)S(1)}, u32[]{:S(2)}, u32[]{:S(2)}) collective-permute-start(bf16[1040,256]{1,0:T(8,128)(2,1)} %get-tuple-element.46), channel_id=1, source_target_pairs={{0,4},{4,8},{8,12},{12,0},{1,5},{5,9},{9,13},{13,1},{2,6},{6,10},{... | collective-permute-start | bytes 1597448 | tf_op jit(solution)/shard_map/ppermute | solution.py:340
  59.7 33.5 %collective-permute-start.17 = (bf16[1040,256]{1,0:T(8,128)(2,1)}, bf16[1040,256]{1,0:T(8,128)(2,1)S(1)}, u32[]{:S(2)}, u32[]{:S(2)}) collective-permute-start(bf16[1040,256]{1,0:T(8,128)(2,1)} %get-tuple-element.47), channel_id=1, source_target_pairs={{0,8},{4,12},{8,0},{12,4},{1,9},{5,13},{9,1},{13,5},{2,10},{6,14},... | collective-permute-start | bytes 1597448 | tf_op jit(solution)/shard_map/ppermute | solution.py:340
  61.5 2.1 %collective-permute-start.6 = (s32[8,128]{1,0:T(8,128)S(1)}, s32[8,128]{1,0:T(8,128)S(1)}, u32[]{:S(2)}, u32[]{:S(2)}) collective-permute-start(s32[8,128]{1,0:T(8,128)S(1)} %add_add_fusion), channel_id=1, source_target_pairs={{0,128},{1,129},{2,130},{3,131},{4,132},{5,133},{6,134},{7,135},{8... | collective-permute-start | bytes 12296 | tf_op jit(solution)/shard_map/ppermute | solution.py:449
  63.6 0.7 collective-permute-start.7
  64.3 0.7 collective-permute-start.8
  65.0 16.2 %collective-permute-start.9 = (s32[8,128]{1,0:T(8,128)S(1)}, s32[8,128]{1,0:T(8,128)S(1)}, u32[]{:S(2)}, u32[]{:S(2)}) collective-permute-start(s32[8,128]{1,0:T(8,128)S(1)} %add.82), channel_id=1, source_target_pairs={{128,0},{129,1},{130,2},{131,3},{132,4},{133,5},{134,6},{135,7},{1... | collective-permute-start | bytes 12296 | tf_op jit(solution)/shard_map/ppermute | solution.py:452
  81.2 15.3 %collective-permute-start.18 = (bf16[1040,256]{1,0:T(8,128)(2,1)}, bf16[1040,256]{1,0:T(8,128)(2,1)S(1)}, u32[]{:S(2)}, u32[]{:S(2)}) collective-permute-start(bf16[1040,256]{1,0:T(8,128)(2,1)} %get-tuple-element.48), channel_id=1, source_target_pairs={{0,12},{4,0},{8,4},{12,8},{1,13},{5,1},{9,5},{13,9},{2,14},{6,2},{... | collective-permute-start | bytes 1597448 | tf_op jit(solution)/shard_map/ppermute | solution.py:340
  83.1 7.7 %collective-permute-start.14 = (bf16[256,128]{1,0:T(8,128)(2,1)S(1)}, bf16[256,128]{1,0:T(8,128)(2,1)S(1)}, u32[]{:S(2)}, u32[]{:S(2)}) collective-permute-start(bf16[256,128]{1,0:T(8,128)(2,1)S(1)} %copy-done.8), channel_id=1, source_target_pairs={{0,1},{1,0},{2,3},{3,2},{4,5},{5,4},{6,7},{7,6},{8,9},{9,8},{10,11... | collective-permute-start | bytes 196616 | tf_op jit(solution)/shard_map/ppermute | solution.py:433
  85.5 29.8 %collective-permute-start.21 = (bf16[896,256]{1,0:T(8,128)(2,1)}, bf16[896,256]{1,0:T(8,128)(2,1)S(1)}, u32[]{:S(2)}, u32[]{:S(2)}) collective-permute-start(bf16[896,256]{1,0:T(8,128)(2,1)} %get-tuple-element.56), channel_id=1, source_target_pairs={{0,12},{4,0},{8,4},{12,8},{1,13},{5,1},{9,5},{13,9},{2,14},{6,2},{... | collective-permute-start | bytes 1376264 | tf_op jit(solution)/shard_map/ppermute | solution.py:340
  90.8 24.6 %collective-permute-start.22 = (bf16[256,896]{1,0:T(8,128)(2,1)S(1)}, bf16[256,896]{1,0:T(8,128)(2,1)}, u32[]{:S(2)}, u32[]{:S(2)}) collective-permute-start(bf16[256,896]{1,0:T(8,128)(2,1)S(1)} %copy-done.5), channel_id=1, source_target_pairs={{0,4},{4,8},{8,12},{12,0},{1,5},{5,9},{9,13},{13,1},{2,6},{6,10},{... | collective-permute-start | bytes 1376264 | tf_op jit(solution)/shard_map/ppermute | solution.py:340
  91.0 24.3 %collective-permute-start.23 = (bf16[256,896]{1,0:T(8,128)(2,1)S(1)}, bf16[256,896]{1,0:T(8,128)(2,1)}, u32[]{:S(2)}, u32[]{:S(2)}) collective-permute-start(bf16[256,896]{1,0:T(8,128)(2,1)S(1)} %copy-done.5), channel_id=1, source_target_pairs={{0,8},{4,12},{8,0},{12,4},{1,9},{5,13},{9,1},{13,5},{2,10},{6,14},... | collective-permute-start | bytes 1376264 | tf_op jit(solution)/shard_map/ppermute | solution.py:340
  93.2 32.4 %collective-permute-start.24 = (bf16[256,896]{1,0:T(8,128)(2,1)S(1)}, bf16[256,896]{1,0:T(8,128)(2,1)}, u32[]{:S(2)}, u32[]{:S(2)}) collective-permute-start(bf16[256,896]{1,0:T(8,128)(2,1)S(1)} %copy-done.5), channel_id=1, source_target_pairs={{0,12},{4,0},{8,4},{12,8},{1,13},{5,1},{9,5},{13,9},{2,14},{6,2},{... | collective-permute-start | bytes 1376264 | tf_op jit(solution)/shard_map/ppermute | solution.py:340
  96.5 80.9 %collective-permute-start.15 = (bf16[3584,128]{1,0:T(8,128)(2,1)S(1)}, bf16[3584,128]{1,0:T(8,128)(2,1)}, u32[]{:S(2)}, u32[]{:S(2)}) collective-permute-start(bf16[3584,128]{1,0:T(8,128)(2,1)S(1)} %bitcast.31), channel_id=1, source_target_pairs={{0,3},{3,0},{1,2},{2,1},{4,7},{7,4},{5,6},{6,5},{8,11},{11,8},{9,1... | collective-permute-start | bytes 2752520 | tf_op jit(solution)/shard_map/ppermute | solution.py:301
  131.9 12.8 %collective-permute-start.25 = (bf16[4,56,1024]{2,1,0:T(8,128)(2,1)}, bf16[4,56,1024]{2,1,0:T(8,128)(2,1)S(1)}, u32[]{:S(2)}, u32[]{:S(2)}) collective-permute-start(bf16[4,56,1024]{2,1,0:T(8,128)(2,1)} %get-tuple-element.59), channel_id=1, source_target_pairs={{0,2},{2,0},{16,18},{18,16},{32,34},{34,32},{48,50},{50,48},{64,66... | collective-permute-start | bytes 1376264 | tf_op jit(solution)/shard_map/ppermute | solution.py:29
  133.1 13.6 %collective-permute-start.26 = (bf16[4,56,1024]{2,1,0:T(8,128)(2,1)}, bf16[4,56,1024]{2,1,0:T(8,128)(2,1)S(1)}, u32[]{:S(2)}, u32[]{:S(2)}) collective-permute-start(bf16[4,56,1024]{2,1,0:T(8,128)(2,1)} %get-tuple-element.60), channel_id=1, source_target_pairs={{0,16},{2,18},{16,0},{18,2},{32,48},{34,50},{48,32},{50,34},{64,80... | collective-permute-start | bytes 1376264 | tf_op jit(solution)/shard_map/ppermute | solution.py:29
  134.2 21.0 %collective-permute-start.27 = (bf16[4,56,1024]{2,1,0:T(8,128)(2,1)}, bf16[4,56,1024]{2,1,0:T(8,128)(2,1)S(1)}, u32[]{:S(2)}, u32[]{:S(2)}) collective-permute-start(bf16[4,56,1024]{2,1,0:T(8,128)(2,1)} %get-tuple-element.61), channel_id=1, source_target_pairs={{0,18},{2,16},{16,2},{18,0},{32,50},{34,48},{48,34},{50,32},{64,82... | collective-permute-start | bytes 1376264 | tf_op jit(solution)/shard_map/ppermute | solution.py:29
  158.3 7.1 %collective-permute-start.28 = (bf16[56,1024]{1,0:T(8,128)(2,1)}, bf16[56,1024]{1,0:T(8,128)(2,1)S(1)}, u32[]{:S(2)}, u32[]{:S(2)}) collective-permute-start(bf16[56,1024]{1,0:T(8,128)(2,1)} %get-tuple-element.63), channel_id=1, source_target_pairs={{0,32},{2,34},{16,48},{18,50},{32,0},{34,2},{48,16},{50,18},{64,96... | collective-permute-start | bytes 344072 | tf_op jit(solution)/shard_map/ppermute | solution.py:29
  160.2 11.4 %collective-permute-start.29 = (bf16[56,1024]{1,0:T(8,128)(2,1)}, bf16[56,1024]{1,0:T(8,128)(2,1)S(1)}, u32[]{:S(2)}, u32[]{:S(2)}) collective-permute-start(bf16[56,1024]{1,0:T(8,128)(2,1)} %get-tuple-element.64), channel_id=1, source_target_pairs={{0,64},{2,66},{16,80},{18,82},{32,96},{34,98},{48,112},{50,114},{6... | collective-permute-start | bytes 344072 | tf_op jit(solution)/shard_map/ppermute | solution.py:29
  165.4 8.6 %collective-permute-start.30 = (bf16[56,1024]{1,0:T(8,128)(2,1)}, bf16[56,1024]{1,0:T(8,128)(2,1)S(1)}, u32[]{:S(2)}, u32[]{:S(2)}) collective-permute-start(bf16[56,1024]{1,0:T(8,128)(2,1)} %get-tuple-element.65), channel_id=1, source_target_pairs={{0,96},{2,98},{16,112},{18,114},{32,64},{34,66},{48,80},{50,82},{6... | collective-permute-start | bytes 344072 | tf_op jit(solution)/shard_map/ppermute | solution.py:29
  176.1 8.1 %collective-permute-start.31 = (f32[1,56]{1,0:T(1,128)}, f32[1,56]{1,0:T(1,128)S(1)}, u32[]{:S(2)}, u32[]{:S(2)}) collective-permute-start(f32[1,56]{1,0:T(1,128)} %get-tuple-element.67), channel_id=1, source_target_pairs={{0,1},{1,0},{2,3},{3,2},{4,5},{5,4},{6,7},{7,6},{8,9},{9,8},{10,11... | collective-permute-start | bytes 680 | tf_op jit(solution)/shard_map/ppermute | solution.py:19
  (23 other events, 341.3 us)

commit v4 on v3

--- a/solution.py
+++ b/solution.py
@@ -145,12 +145,12 @@
 EXTRA = 16
 
 
-def owners_kernel(upper_ref, y_ref, *refs):
-    (upper_dy, upper_values, lower_dy, lower_values, weight_ref), refs = refs[:5], refs[5:]
+def owners_kernel(active_ref, y_ref, dy_hbm, values_ref, weight_ref, *refs):
     out_refs, turned_ref, dy_buffer, sems = refs[:NY], refs[NY], refs[NY + 1], refs[NY + 2]
     block = dy_buffer.shape[2]
 
-    def turn(dy_hbm, values_ref):
+    @pl.when(active_ref[0] == 1)
+    def _():
         tokens, width = dy_hbm.shape
         copies = [
             pltpu.make_async_copy(
@@ -172,34 +172,36 @@
         for n, copy in enumerate(copies):
             copy.wait()
             turned_ref[n * block : (n + 1) * block] = dy_buffer[n].T
-
-    @pl.when(upper_ref[0] == 1)
-    def _():
-        turn(upper_dy, upper_values)
-
-    @pl.when(upper_ref[0] == 0)
-    def _():
-        turn(lower_dy, lower_values)
-
-    deal(out_refs, turned_ref, y_ref[0])
-
-
-def products_kernel(own_ref, scale_ref, *refs):
-    groups, refs = [refs[n * NY : (n + 1) * NY] for n in range(5)], refs[5 * NY :]
+        deal(out_refs, turned_ref, y_ref[0])
+
+
+def products_kernel(own_ref, upper_ref, scale_ref, *refs):
+    groups, refs = [refs[n * NY : (n + 1) * NY] for n in range(8)], refs[8 * NY :]
     out_refs, total_ref = refs[:-1], refs[-1]
     tokens = groups[0][0].shape[1]
     lane = lax.broadcasted_iota(jnp.int32, (1, tokens), 1)
     chosen = jnp.where(lane // 64 % 2 == 0, scale_ref[0], 0.0)
-    value, output = 0.0, 0.0
-    for dy_ref, values_ref, weight_ref, normed_ref, mixed_ref in zip(*groups):
-        rows = weight_ref[...].astype(F32)
-        weight = rows[0:1] + rows[1:2] - chosen
-        dy = (weight * dy_ref[...].astype(F32)).astype(BF16)
-        values_t = (weight * values_ref[...].astype(F32)).astype(BF16)
-        output = output + dot(dy, mixed_ref[...], ((1,), (0,)))
-        value = value + dot(normed_ref[...], values_t, ((1,), (1,)))
-    total_ref[:, :HEAD_DIM] = value
-    total_ref[:, HEAD_DIM:] = output
+
+    def add_up(messages):
+        value, output = 0.0, 0.0
+        for dy_ref, values_ref, weight_ref, normed_ref, mixed_ref in zip(*messages, *groups[6:]):
+            rows = weight_ref[...].astype(F32)
+            weight = rows[0:1] + rows[1:2] - chosen
+            dy = (weight * dy_ref[...].astype(F32)).astype(BF16)
+            values_t = (weight * values_ref[...].astype(F32)).astype(BF16)
+            output = output + dot(dy, mixed_ref[...], ((1,), (0,)))
+            value = value + dot(normed_ref[...], values_t, ((1,), (1,)))
+        total_ref[:, :HEAD_DIM] = value
+        total_ref[:, HEAD_DIM:] = output
+
+    @pl.when(upper_ref[0] == 1)
+    def _():
+        add_up(groups[:3])
+
+    @pl.when(upper_ref[0] == 0)
+    def _():
+        add_up(groups[3:6])
+
     count, size = out_refs[0].shape[:2]
     for k, out_ref in enumerate(out_refs):
         for n in range(count):
@@ -336,8 +338,9 @@
     mixed, turned_0, *normed = forward(0)
     mixed, turned_1, *normed = forward(1, mixed, *normed)
 
-    def around(block, shift):
-        return lax.ppermute(block, "y", [(i, (i + shift) % NY) for i in range(NY)])
+    def around(block, shift, sections=(0, 1)):
+        route = [(n * NY + i, n * NY + (i + shift) % NY) for n in sections for i in range(NY)]
+        return lax.ppermute(block, ("pipe", "y"), route)
 
     mixed_all = [mixed] + [around(mixed, s) for s in range(1, NY)]
     normed_all = [normed[0]] + [around(normed[s], s) for s in range(1, NY)]
@@ -346,7 +349,7 @@
     is_upper = upper.astype(jnp.int32).reshape(1)
     is_lower = 1 - is_upper
     tensor = ti.astype(jnp.int32).reshape(1)
-    block = width // 4
+    block = width // 2
 
     def values_of(kernel, scalars, blocks, more):
         def along(*shape):
@@ -446,6 +449,27 @@
     rows_1 = rows_of(is_upper, own_1, other_1, other_wv_1, raw)
     incoming = lax.ppermute(rows_1, "pipe", [(1, 0)])
 
+    below = HEAD_DIM + EXTRA
+    bare = jnp.stack([-DPO_BETA * weight_pair, DPO_BETA * weight_pair], axis=1)
+    bare_row = jnp.broadcast_to(bare[:, :, None], (pairs, 2, seq)).reshape(1, tokens)
+    bare_row = lax.optimization_barrier(bare_row)
+
+    def sent(active, dy, values, section_id):
+        turned = pl.pallas_call(
+            owners_kernel,
+            out_shape=(shaped(width // NY + below, tokens),) * NY,
+            in_specs=[SMEM, SMEM, ANY, VMEM, VMEM],
+            out_specs=(VMEM,) * NY,
+            scratch_shapes=[
+                pltpu.VMEM((width, tokens), BF16),
+                pltpu.VMEM((4, tokens, 896), BF16),
+                pltpu.SemaphoreType.DMA((4,)),
+            ],
+        )(active, y_index, dy, values, bare_row)
+        return [turned[0]] + [around(turned[s], s, (section_id,)) for s in range(1, NY)]
+
+    blocks_1 = sent(is_upper, raw, own_1, 1)
+
     partial_count = lax.ppermute(count, "pipe", [(0, 1)])
     full_count = partial_count + exchanged(partial_count, 2, 0, 0, 1)
     full_count = full_count + exchanged(full_count, 4, 0, 0, 1)
@@ -453,9 +477,6 @@
     chosen_total = jnp.where(upper, full_count, count_down)[0, 0]
     pair_total = pairs * NZ * NY * NX
     scale = LIKELIHOOD_COEF * jnp.asarray(pair_total, F32) / chosen_total.astype(F32)
-    bare = jnp.stack([-DPO_BETA * weight_pair, DPO_BETA * weight_pair], axis=1)
-    bare_row = jnp.broadcast_to(bare[:, :, None], (pairs, 2, seq)).reshape(1, tokens)
-    bare_row = lax.optimization_barrier(bare_row)
     lane = lax.broadcasted_iota(jnp.int32, (1, tokens), 1)
     weight = bare_row - jnp.where(lane // seq % 2 == 0, scale, 0.0)
     weight = weight.reshape(tokens, 1)
@@ -464,42 +485,40 @@
     other_0 = swapped(own_0, 0)
     other_wv_0 = across(wv, 0)
 
-    below = HEAD_DIM + EXTRA
-    turned = pl.pallas_call(
-        owners_kernel,
-        out_shape=(shaped(width // NY + below, tokens),) * NY,
-        in_specs=[SMEM, SMEM, ANY, VMEM, ANY, VMEM, VMEM],
-        out_specs=(VMEM,) * NY,
-        scratch_shapes=[
-            pltpu.VMEM((width, tokens), BF16),
-            pltpu.VMEM((4, tokens, 896), BF16),
-            pltpu.SemaphoreType.DMA((4,)),
-        ],
-    )(is_upper, y_index, raw, own_1, incoming, own_0, bare_row)
-    blocks = [turned[0]] + [around(turned[s], s) for s in range(1, NY)]
+    blocks_0 = sent(is_lower, incoming, own_0, 0)
 
     first_own = ((zi % 2) * NX + xi).astype(jnp.int32).reshape(1)
     group = width // NY // 2
+
+    def message_specs(wanted):
+        def step(i, on):
+            return i * on[0] if wanted else i * (1 - on[0])
+
+        at = 2 * group
+        return (
+            [pl.BlockSpec((group, tokens), lambda i, own, on: (step(i, on), 0))] * NY
+            + [pl.BlockSpec((HEAD_DIM, tokens), lambda i, own, on: (at // HEAD_DIM, 0))] * NY
+            + [pl.BlockSpec((EXTRA, tokens), lambda i, own, on: ((at + HEAD_DIM) // EXTRA, 0))] * NY
+        )
 
     parts = pl.pallas_call(
         products_kernel,
         out_shape=(shaped(4, share_rows, columns),) * 4,
         grid_spec=pltpu.PrefetchScalarGridSpec(
-            num_scalar_prefetch=1,
+            num_scalar_prefetch=2,
             grid=(2,),
             in_specs=[SMEM]
-            + [pl.BlockSpec((group, tokens), lambda i, own: (i, 0))] * NY
-            + [pl.BlockSpec((HEAD_DIM, tokens), lambda i, own: (2 * group // HEAD_DIM, 0))] * NY
-            + [pl.BlockSpec((EXTRA, tokens), lambda i, own: ((2 * group + HEAD_DIM) // EXTRA, 0))]
-            * NY
-            + [pl.BlockSpec((group, tokens), lambda i, own: (i, 0))] * NY
+            + message_specs(True)
+            + message_specs(False)
+            + [pl.BlockSpec((group, tokens), lambda i, own, on: (i, 0))] * NY
             + [whole_of(tokens, heads * HEAD_DIM)] * NY,
-            out_specs=(pl.BlockSpec((2, share_rows, columns), lambda i, own: (i, 0, 0)),) * 4,
+            out_specs=(pl.BlockSpec((2, share_rows, columns), lambda i, own, on: (i, 0, 0)),)
+            * 4,
             scratch_shapes=[pltpu.VMEM((group, columns), F32)],
         ),
     )(
-        first_own, scale.reshape(1), *after(tuple(blocks), other_0), *blocks, *blocks,
-        *normed_all, *mixed_all,
+        first_own, is_upper, scale.reshape(1), *blocks_1, *blocks_1, *blocks_1,
+        *after(tuple(blocks_0), other_0), *blocks_0, *blocks_0, *normed_all, *mixed_all,
     )
     got = [parts[0]] + [over_xz(parts[k], k) for k in (1, 2, 3)]
     parts = pl.pallas_call(

time: 188 us -> 197 us (1.048)
  the two profiles are of different devices: /device:TPU:4 before, /device:TPU:56 now
where the time goes in v4:
time: 197 us; the launch traced here: 196 us
  starting transfers between devices  70 us (36%)
  waiting for transfers between devices  68.7 us (35%)
  Pallas kernels  42 us (21%)
  local copies, waits for them, and re-layouts  10.9 us (6%)
  other arithmetic  3.16 us (2%)
    ppermute x12, waiting for transfers between devices, around(): return lax.ppermute(block, ('pipe', 'y'), route)  33.7 us
    ppermute x6, waiting for transfers between devices, over_xz(): return lax.ppermute(block, ('z', 'x'), route)  26.7 us
    ppermute x12, starting transfers between devices, around(): return lax.ppermute(block, ('pipe', 'y'), route)  21.3 us
    ppermute x8, starting transfers between devices, exchanged(): return lax.ppermute(block, ('pipe', 'z', 'y', 'x'), route)  21.2 us
    ppermute x6, starting transfers between devices, over_xz(): return lax.ppermute(block, ('z', 'x'), route)  10.1 us
    pallas_call x2, Pallas kernels, values_of(): pl.pallas_call(kernel, out_shape=out_shape, grid_spec=pltpu.PrefetchScala...  8.9 us
    pallas_call x1, Pallas kernels, section_step(): pl.pallas_call(products_kernel, out_shape=(shaped(4, share_rows, columns)...  6.81 us
    pallas_call x2, Pallas kernels, forward(): pl.pallas_call(forward_kernel, out_shape=(shaped(tokens, heads * HEAD_DIM...  6.67 us
  transfers between devices with their start and end apart: 35, of which 13 were waited for; matrix products, arithmetic and copies ran while one was open for 4% of the time, Pallas kernels for 20%

profile of v4, /device:TPU:56, one launch (start us, length us, event | category | flops | bytes accessed | tf_op | source)
XLA Modules:
  0.0 196.5 jit_solution(18072538780639732555)
XLA Ops:
  4.7 3.3 %shard_map.120 = (bf16[256,896]{1,0:T(8,128)(2,1)}, bf16[2,64,448]{2,1,0:T(8,128)(2,1)}, bf16[896,256]{1,0:T(8,128)(2,1)}, bf16[896,256]{1,0:T(8,128)(2,1)}, bf1...) custom-call(s32[1]{0:T(128)} %bitcast.6.y_ref, bf16[256,3584]{1,0:T(8,128)(2,1)} %bitcast.20, f32[1,3584]{1,0:T(1,128)} %refs_5_.3, ...), custom_call_target="tpu_custom_call" | custom-call | tf_op jit(solution)/shard_map/pallas_call | solution.py:314
  8.0 3.4 %shard_map.121 = (bf16[256,896]{1,0:T(8,128)(2,1)}, bf16[2,64,448]{2,1,0:T(8,128)(2,1)}, bf16[896,256]{1,0:T(8,128)(2,1)}, bf16[896,256]{1,0:T(8,128)(2,1)}, bf1...) custom-call(s32[1]{0:T(128)} %bitcast.6.y_ref, ...), custom_call_target="tpu_custom_call", output_to_operand_aliasing={{0}: (5, {}), {2}: (6, {}), {3}: (7, {}), {4}: (8, {}), {5}... | custom-call | tf_op jit(solution)/shard_map/pallas_call | solution.py:314
  12.3 3.3 %shard_map.122 = (bf16[256,128]{1,0:T(8,128)(2,1)}, bf16[256,3584]{1,0:T(8,128)(2,1)}) custom-call(s32[1]{0:T(128)} %bitcast.active_ref.upper_ref, s32[1]{0:T(128)} %bitcast.1.tensor_ref, bf16[2,64,3584]{2,1,0:T(8,128)(2,1)} %bitcast.35, bf16[2,64,3584]{2,1,0:T(8,128)(2,1)} %copy-done.7, f32[256,1]{1,0:T(8,128)} %reshape.237.mask_ref, ...), custom_call_target="tpu_custom_call" | custom-call | tf_op jit(solution)/shard_map/pallas_call | solution.py:368
  17.2 2.6 %shard_map.123.done_ref = bf16[256,3584]{1,0:T(8,128)(2,1)} custom-call(s32[1]{0:T(128)} %bitcast.active_ref.upper_ref, bf16[256,128]{1,0:T(8,128)(2,1)} %get-tuple-element.47.refs_0_.values_ref, bf16[256,128]{1,0:T(8,128)(2,1)} %copy-done.16, bf16[3584,128]{1,0:T(8,128)(2,1)} %bitcast.29, bf16[3584,128]{1,0:T(8,128)(2,1)} %copy-done.8, ...), custom_call_target="tpu_custom_call" | custom-call | tf_op jit(solution)/shard_map/pallas_call | solution.py:387
  22.4 3.6 %collective-permute-start.2 = (s32[8,128]{1,0:T(8,128)S(1)}, s32[8,128]{1,0:T(8,128)S(1)}, u32[]{:S(2)}, u32[]{:S(2)}) collective-permute-start(s32[8,128]{1,0:T(8,128)S(1)} %broadcast_in_dim.11), channel_id=1, source_target_pairs={{0,6},{2,4},{4,2},{6,0},{8,14},{10,12},{12,10},{14,8},{16,22},{18,... | collective-permute-start | bytes 12296 | tf_op jit(solution)/shard_map/ppermute | solution.py:285
  26.0 2.4 %collective-permute-start = (s32[8,128]{1,0:T(8,128)S(1)}, s32[8,128]{1,0:T(8,128)S(1)}, u32[]{:S(2)}, u32[]{:S(2)}) collective-permute-start(s32[8,128]{1,0:T(8,128)S(1)} %broadcast_in_dim.11), channel_id=1, source_target_pairs={{0,2},{2,0},{4,6},{6,4},{8,10},{10,8},{12,14},{14,12},{16,18},{18,... | collective-permute-start | bytes 12296 | tf_op jit(solution)/shard_map/ppermute | solution.py:285
  28.4 3.2 %collective-permute-start.1 = (s32[8,128]{1,0:T(8,128)S(1)}, s32[8,128]{1,0:T(8,128)S(1)}, u32[]{:S(2)}, u32[]{:S(2)}) collective-permute-start(s32[8,128]{1,0:T(8,128)S(1)} %broadcast_in_dim.11), channel_id=1, source_target_pairs={{0,4},{2,6},{4,0},{6,2},{8,12},{10,14},{12,8},{14,10},{16,20},{18,... | collective-permute-start | bytes 12296 | tf_op jit(solution)/shard_map/ppermute | solution.py:285
  33.9 4.1 %collective-permute-start.5 = (s32[8,128]{1,0:T(8,128)S(1)}, s32[8,128]{1,0:T(8,128)S(1)}, u32[]{:S(2)}, u32[]{:S(2)}) collective-permute-start(s32[8,128]{1,0:T(8,128)S(1)} %add_add_fusion.1), channel_id=1, source_target_pairs={{0,24},{2,26},{4,28},{6,30},{8,16},{10,18},{12,20},{14,22},{16,8},... | collective-permute-start | bytes 12296 | tf_op jit(solution)/shard_map/ppermute | solution.py:285
  38.0 2.1 %collective-permute-start.3 = (s32[8,128]{1,0:T(8,128)S(1)}, s32[8,128]{1,0:T(8,128)S(1)}, u32[]{:S(2)}, u32[]{:S(2)}) collective-permute-start(s32[8,128]{1,0:T(8,128)S(1)} %add_add_fusion.1), channel_id=1, source_target_pairs={{0,16},{2,18},{4,20},{6,22},{8,24},{10,26},{12,28},{14,30},{16,0},... | collective-permute-start | bytes 12296 | tf_op jit(solution)/shard_map/ppermute | solution.py:285
  40.2 4.5 %collective-permute-start.4 = (s32[8,128]{1,0:T(8,128)S(1)}, s32[8,128]{1,0:T(8,128)S(1)}, u32[]{:S(2)}, u32[]{:S(2)}) collective-permute-start(s32[8,128]{1,0:T(8,128)S(1)} %add_add_fusion.1), channel_id=1, source_target_pairs={{0,8},{2,10},{4,12},{6,14},{8,0},{10,2},{12,4},{14,6},{16,24},{18,... | collective-permute-start | bytes 12296 | tf_op jit(solution)/shard_map/ppermute | solution.py:285
  47.2 3.0 %collective-permute-start.6 = (s32[8,128]{1,0:T(8,128)S(1)}, s32[8,128]{1,0:T(8,128)S(1)}, u32[]{:S(2)}, u32[]{:S(2)}) collective-permute-start(s32[8,128]{1,0:T(8,128)S(1)} %add_add_fusion), channel_id=1, source_target_pairs={{0,128},{1,129},{2,130},{3,131},{4,132},{5,133},{6,134},{7,135},{8... | collective-permute-start | bytes 12296 | tf_op jit(solution)/shard_map/ppermute | solution.py:473
  54.4 5.6 %shard_map.124.refs_0_.values_ref = bf16[256,128]{1,0:T(8,128)(2,1)} custom-call(s32[1]{0:T(128)S(6)} %sub.35.active_ref, bf16[256,3584]{1,0:T(8,128)(2,1)} %copy-done, bf16[896,3584]{1,0:T(8,128)(2,1)} %bitcast.25, bf16[2,64,448]{2,1,0:T(8,128)(2,1)} %get-tuple-element.40.a_ref, bf16[2,64,448]{2,1,0:T(8,128)(2,1)} %get-tuple-element.46.b_ref), custom_call_target="tpu_custom_call" | custom-call | tf_op jit(solution)/shard_map/pallas_call | solution.py:368
  60.0 4.2 %shard_map.127 = (bf16[1040,256]{1,0:T(8,128)(2,1)}, bf16[1040,256]{1,0:T(8,128)(2,1)}, bf16[1040,256]{1,0:T(8,128)(2,1)}, bf16[1040,256]{1,0:T(8,128)(2,1)}) custom-call(s32[1]{0:T(128)S(6)} %sub.35.active_ref, s32[1]{0:T(128)} %bitcast.6.y_ref, bf16[256,3584]{1,0:T(8,128)(2,1)} %copy-done, bf16[256,128]{1,0:T(8,128)(2,1)} %shard_map.124.refs_0_.values_ref, ...), custom_call_target="tpu_custom_call" | custom-call | tf_op jit(solution)/shard_map/pallas_call | solution.py:458
  64.2 4.8 %collective-permute-start.19 = (bf16[1040,256]{1,0:T(8,128)(2,1)}, bf16[1040,256]{1,0:T(8,128)(2,1)S(1)}, u32[]{:S(2)}, u32[]{:S(2)}) collective-permute-start(bf16[1040,256]{1,0:T(8,128)(2,1)} %get-tuple-element.54), channel_id=1, source_target_pairs={{0,4},{4,8},{8,12},{12,0},{1,5},{5,9},{9,13},{13,1},{2,6},{6,10},{... | collective-permute-start | bytes 1597448 | tf_op jit(solution)/shard_map/ppermute | solution.py:343
  70.4 4.4 %collective-permute-done.9 = s32[8,128]{1,0:T(8,128)S(1)} collective-permute-done((s32[8,128]{1,0:T(8,128)S(1)}, s32[8,128]{1,0:T(8,128)S(1)}, u32[]{:S(2)}, u32[]{:S(2)}) %collective-permute-start.9) | collective-permute-done | bytes 4128 | tf_op jit(solution)/shard_map/ppermute | solution.py:476
  74.8 2.9 %collective-permute-start.25 = (bf16[256,896]{1,0:T(8,128)(2,1)S(1)}, bf16[256,896]{1,0:T(8,128)(2,1)S(1)}, u32[]{:S(2)}, u32[]{:S(2)}) collective-permute-start(bf16[256,896]{1,0:T(8,128)(2,1)S(1)} %copy-done.6), channel_id=1, source_target_pairs={{0,4},{4,8},{8,12},{12,0},{128,132},{132,136},{136,140},{140,128},... | collective-permute-start | bytes 1376264 | tf_op jit(solution)/shard_map/ppermute | solution.py:343
  77.7 5.4 %collective-permute-start.20 = (bf16[1040,256]{1,0:T(8,128)(2,1)}, bf16[1040,256]{1,0:T(8,128)(2,1)S(1)}, u32[]{:S(2)}, u32[]{:S(2)}) collective-permute-start(bf16[1040,256]{1,0:T(8,128)(2,1)} %get-tuple-element.55), channel_id=1, source_target_pairs={{0,8},{4,12},{8,0},{12,4},{1,9},{5,13},{9,1},{13,5},{2,10},{6,14},... | collective-permute-start | bytes 1597448 | tf_op jit(solution)/shard_map/ppermute | solution.py:343
  83.1 1.9 collective-permute-start.21
  85.1 18.3 %collective-permute-done.25.refs_29_ = bf16[256,896]{1,0:T(8,128)(2,1)S(1)} collective-permute-done((bf16[256,896]{1,0:T(8,128)(2,1)S(1)}, bf16[256,896]{1,0:T(8,128)(2,1)S(1)}, u32[]{:S(2)}, u32[]{:S(2)}) %collective-permute-start.25) | collective-permute-done | bytes 458784 | tf_op jit(solution)/shard_map/ppermute | solution.py:343
  103.3 4.1 %collective-permute-start.14 = (bf16[256,128]{1,0:T(8,128)(2,1)}, bf16[256,128]{1,0:T(8,128)(2,1)}, u32[]{:S(2)}, u32[]{:S(2)}) collective-permute-start(bf16[256,128]{1,0:T(8,128)(2,1)} %shard_map.124.refs_0_.values_ref), channel_id=1, source_target_pairs={{0,1},{1,0},{2,3},{3,2},{4,5},{5,4},{6,7},{7,6},{8,9},{9,8},{10,11... | collective-permute-start | bytes 196616 | tf_op jit(solution)/shard_map/ppermute | solution.py:436
  107.5 2.2 %shard_map.126 = (bf16[1040,256]{1,0:T(8,128)(2,1)}, bf16[1040,256]{1,0:T(8,128)(2,1)}, bf16[1040,256]{1,0:T(8,128)(2,1)}, bf16[1040,256]{1,0:T(8,128)(2,1)}) custom-call(s32[1]{0:T(128)} %bitcast.active_ref.upper_ref, s32[1]{0:T(128)} %bitcast.6.y_ref, bf16[256,3584]{1,0:T(8,128)(2,1)} %get-tuple-element.48.refs_6_.dy_hbm, ...), custom_call_target="tpu_custom_call" | custom-call | tf_op jit(solution)/shard_map/pallas_call | solution.py:458
  114.5 4.0 %collective-permute-start.15 = (bf16[3584,128]{1,0:T(8,128)(2,1)S(1)}, bf16[3584,128]{1,0:T(8,128)(2,1)}, u32[]{:S(2)}, u32[]{:S(2)}) collective-permute-start(bf16[3584,128]{1,0:T(8,128)(2,1)S(1)} %bitcast.31), channel_id=1, source_target_pairs={{0,3},{3,0},{1,2},{2,1},{4,7},{7,4},{5,6},{6,5},{8,11},{11,8},{9,1... | collective-permute-start | bytes 2752520 | tf_op jit(solution)/shard_map/ppermute | solution.py:303
  119.7 15.4 %collective-permute-done.27.refs_31_ = bf16[256,896]{1,0:T(8,128)(2,1)} collective-permute-done((bf16[256,896]{1,0:T(8,128)(2,1)S(1)}, bf16[256,896]{1,0:T(8,128)(2,1)}, u32[]{:S(2)}, u32[]{:S(2)}) %collective-permute-start.27) | collective-permute-done | bytes 458784 | tf_op jit(solution)/shard_map/ppermute | solution.py:343
  135.9 6.8 %shard_map.128 = (bf16[4,56,1024]{2,1,0:T(8,128)(2,1)}, bf16[4,56,1024]{2,1,0:T(8,128)(2,1)}, bf16[4,56,1024]{2,1,0:T(8,128)(2,1)}, bf16[4,56,1024]{2,1,0:T(8,128)(2,1)}) custom-call(s32[1]{0:T(128)} %bitcast.13.own_ref, s32[1]{0:T(128)} %bitcast.active_ref.upper_ref, f32[1]{0:T(128)} %bitcast.14.scale_ref, ...), custom_call_target="tpu_custom_call" | custom-call | tf_op jit(solution)/shard_map/pallas_call | solution.py:504
  148.2 3.5 %collective-permute-done.28.b_ref = bf16[4,56,1024]{2,1,0:T(8,128)(2,1)S(1)} collective-permute-done((bf16[4,56,1024]{2,1,0:T(8,128)(2,1)}, bf16[4,56,1024]{2,1,0:T(8,128)(2,1)S(1)}, u32[]{:S(2)}, u32[]{:S(2)}) %collective-permute-start.28) | collective-permute-done | bytes 458784 | tf_op jit(solution)/shard_map/ppermute | solution.py:29
  152.7 10.6 %collective-permute-done.30.d_ref = bf16[4,56,1024]{2,1,0:T(8,128)(2,1)S(1)} collective-permute-done((bf16[4,56,1024]{2,1,0:T(8,128)(2,1)}, bf16[4,56,1024]{2,1,0:T(8,128)(2,1)S(1)}, u32[]{:S(2)}, u32[]{:S(2)}) %collective-permute-start.30) | collective-permute-done | bytes 458784 | tf_op jit(solution)/shard_map/ppermute | solution.py:29
  164.1 2.3 %shard_map.129 = (f32[56,1024]{1,0:T(8,128)}, bf16[56,1024]{1,0:T(8,128)(2,1)}, bf16[56,1024]{1,0:T(8,128)(2,1)}, bf16[56,1024]{1,0:T(8,128)(2,1)}) custom-call(s32[1]{0:T(128)} %bitcast.12.own_ref, bf16[4,56,1024]{2,1,0:T(8,128)(2,1)} %get-tuple-element.66.a_ref, bf16[4,56,1024]{2,1,0:T(8,128)(2,1)} %copy-done.10, bf16[4,56,1024]{2,1,0:T(8,128)(2,1)} %copy-done.11, ...), custom_call_target="tpu_custom_call" | custom-call | tf_op jit(solution)/shard_map/pallas_call | solution.py:524
  169.1 3.8 %collective-permute-start.33 = (bf16[56,1024]{1,0:T(8,128)(2,1)}, bf16[56,1024]{1,0:T(8,128)(2,1)S(1)}, u32[]{:S(2)}, u32[]{:S(2)}) collective-permute-start(bf16[56,1024]{1,0:T(8,128)(2,1)} %get-tuple-element.73), channel_id=1, source_target_pairs={{0,96},{2,98},{16,112},{18,114},{32,64},{34,66},{48,80},{50,82},{6... | collective-permute-start | bytes 344072 | tf_op jit(solution)/shard_map/ppermute | solution.py:29
  174.4 2.5 %collective-permute-done.32.c_ref = bf16[56,1024]{1,0:T(8,128)(2,1)S(1)} collective-permute-done((bf16[56,1024]{1,0:T(8,128)(2,1)}, bf16[56,1024]{1,0:T(8,128)(2,1)S(1)}, u32[]{:S(2)}, u32[]{:S(2)}) %collective-permute-start.32) | collective-permute-done | bytes 114720 | tf_op jit(solution)/shard_map/ppermute | solution.py:29
  177.0 7.6 %collective-permute-done.33.d_ref = bf16[56,1024]{1,0:T(8,128)(2,1)S(1)} collective-permute-done((bf16[56,1024]{1,0:T(8,128)(2,1)}, bf16[56,1024]{1,0:T(8,128)(2,1)S(1)}, u32[]{:S(2)}, u32[]{:S(2)}) %collective-permute-start.33) | collective-permute-done | bytes 114720 | tf_op jit(solution)/shard_map/ppermute | solution.py:29
  189.2 4.9 %shard_map.125 = bf16[1,128,3584]{2,1,0:T(8,128)(2,1)} custom-call(s32[1]{0:T(128)S(6)} %sub.35.active_ref, s32[1]{0:T(128)} %bitcast.1.tensor_ref, f32[256,1]{1,0:T(8,128)} %copy.20.weight_ref, bf16[256,3584]{1,0:T(8,128)(2,1)} %shard_map.123.done_ref, bf16[256,128]{1,0:T(8,128)(2,1)} %shard_map.124.refs_0_.values_ref, ...), custom_call_target="tpu_custom_call" | custom-call | tf_op jit(solution)/shard_map/pallas_call | solution.py:413
  194.1 1.8 shard_map.131
  (116 shorter events, 42.0 us)
Async XLA Ops:
  0.6 10.7 %collective-permute-start.10 = (bf16[2,64,3584]{2,1,0:T(8,128)(2,1)}, bf16[2,64,3584]{2,1,0:T(8,128)(2,1)S(1)}, u32[]{:S(2)}, u32[]{:S(2)}) collective-permute-start(bf16[2,64,3584]{2,1,0:T(8,128)(2,1)} %bitcast.34), channel_id=1, source_target_pairs={{128,129},{129,128},{130,131},{131,130},{132,133},{133,132},{134,1... | collective-permute-start | bytes 2752520 | tf_op jit(solution)/shard_map/ppermute | solution.py:268
  1.4 14.9 %collective-permute-start.12 = (bf16[3584,128]{1,0:T(8,128)(2,1)}, bf16[3584,128]{1,0:T(8,128)(2,1)S(1)}, u32[]{:S(2)}, u32[]{:S(2)}) collective-permute-start(bf16[3584,128]{1,0:T(8,128)(2,1)} %bitcast.26), channel_id=1, source_target_pairs={{128,131},{131,128},{129,130},{130,129},{132,135},{135,132},{133,1... | collective-permute-start | bytes 2752520 | tf_op jit(solution)/shard_map/ppermute | solution.py:303
  19.7 33.4 %collective-permute-start.13 = (bf16[256,3584]{1,0:T(8,128)(2,1)}, bf16[256,3584]{1,0:T(8,128)(2,1)S(1)}, u32[]{:S(2)}, u32[]{:S(2)}) collective-permute-start(bf16[256,3584]{1,0:T(8,128)(2,1)} %shard_map.123.done_ref), channel_id=1, source_target_pairs={{128,0},{129,1},{130,2},{131,3},{132,4},{133,5},{134,6},{135,7},{1... | collective-permute-start | bytes 5505032 | tf_op jit(solution)/shard_map/ppermute | solution.py:450
  22.4 9.7 %collective-permute-start.2 = (s32[8,128]{1,0:T(8,128)S(1)}, s32[8,128]{1,0:T(8,128)S(1)}, u32[]{:S(2)}, u32[]{:S(2)}) collective-permute-start(s32[8,128]{1,0:T(8,128)S(1)} %broadcast_in_dim.11), channel_id=1, source_target_pairs={{0,6},{2,4},{4,2},{6,0},{8,14},{10,12},{12,10},{14,8},{16,22},{18,... | collective-permute-start | bytes 12296 | tf_op jit(solution)/shard_map/ppermute | solution.py:285
  26.0 6.1 %collective-permute-start = (s32[8,128]{1,0:T(8,128)S(1)}, s32[8,128]{1,0:T(8,128)S(1)}, u32[]{:S(2)}, u32[]{:S(2)}) collective-permute-start(s32[8,128]{1,0:T(8,128)S(1)} %broadcast_in_dim.11), channel_id=1, source_target_pairs={{0,2},{2,0},{4,6},{6,4},{8,10},{10,8},{12,14},{14,12},{16,18},{18,... | collective-permute-start | bytes 12296 | tf_op jit(solution)/shard_map/ppermute | solution.py:285
  28.4 5.5 %collective-permute-start.1 = (s32[8,128]{1,0:T(8,128)S(1)}, s32[8,128]{1,0:T(8,128)S(1)}, u32[]{:S(2)}, u32[]{:S(2)}) collective-permute-start(s32[8,128]{1,0:T(8,128)S(1)} %broadcast_in_dim.11), channel_id=1, source_target_pairs={{0,4},{2,6},{4,0},{6,2},{8,12},{10,14},{12,8},{14,10},{16,20},{18,... | collective-permute-start | bytes 12296 | tf_op jit(solution)/shard_map/ppermute | solution.py:285
  31.6 46.1 %collective-permute-start.22 = (bf16[896,256]{1,0:T(8,128)(2,1)}, bf16[896,256]{1,0:T(8,128)(2,1)}, u32[]{:S(2)}, u32[]{:S(2)}) collective-permute-start(bf16[896,256]{1,0:T(8,128)(2,1)} %get-tuple-element.62), channel_id=1, source_target_pairs={{0,4},{4,8},{8,12},{12,0},{128,132},{132,136},{136,140},{140,128},... | collective-permute-start | bytes 1376264 | tf_op jit(solution)/shard_map/ppermute | solution.py:343
  33.9 10.8 %collective-permute-start.5 = (s32[8,128]{1,0:T(8,128)S(1)}, s32[8,128]{1,0:T(8,128)S(1)}, u32[]{:S(2)}, u32[]{:S(2)}) collective-permute-start(s32[8,128]{1,0:T(8,128)S(1)} %add_add_fusion.1), channel_id=1, source_target_pairs={{0,24},{2,26},{4,28},{6,30},{8,16},{10,18},{12,20},{14,22},{16,8},... | collective-permute-start | bytes 12296 | tf_op jit(solution)/shard_map/ppermute | solution.py:285
  38.0 7.8 %collective-permute-start.3 = (s32[8,128]{1,0:T(8,128)S(1)}, s32[8,128]{1,0:T(8,128)S(1)}, u32[]{:S(2)}, u32[]{:S(2)}) collective-permute-start(s32[8,128]{1,0:T(8,128)S(1)} %add_add_fusion.1), channel_id=1, source_target_pairs={{0,16},{2,18},{4,20},{6,22},{8,24},{10,26},{12,28},{14,30},{16,0},... | collective-permute-start | bytes 12296 | tf_op jit(solution)/shard_map/ppermute | solution.py:285
  40.2 7.0 %collective-permute-start.4 = (s32[8,128]{1,0:T(8,128)S(1)}, s32[8,128]{1,0:T(8,128)S(1)}, u32[]{:S(2)}, u32[]{:S(2)}) collective-permute-start(s32[8,128]{1,0:T(8,128)S(1)} %add_add_fusion.1), channel_id=1, source_target_pairs={{0,8},{2,10},{4,12},{6,14},{8,0},{10,2},{12,4},{14,6},{16,24},{18,... | collective-permute-start | bytes 12296 | tf_op jit(solution)/shard_map/ppermute | solution.py:285
  44.8 32.9 %collective-permute-start.23 = (bf16[896,256]{1,0:T(8,128)(2,1)}, bf16[896,256]{1,0:T(8,128)(2,1)}, u32[]{:S(2)}, u32[]{:S(2)}) collective-permute-start(bf16[896,256]{1,0:T(8,128)(2,1)} %get-tuple-element.63), channel_id=1, source_target_pairs={{0,8},{4,12},{8,0},{12,4},{128,136},{132,140},{136,128},{140,132},... | collective-permute-start | bytes 1376264 | tf_op jit(solution)/shard_map/ppermute | solution.py:343
  45.8 37.3 %collective-permute-start.24 = (bf16[896,256]{1,0:T(8,128)(2,1)}, bf16[896,256]{1,0:T(8,128)(2,1)}, u32[]{:S(2)}, u32[]{:S(2)}) collective-permute-start(bf16[896,256]{1,0:T(8,128)(2,1)} %get-tuple-element.64), channel_id=1, source_target_pairs={{0,12},{4,0},{8,4},{12,8},{128,140},{132,128},{136,132},{140,136},... | collective-permute-start | bytes 1376264 | tf_op jit(solution)/shard_map/ppermute | solution.py:343
  51.8 17.3 %collective-permute-start.8 = (s32[8,128]{1,0:T(8,128)S(1)}, s32[8,128]{1,0:T(8,128)S(1)}, u32[]{:S(2)}, u32[]{:S(2)}) collective-permute-start(s32[8,128]{1,0:T(8,128)S(1)} %add.81), channel_id=1, source_target_pairs={{128,192},{130,194},{132,196},{134,198},{136,200},{138,202},{140,2... | collective-permute-start | bytes 12296 | tf_op jit(solution)/shard_map/ppermute | solution.py:285
  64.2 48.8 %collective-permute-start.19 = (bf16[1040,256]{1,0:T(8,128)(2,1)}, bf16[1040,256]{1,0:T(8,128)(2,1)S(1)}, u32[]{:S(2)}, u32[]{:S(2)}) collective-permute-start(bf16[1040,256]{1,0:T(8,128)(2,1)} %get-tuple-element.54), channel_id=1, source_target_pairs={{0,4},{4,8},{8,12},{12,0},{1,5},{5,9},{9,13},{13,1},{2,6},{6,10},{... | collective-permute-start | bytes 1597448 | tf_op jit(solution)/shard_map/ppermute | solution.py:343
  69.1 5.7 %collective-permute-start.9 = (s32[8,128]{1,0:T(8,128)S(1)}, s32[8,128]{1,0:T(8,128)S(1)}, u32[]{:S(2)}, u32[]{:S(2)}) collective-permute-start(s32[8,128]{1,0:T(8,128)S(1)} %add.82), channel_id=1, source_target_pairs={{128,0},{129,1},{130,2},{131,3},{132,4},{133,5},{134,6},{135,7},{1... | collective-permute-start | bytes 12296 | tf_op jit(solution)/shard_map/ppermute | solution.py:476
  74.8 28.6 %collective-permute-start.25 = (bf16[256,896]{1,0:T(8,128)(2,1)S(1)}, bf16[256,896]{1,0:T(8,128)(2,1)S(1)}, u32[]{:S(2)}, u32[]{:S(2)}) collective-permute-start(bf16[256,896]{1,0:T(8,128)(2,1)S(1)} %copy-done.6), channel_id=1, source_target_pairs={{0,4},{4,8},{8,12},{12,0},{128,132},{132,136},{136,140},{140,128},... | collective-permute-start | bytes 1376264 | tf_op jit(solution)/shard_map/ppermute | solution.py:343
  77.7 32.0 %collective-permute-start.26 = (bf16[256,896]{1,0:T(8,128)(2,1)S(1)}, bf16[256,896]{1,0:T(8,128)(2,1)}, u32[]{:S(2)}, u32[]{:S(2)}) collective-permute-start(bf16[256,896]{1,0:T(8,128)(2,1)S(1)} %copy-done.6), channel_id=1, source_target_pairs={{0,8},{4,12},{8,0},{12,4},{128,136},{132,140},{136,128},{140,132},... | collective-permute-start | bytes 1376264 | tf_op jit(solution)/shard_map/ppermute | solution.py:343
  77.7 36.7 %collective-permute-start.20 = (bf16[1040,256]{1,0:T(8,128)(2,1)}, bf16[1040,256]{1,0:T(8,128)(2,1)S(1)}, u32[]{:S(2)}, u32[]{:S(2)}) collective-permute-start(bf16[1040,256]{1,0:T(8,128)(2,1)} %get-tuple-element.55), channel_id=1, source_target_pairs={{0,8},{4,12},{8,0},{12,4},{1,9},{5,13},{9,1},{13,5},{2,10},{6,14},... | collective-permute-start | bytes 1597448 | tf_op jit(solution)/shard_map/ppermute | solution.py:343
  83.1 31.3 %collective-permute-start.21 = (bf16[1040,256]{1,0:T(8,128)(2,1)}, bf16[1040,256]{1,0:T(8,128)(2,1)S(1)}, u32[]{:S(2)}, u32[]{:S(2)}) collective-permute-start(bf16[1040,256]{1,0:T(8,128)(2,1)} %get-tuple-element.56), channel_id=1, source_target_pairs={{0,12},{4,0},{8,4},{12,8},{1,13},{5,1},{9,5},{13,9},{2,14},{6,2},{... | collective-permute-start | bytes 1597448 | tf_op jit(solution)/shard_map/ppermute | solution.py:343
  103.3 8.0 %collective-permute-start.14 = (bf16[256,128]{1,0:T(8,128)(2,1)}, bf16[256,128]{1,0:T(8,128)(2,1)}, u32[]{:S(2)}, u32[]{:S(2)}) collective-permute-start(bf16[256,128]{1,0:T(8,128)(2,1)} %shard_map.124.refs_0_.values_ref), channel_id=1, source_target_pairs={{0,1},{1,0},{2,3},{3,2},{4,5},{5,4},{6,7},{7,6},{8,9},{9,8},{10,11... | collective-permute-start | bytes 196616 | tf_op jit(solution)/shard_map/ppermute | solution.py:436
  109.7 25.3 %collective-permute-start.16 = (bf16[1040,256]{1,0:T(8,128)(2,1)}, bf16[1040,256]{1,0:T(8,128)(2,1)S(1)}, u32[]{:S(2)}, u32[]{:S(2)}) collective-permute-start(bf16[1040,256]{1,0:T(8,128)(2,1)} %get-tuple-element.50), channel_id=1, source_target_pairs={{128,132},{132,136},{136,140},{140,128},{129,133},{133,137},{137,1... | collective-permute-start | bytes 1597448 | tf_op jit(solution)/shard_map/ppermute | solution.py:343
  111.3 23.8 %collective-permute-start.17 = (bf16[1040,256]{1,0:T(8,128)(2,1)}, bf16[1040,256]{1,0:T(8,128)(2,1)}, u32[]{:S(2)}, u32[]{:S(2)}) collective-permute-start(bf16[1040,256]{1,0:T(8,128)(2,1)} %get-tuple-element.51), channel_id=1, source_target_pairs={{128,136},{132,140},{136,128},{140,132},{129,137},{133,141},{137,1... | collective-permute-start | bytes 1597448 | tf_op jit(solution)/shard_map/ppermute | solution.py:343
  113.0 22.1 %collective-permute-start.18 = (bf16[1040,256]{1,0:T(8,128)(2,1)}, bf16[1040,256]{1,0:T(8,128)(2,1)}, u32[]{:S(2)}, u32[]{:S(2)}) collective-permute-start(bf16[1040,256]{1,0:T(8,128)(2,1)} %get-tuple-element.52), channel_id=1, source_target_pairs={{128,140},{132,128},{136,132},{140,136},{129,141},{133,129},{137,1... | collective-permute-start | bytes 1597448 | tf_op jit(solution)/shard_map/ppermute | solution.py:343
  114.5 20.6 %collective-permute-start.27 = (bf16[256,896]{1,0:T(8,128)(2,1)S(1)}, bf16[256,896]{1,0:T(8,128)(2,1)}, u32[]{:S(2)}, u32[]{:S(2)}) collective-permute-start(bf16[256,896]{1,0:T(8,128)(2,1)S(1)} %copy-done.6), channel_id=1, source_target_pairs={{0,12},{4,0},{8,4},{12,8},{128,140},{132,128},{136,132},{140,136},... | collective-permute-start | bytes 1376264 | tf_op jit(solution)/shard_map/ppermute | solution.py:343
  114.5 74.7 %collective-permute-start.15 = (bf16[3584,128]{1,0:T(8,128)(2,1)S(1)}, bf16[3584,128]{1,0:T(8,128)(2,1)}, u32[]{:S(2)}, u32[]{:S(2)}) collective-permute-start(bf16[3584,128]{1,0:T(8,128)(2,1)S(1)} %bitcast.31), channel_id=1, source_target_pairs={{0,3},{3,0},{1,2},{2,1},{4,7},{7,4},{5,6},{6,5},{8,11},{11,8},{9,1... | collective-permute-start | bytes 2752520 | tf_op jit(solution)/shard_map/ppermute | solution.py:303
  142.7 9.0 %collective-permute-start.28 = (bf16[4,56,1024]{2,1,0:T(8,128)(2,1)}, bf16[4,56,1024]{2,1,0:T(8,128)(2,1)S(1)}, u32[]{:S(2)}, u32[]{:S(2)}) collective-permute-start(bf16[4,56,1024]{2,1,0:T(8,128)(2,1)} %get-tuple-element.67), channel_id=1, source_target_pairs={{0,2},{2,0},{16,18},{18,16},{32,34},{34,32},{48,50},{50,48},{64,66... | collective-permute-start | bytes 1376264 | tf_op jit(solution)/shard_map/ppermute | solution.py:29
  143.5 9.2 %collective-permute-start.29 = (bf16[4,56,1024]{2,1,0:T(8,128)(2,1)}, bf16[4,56,1024]{2,1,0:T(8,128)(2,1)S(1)}, u32[]{:S(2)}, u32[]{:S(2)}) collective-permute-start(bf16[4,56,1024]{2,1,0:T(8,128)(2,1)} %get-tuple-element.68), channel_id=1, source_target_pairs={{0,16},{2,18},{16,0},{18,2},{32,48},{34,50},{48,32},{50,34},{64,80... | collective-permute-start | bytes 1376264 | tf_op jit(solution)/shard_map/ppermute | solution.py:29
  144.5 18.8 %collective-permute-start.30 = (bf16[4,56,1024]{2,1,0:T(8,128)(2,1)}, bf16[4,56,1024]{2,1,0:T(8,128)(2,1)S(1)}, u32[]{:S(2)}, u32[]{:S(2)}) collective-permute-start(bf16[4,56,1024]{2,1,0:T(8,128)(2,1)} %get-tuple-element.69), channel_id=1, source_target_pairs={{0,18},{2,16},{16,2},{18,0},{32,50},{34,48},{48,34},{50,32},{64,82... | collective-permute-start | bytes 1376264 | tf_op jit(solution)/shard_map/ppermute | solution.py:29
  166.4 8.0 %collective-permute-start.31 = (bf16[56,1024]{1,0:T(8,128)(2,1)}, bf16[56,1024]{1,0:T(8,128)(2,1)S(1)}, u32[]{:S(2)}, u32[]{:S(2)}) collective-permute-start(bf16[56,1024]{1,0:T(8,128)(2,1)} %get-tuple-element.71), channel_id=1, source_target_pairs={{0,32},{2,34},{16,48},{18,50},{32,0},{34,2},{48,16},{50,18},{64,96... | collective-permute-start | bytes 344072 | tf_op jit(solution)/shard_map/ppermute | solution.py:29
  167.9 9.1 %collective-permute-start.32 = (bf16[56,1024]{1,0:T(8,128)(2,1)}, bf16[56,1024]{1,0:T(8,128)(2,1)S(1)}, u32[]{:S(2)}, u32[]{:S(2)}) collective-permute-start(bf16[56,1024]{1,0:T(8,128)(2,1)} %get-tuple-element.72), channel_id=1, source_target_pairs={{0,64},{2,66},{16,80},{18,82},{32,96},{34,98},{48,112},{50,114},{6... | collective-permute-start | bytes 344072 | tf_op jit(solution)/shard_map/ppermute | solution.py:29
  169.1 15.5 %collective-permute-start.33 = (bf16[56,1024]{1,0:T(8,128)(2,1)}, bf16[56,1024]{1,0:T(8,128)(2,1)S(1)}, u32[]{:S(2)}, u32[]{:S(2)}) collective-permute-start(bf16[56,1024]{1,0:T(8,128)(2,1)} %get-tuple-element.73), channel_id=1, source_target_pairs={{0,96},{2,98},{16,112},{18,114},{32,64},{34,66},{48,80},{50,82},{6... | collective-permute-start | bytes 344072 | tf_op jit(solution)/shard_map/ppermute | solution.py:29
  186.7 9.2 %collective-permute-start.34 = (f32[1,56]{1,0:T(1,128)}, f32[1,56]{1,0:T(1,128)S(1)}, u32[]{:S(2)}, u32[]{:S(2)}) collective-permute-start(f32[1,56]{1,0:T(1,128)} %get-tuple-element.75), channel_id=1, source_target_pairs={{0,1},{1,0},{2,3},{3,2},{4,5},{5,4},{6,7},{7,6},{8,9},{9,8},{10,11... | collective-permute-start | bytes 680 | tf_op jit(solution)/shard_map/ppermute | solution.py:19
  (24 other events, 269.7 us)

commit v5 on v3

--- a/solution.py
+++ b/solution.py
@@ -52,12 +52,11 @@
 
 
 def forward_kernel(y_ref, x_ref, gain_ref, wv_ref, pattern_ref, *refs):
-    mixed_ref, turned_ref, normed_refs, normed_t_ref = refs[-7], refs[-6], refs[-5:-1], refs[-1]
+    turned_ref, operand_refs, normed_t_ref, mixed_ref = refs[-7], refs[-6:-2], refs[-2], refs[-1]
     heads, seq = pattern_ref.shape[1:3]
     x = x_ref[...].astype(F32)
     normed = (x * rms_of(x) * gain_ref[...]).astype(BF16)
     normed_t_ref[...] = normed.T
-    deal(normed_refs, normed_t_ref, y_ref[0])
     values = dot(normed, wv_ref[...], ((1,), (0,))).astype(BF16)
     for part in range(2):
         at = slice(part * seq, (part + 1) * seq)
@@ -66,6 +65,11 @@
         mixed = dot(pattern, values[at], ((1,), (0,))).astype(BF16)
         for h in range(heads):
             mixed_ref[at, h * HEAD_DIM : (h + 1) * HEAD_DIM] = mixed[h * seq : (h + 1) * seq]
+    mixed_t = mixed_ref[...].T
+    above = mixed_t.shape[0]
+    for operand_ref in operand_refs:
+        operand_ref[:above] = mixed_t
+    deal([r.at[above:] for r in operand_refs], normed_t_ref, y_ref[0])
 
 
 def add_values(step, dy, wo_ref, turned_refs, values_ref, mixed_ref):
@@ -196,7 +200,7 @@
         weight = rows[0:1] + rows[1:2] - chosen
         dy = (weight * dy_ref[...].astype(F32)).astype(BF16)
         values_t = (weight * values_ref[...].astype(F32)).astype(BF16)
-        output = output + dot(dy, mixed_ref[...], ((1,), (0,)))
+        output = output + dot(dy, mixed_ref[...], ((1,), (1,)))
         value = value + dot(normed_ref[...], values_t, ((1,), (1,)))
     total_ref[:, :HEAD_DIM] = value
     total_ref[:, HEAD_DIM:] = output
@@ -308,11 +312,13 @@
 
     y_index = yi.astype(jnp.int32).reshape(1)
 
+    above = heads * HEAD_DIM
+
     def forward(p, *earlier):
         return pl.pallas_call(
             forward_kernel,
-            out_shape=(shaped(tokens, heads * HEAD_DIM), shaped(2, seq, heads * seq))
-            + (shaped(width // NY, tokens),) * NY,
+            out_shape=(shaped(2, seq, heads * seq),)
+            + (shaped(above + width // NY, tokens),) * NY,
             grid_spec=pltpu.PrefetchScalarGridSpec(
                 num_scalar_prefetch=1,
                 grid=(1,),
@@ -323,30 +329,26 @@
                     pl.BlockSpec((2, heads, seq, seq), lambda i, y: (p, 0, 0, 0)),
                 ]
                 + [ANY] * len(earlier),
-                out_specs=(
-                    pl.BlockSpec((half, heads * HEAD_DIM), lambda i, y: (p, 0)),
-                    pl.BlockSpec((2, seq, heads * seq), lambda i, y: (0, 0, 0)),
-                )
-                + (pl.BlockSpec((width // NY, half), lambda i, y: (0, p)),) * NY,
-                scratch_shapes=[pltpu.VMEM((width, half), BF16)],
+                out_specs=(pl.BlockSpec((2, seq, heads * seq), lambda i, y: (0, 0, 0)),)
+                + (pl.BlockSpec((above + width // NY, half), lambda i, y: (0, p)),) * NY,
+                scratch_shapes=[pltpu.VMEM((width, half), BF16), pltpu.VMEM((half, above), BF16)],
             ),
-            input_output_aliases={5: 0, 6: 2, 7: 3, 8: 4, 9: 5} if earlier else {},
+            input_output_aliases={5 + n: 1 + n for n in range(len(earlier))},
         )(y_index, x, norm_gain, wv, patterns, *earlier)
 
-    mixed, turned_0, *normed = forward(0)
-    mixed, turned_1, *normed = forward(1, mixed, *normed)
+    turned_0, *operands = forward(0)
+    turned_1, *operands = forward(1, *operands)
 
     def around(block, shift):
         return lax.ppermute(block, "y", [(i, (i + shift) % NY) for i in range(NY)])
 
-    mixed_all = [mixed] + [around(mixed, s) for s in range(1, NY)]
-    normed_all = [normed[0]] + [around(normed[s], s) for s in range(1, NY)]
+    operands = [operands[0]] + [around(operands[s], s) for s in range(1, NY)]
 
     upper = section == 1
     is_upper = upper.astype(jnp.int32).reshape(1)
     is_lower = 1 - is_upper
     tensor = ti.astype(jnp.int32).reshape(1)
-    block = width // 4
+    block = width // 2
 
     def values_of(kernel, scalars, blocks, more):
         def along(*shape):
@@ -492,14 +494,14 @@
             + [pl.BlockSpec((HEAD_DIM, tokens), lambda i, own: (2 * group // HEAD_DIM, 0))] * NY
             + [pl.BlockSpec((EXTRA, tokens), lambda i, own: ((2 * group + HEAD_DIM) // EXTRA, 0))]
             * NY
-            + [pl.BlockSpec((group, tokens), lambda i, own: (i, 0))] * NY
-            + [whole_of(tokens, heads * HEAD_DIM)] * NY,
+            + [pl.BlockSpec((group, tokens), lambda i, own: (i + above // group, 0))] * NY
+            + [whole_of(above, tokens)] * NY,
             out_specs=(pl.BlockSpec((2, share_rows, columns), lambda i, own: (i, 0, 0)),) * 4,
             scratch_shapes=[pltpu.VMEM((group, columns), F32)],
         ),
     )(
         first_own, scale.reshape(1), *after(tuple(blocks), other_0), *blocks, *blocks,
-        *normed_all, *mixed_all,
+        *operands, *operands,
     )
     got = [parts[0]] + [over_xz(parts[k], k) for k in (1, 2, 3)]
     parts = pl.pallas_call(

time: 188 us -> 180 us (0.957)
  the two profiles are of different devices: /device:TPU:4 before, /device:TPU:40 now
where the time goes in v5:
time: 180 us; the launch traced here: 179 us
  waiting for transfers between devices  62 us (34%)
  starting transfers between devices  61.3 us (34%)
  Pallas kernels  40.1 us (22%)
  local copies, waits for them, and re-layouts  10.5 us (6%)
  other arithmetic  3.17 us (2%)
    ppermute x6, waiting for transfers between devices, over_xz(): return lax.ppermute(block, ('z', 'x'), route)  29.1 us
    ppermute x8, starting transfers between devices, exchanged(): return lax.ppermute(block, ('pipe', 'z', 'y', 'x'), route)  21.2 us
    ppermute x6, waiting for transfers between devices, around(): return lax.ppermute(block, 'y', [(i, (i + shift) % NY) for i in range(NY)])  15.1 us
    ppermute x1, waiting for transfers between devices, section_step(): count_down = lax.ppermute(full_count, 'pipe', [(1, 0)])  14.1 us
    ppermute x6, starting transfers between devices, over_xz(): return lax.ppermute(block, ('z', 'x'), route)  11.3 us
    ppermute x6, starting transfers between devices, around(): return lax.ppermute(block, 'y', [(i, (i + shift) % NY) for i in range(NY)])  9.47 us
    pallas_call x2, Pallas kernels, values_of(): pl.pallas_call(kernel, out_shape=out_shape, grid_spec=pltpu.PrefetchScala...  8.92 us
    pallas_call x2, Pallas kernels, forward(): pl.pallas_call(forward_kernel, out_shape=(shaped(2, seq, heads * seq),) +...  7.6 us
  transfers between devices with their start and end apart: 29, of which 12 were waited for; matrix products, arithmetic and copies ran while one was open for 5% of the time, Pallas kernels for 21%

profile of v5, /device:TPU:40, one launch (start us, length us, event | category | flops | bytes accessed | tf_op | source)
XLA Modules:
  0.0 178.8 jit_solution(13075948131908122932)
XLA Ops:
  4.7 3.8 %shard_map.120 = (bf16[2,64,448]{2,1,0:T(8,128)(2,1)}, bf16[1792,256]{1,0:T(8,128)(2,1)}, bf16[1792,256]{1,0:T(8,128)(2,1)}, bf16[1792,256]{1,0:T(8,128)(2,1)}, bf16[1792,256]{1,0:T(8,128)(2,1)}) custom-call(s32[1]{0:T(128)} %bitcast.6.y_ref, bf16[256,3584]{1,0:T(8,128)(2,1)} %bitcast.20, f32[1,3584]{1,0:T(1,128)} %refs_5_.3, bf16[3584,128]{1,0:T(8,128)(2,1)} %bitcast.27, ...), custom_call_target="tpu_custom_call" | custom-call | tf_op jit(solution)/shard_map/pallas_call | solution.py:318
  8.5 3.8 %shard_map.121 = (bf16[2,64,448]{2,1,0:T(8,128)(2,1)}, bf16[1792,256]{1,0:T(8,128)(2,1)}, bf16[1792,256]{1,0:T(8,128)(2,1)}, bf16[1792,256]{1,0:T(8,128)(2,1)}, bf16[1792,256]{1,0:T(8,128)(2,1)}) custom-call(s32[1]{0:T(128)} %bitcast.6.y_ref, bf16[256,3584]{1,0:T(8,128)(2,1)} %bitcast.21, ...), custom_call_target="tpu_custom_call", output_to_operand_aliasing={{1}: (5, {}), {2}: (6, {}), {3}: (7, {}), {4}: (8, {})} | custom-call | tf_op jit(solution)/shard_map/pallas_call | solution.py:318
  13.2 3.3 %shard_map.122 = (bf16[256,128]{1,0:T(8,128)(2,1)}, bf16[256,3584]{1,0:T(8,128)(2,1)}) custom-call(s32[1]{0:T(128)} %bitcast.active_ref.upper_ref, s32[1]{0:T(128)} %bitcast.1.tensor_ref, bf16[2,64,3584]{2,1,0:T(8,128)(2,1)} %bitcast.35, bf16[2,64,3584]{2,1,0:T(8,128)(2,1)} %copy-done.6, f32[256,1]{1,0:T(8,128)} %reshape.237.mask_ref, ...), custom_call_target="tpu_custom_call" | custom-call | tf_op jit(solution)/shard_map/pallas_call | solution.py:367
  18.1 2.6 %shard_map.123.done_ref = bf16[256,3584]{1,0:T(8,128)(2,1)} custom-call(s32[1]{0:T(128)} %bitcast.active_ref.upper_ref, bf16[256,128]{1,0:T(8,128)(2,1)} %get-tuple-element.40.refs_0_.refs_1_, bf16[256,128]{1,0:T(8,128)(2,1)} %copy-done.16, bf16[3584,128]{1,0:T(8,128)(2,1)} %bitcast.29, bf16[3584,128]{1,0:T(8,128)(2,1)} %copy-done.7, ...), custom_call_target="tpu_custom_call" | custom-call | tf_op jit(solution)/shard_map/pallas_call | solution.py:386
  23.4 3.3 %collective-permute-start.2 = (s32[8,128]{1,0:T(8,128)S(1)}, s32[8,128]{1,0:T(8,128)S(1)}, u32[]{:S(2)}, u32[]{:S(2)}) collective-permute-start(s32[8,128]{1,0:T(8,128)S(1)} %broadcast_in_dim.11), channel_id=1, source_target_pairs={{0,6},{2,4},{4,2},{6,0},{8,14},{10,12},{12,10},{14,8},{16,22},{18,... | collective-permute-start | bytes 12296 | tf_op jit(solution)/shard_map/ppermute | solution.py:287
  26.7 2.4 %collective-permute-start = (s32[8,128]{1,0:T(8,128)S(1)}, s32[8,128]{1,0:T(8,128)S(1)}, u32[]{:S(2)}, u32[]{:S(2)}) collective-permute-start(s32[8,128]{1,0:T(8,128)S(1)} %broadcast_in_dim.11), channel_id=1, source_target_pairs={{0,2},{2,0},{4,6},{6,4},{8,10},{10,8},{12,14},{14,12},{16,18},{18,... | collective-permute-start | bytes 12296 | tf_op jit(solution)/shard_map/ppermute | solution.py:287
  29.1 3.5 %collective-permute-start.1 = (s32[8,128]{1,0:T(8,128)S(1)}, s32[8,128]{1,0:T(8,128)S(1)}, u32[]{:S(2)}, u32[]{:S(2)}) collective-permute-start(s32[8,128]{1,0:T(8,128)S(1)} %broadcast_in_dim.11), channel_id=1, source_target_pairs={{0,4},{2,6},{4,0},{6,2},{8,12},{10,14},{12,8},{14,10},{16,20},{18,... | collective-permute-start | bytes 12296 | tf_op jit(solution)/shard_map/ppermute | solution.py:287
  34.6 4.0 %collective-permute-start.5 = (s32[8,128]{1,0:T(8,128)S(1)}, s32[8,128]{1,0:T(8,128)S(1)}, u32[]{:S(2)}, u32[]{:S(2)}) collective-permute-start(s32[8,128]{1,0:T(8,128)S(1)} %add_add_fusion.1), channel_id=1, source_target_pairs={{0,24},{2,26},{4,28},{6,30},{8,16},{10,18},{12,20},{14,22},{16,8},... | collective-permute-start | bytes 12296 | tf_op jit(solution)/shard_map/ppermute | solution.py:287
  38.7 3.8 %collective-permute-start.3 = (s32[8,128]{1,0:T(8,128)S(1)}, s32[8,128]{1,0:T(8,128)S(1)}, u32[]{:S(2)}, u32[]{:S(2)}) collective-permute-start(s32[8,128]{1,0:T(8,128)S(1)} %add_add_fusion.1), channel_id=1, source_target_pairs={{0,16},{2,18},{4,20},{6,22},{8,24},{10,26},{12,28},{14,30},{16,0},... | collective-permute-start | bytes 12296 | tf_op jit(solution)/shard_map/ppermute | solution.py:287
  42.5 2.9 %collective-permute-start.4 = (s32[8,128]{1,0:T(8,128)S(1)}, s32[8,128]{1,0:T(8,128)S(1)}, u32[]{:S(2)}, u32[]{:S(2)}) collective-permute-start(s32[8,128]{1,0:T(8,128)S(1)} %add_add_fusion.1), channel_id=1, source_target_pairs={{0,8},{2,10},{4,12},{6,14},{8,0},{10,2},{12,4},{14,6},{16,24},{18,... | collective-permute-start | bytes 12296 | tf_op jit(solution)/shard_map/ppermute | solution.py:287
  46.2 2.6 %collective-permute-start.20 = (bf16[1792,256]{1,0:T(8,128)(2,1)}, bf16[1792,256]{1,0:T(8,128)(2,1)}, u32[]{:S(2)}, u32[]{:S(2)}) collective-permute-start(bf16[1792,256]{1,0:T(8,128)(2,1)} %get-tuple-element.52), channel_id=1, source_target_pairs={{0,8},{4,12},{8,0},{12,4},{1,9},{5,13},{9,1},{13,5},{2,10},{6,14},... | collective-permute-start | bytes 2752520 | tf_op jit(solution)/shard_map/ppermute | solution.py:343
  48.8 5.6 %shard_map.124.refs_0_.refs_3_ = bf16[256,128]{1,0:T(8,128)(2,1)} custom-call(s32[1]{0:T(128)S(6)} %sub.35.active_ref, bf16[256,3584]{1,0:T(8,128)(2,1)} %copy-done, bf16[896,3584]{1,0:T(8,128)(2,1)} %bitcast.25, bf16[2,64,448]{2,1,0:T(8,128)(2,1)} %get-tuple-element.34.a_ref, bf16[2,64,448]{2,1,0:T(8,128)(2,1)} %get-tuple-element.39.b_ref), custom_call_target="tpu_custom_call" | custom-call | tf_op jit(solution)/shard_map/pallas_call | solution.py:367
  54.4 4.2 %shard_map.126 = (bf16[1040,256]{1,0:T(8,128)(2,1)}, bf16[1040,256]{1,0:T(8,128)(2,1)}, bf16[1040,256]{1,0:T(8,128)(2,1)}, bf16[1040,256]{1,0:T(8,128)(2,1)}) custom-call(s32[1]{0:T(128)} %bitcast.active_ref.upper_ref, s32[1]{0:T(128)} %bitcast.6.y_ref, bf16[256,3584]{1,0:T(8,128)(2,1)} %get-tuple-element.41.refs_6_.refs_0_, ...), custom_call_target="tpu_custom_call" | custom-call | tf_op jit(solution)/shard_map/pallas_call | solution.py:470
  58.6 2.0 %collective-permute-start.21 = (bf16[1792,256]{1,0:T(8,128)(2,1)}, bf16[1792,256]{1,0:T(8,128)(2,1)S(1)}, u32[]{:S(2)}, u32[]{:S(2)}) collective-permute-start(bf16[1792,256]{1,0:T(8,128)(2,1)} %get-tuple-element.53), channel_id=1, source_target_pairs={{0,12},{4,0},{8,4},{12,8},{1,13},{5,1},{9,5},{13,9},{2,14},{6,2},{... | collective-permute-start | bytes 2752520 | tf_op jit(solution)/shard_map/ppermute | solution.py:343
  65.5 14.1 %collective-permute-done.9 = s32[8,128]{1,0:T(8,128)S(1)} collective-permute-done((s32[8,128]{1,0:T(8,128)S(1)}, s32[8,128]{1,0:T(8,128)S(1)}, u32[]{:S(2)}, u32[]{:S(2)}) %collective-permute-start.9) | collective-permute-done | bytes 4128 | tf_op jit(solution)/shard_map/ppermute | solution.py:454
  79.6 4.9 %collective-permute-start.14 = (bf16[256,128]{1,0:T(8,128)(2,1)S(1)}, bf16[256,128]{1,0:T(8,128)(2,1)S(1)}, u32[]{:S(2)}, u32[]{:S(2)}) collective-permute-start(bf16[256,128]{1,0:T(8,128)(2,1)S(1)} %copy-done.8), channel_id=1, source_target_pairs={{0,1},{1,0},{2,3},{3,2},{4,5},{5,4},{6,7},{7,6},{8,9},{9,8},{10,11... | collective-permute-start | bytes 196616 | tf_op jit(solution)/shard_map/ppermute | solution.py:435
  84.6 2.7 %collective-permute-done.14.refs_1_ = bf16[256,128]{1,0:T(8,128)(2,1)S(1)} collective-permute-done((bf16[256,128]{1,0:T(8,128)(2,1)S(1)}, bf16[256,128]{1,0:T(8,128)(2,1)S(1)}, u32[]{:S(2)}, u32[]{:S(2)}) %collective-permute-start.14) | collective-permute-done | bytes 65568 | tf_op jit(solution)/shard_map/ppermute | solution.py:435
  87.9 2.4 %collective-permute-start.17 = (bf16[1040,256]{1,0:T(8,128)(2,1)}, bf16[1040,256]{1,0:T(8,128)(2,1)S(1)}, u32[]{:S(2)}, u32[]{:S(2)}) collective-permute-start(bf16[1040,256]{1,0:T(8,128)(2,1)} %get-tuple-element.44), channel_id=1, source_target_pairs={{0,8},{4,12},{8,0},{12,4},{1,9},{5,13},{9,1},{13,5},{2,10},{6,14},... | collective-permute-start | bytes 1597448 | tf_op jit(solution)/shard_map/ppermute | solution.py:343
  91.0 12.2 %collective-permute-done.17.refs_2_.refs_6_.refs_10_ = bf16[1040,256]{1,0:T(8,128)(2,1)S(1)} collective-permute-done((bf16[1040,256]{1,0:T(8,128)(2,1)}, bf16[1040,256]{1,0:T(8,128)(2,1)S(1)}, u32[]{:S(2)}, u32[]{:S(2)}) %collective-permute-start.17) | collective-permute-done | bytes 532512 | tf_op jit(solution)/shard_map/ppermute | solution.py:343
  103.2 6.1 %collective-permute-start.15 = (bf16[3584,128]{1,0:T(8,128)(2,1)S(1)}, bf16[3584,128]{1,0:T(8,128)(2,1)}, u32[]{:S(2)}, u32[]{:S(2)}) collective-permute-start(bf16[3584,128]{1,0:T(8,128)(2,1)S(1)} %bitcast.31), channel_id=1, source_target_pairs={{0,3},{3,0},{1,2},{2,1},{4,7},{7,4},{5,6},{6,5},{8,11},{11,8},{9,1... | collective-permute-start | bytes 2752520 | tf_op jit(solution)/shard_map/ppermute | solution.py:305
  110.5 2.9 %collective-permute-done.18.refs_3_.refs_7_.refs_11_ = bf16[1040,256]{1,0:T(8,128)(2,1)S(1)} collective-permute-done((bf16[1040,256]{1,0:T(8,128)(2,1)}, bf16[1040,256]{1,0:T(8,128)(2,1)S(1)}, u32[]{:S(2)}, u32[]{:S(2)}) %collective-permute-start.18) | collective-permute-done | bytes 532512 | tf_op jit(solution)/shard_map/ppermute | solution.py:343
  114.5 6.2 %shard_map.127 = (bf16[4,56,1024]{2,1,0:T(8,128)(2,1)}, bf16[4,56,1024]{2,1,0:T(8,128)(2,1)}, bf16[4,56,1024]{2,1,0:T(8,128)(2,1)}, bf16[4,56,1024]{2,1,0:T(8,128)(2,1)}) custom-call(s32[1]{0:T(128)} %bitcast.13.own_ref, f32[1]{0:T(128)} %bitcast.14.scale_ref, bf16[1040,256]{1,0:T(8,128)(2,1)} %get-tuple-element.46.refs_0_.refs_4_.refs_8_, ...), custom_call_target="tpu_custom_call" | custom-call | tf_op jit(solution)/shard_map/pallas_call | solution.py:486
  126.2 7.7 %collective-permute-done.22.b_ref = bf16[4,56,1024]{2,1,0:T(8,128)(2,1)S(1)} collective-permute-done((bf16[4,56,1024]{2,1,0:T(8,128)(2,1)}, bf16[4,56,1024]{2,1,0:T(8,128)(2,1)S(1)}, u32[]{:S(2)}, u32[]{:S(2)}) %collective-permute-start.22) | collective-permute-done | bytes 458784 | tf_op jit(solution)/shard_map/ppermute | solution.py:29
  133.9 2.2 %collective-permute-done.23.c_ref = bf16[4,56,1024]{2,1,0:T(8,128)(2,1)S(1)} collective-permute-done((bf16[4,56,1024]{2,1,0:T(8,128)(2,1)}, bf16[4,56,1024]{2,1,0:T(8,128)(2,1)S(1)}, u32[]{:S(2)}, u32[]{:S(2)}) %collective-permute-start.23) | collective-permute-done | bytes 458784 | tf_op jit(solution)/shard_map/ppermute | solution.py:29
  136.1 8.9 %collective-permute-done.24.d_ref = bf16[4,56,1024]{2,1,0:T(8,128)(2,1)S(1)} collective-permute-done((bf16[4,56,1024]{2,1,0:T(8,128)(2,1)}, bf16[4,56,1024]{2,1,0:T(8,128)(2,1)S(1)}, u32[]{:S(2)}, u32[]{:S(2)}) %collective-permute-start.24) | collective-permute-done | bytes 458784 | tf_op jit(solution)/shard_map/ppermute | solution.py:29
  145.7 2.3 %shard_map.128 = (f32[56,1024]{1,0:T(8,128)}, bf16[56,1024]{1,0:T(8,128)(2,1)}, bf16[56,1024]{1,0:T(8,128)(2,1)}, bf16[56,1024]{1,0:T(8,128)(2,1)}) custom-call(s32[1]{0:T(128)} %bitcast.12.own_ref, bf16[4,56,1024]{2,1,0:T(8,128)(2,1)} %get-tuple-element.54.a_ref, bf16[4,56,1024]{2,1,0:T(8,128)(2,1)} %copy-done.9, bf16[4,56,1024]{2,1,0:T(8,128)(2,1)} %copy-done.10, ...), custom_call_target="tpu_custom_call" | custom-call | tf_op jit(solution)/shard_map/pallas_call | solution.py:507
  148.1 3.2 %collective-permute-start.25 = (bf16[56,1024]{1,0:T(8,128)(2,1)}, bf16[56,1024]{1,0:T(8,128)(2,1)S(1)}, u32[]{:S(2)}, u32[]{:S(2)}) collective-permute-start(bf16[56,1024]{1,0:T(8,128)(2,1)} %get-tuple-element.59), channel_id=1, source_target_pairs={{0,32},{2,34},{16,48},{18,50},{32,0},{34,2},{48,16},{50,18},{64,96... | collective-permute-start | bytes 344072 | tf_op jit(solution)/shard_map/ppermute | solution.py:29
  151.3 4.5 %collective-permute-start.26 = (bf16[56,1024]{1,0:T(8,128)(2,1)}, bf16[56,1024]{1,0:T(8,128)(2,1)S(1)}, u32[]{:S(2)}, u32[]{:S(2)}) collective-permute-start(bf16[56,1024]{1,0:T(8,128)(2,1)} %get-tuple-element.60), channel_id=1, source_target_pairs={{0,64},{2,66},{16,80},{18,82},{32,96},{34,98},{48,112},{50,114},{6... | collective-permute-start | bytes 344072 | tf_op jit(solution)/shard_map/ppermute | solution.py:29
  155.8 5.0 %collective-permute-done.25.b_ref = bf16[56,1024]{1,0:T(8,128)(2,1)S(1)} collective-permute-done((bf16[56,1024]{1,0:T(8,128)(2,1)}, bf16[56,1024]{1,0:T(8,128)(2,1)S(1)}, u32[]{:S(2)}, u32[]{:S(2)}) %collective-permute-start.25) | collective-permute-done | bytes 114720 | tf_op jit(solution)/shard_map/ppermute | solution.py:29
  161.9 4.2 %collective-permute-done.27.d_ref = bf16[56,1024]{1,0:T(8,128)(2,1)S(1)} collective-permute-done((bf16[56,1024]{1,0:T(8,128)(2,1)}, bf16[56,1024]{1,0:T(8,128)(2,1)S(1)}, u32[]{:S(2)}, u32[]{:S(2)}) %collective-permute-start.27) | collective-permute-done | bytes 114720 | tf_op jit(solution)/shard_map/ppermute | solution.py:29
  168.3 2.4 %collective-permute-start.28 = (f32[1,56]{1,0:T(1,128)}, f32[1,56]{1,0:T(1,128)S(1)}, u32[]{:S(2)}, u32[]{:S(2)}) collective-permute-start(f32[1,56]{1,0:T(1,128)} %get-tuple-element.63), channel_id=1, source_target_pairs={{0,1},{1,0},{2,3},{3,2},{4,5},{5,4},{6,7},{7,6},{8,9},{9,8},{10,11... | collective-permute-start | bytes 680 | tf_op jit(solution)/shard_map/ppermute | solution.py:19
  171.5 4.9 %shard_map.125 = bf16[1,128,3584]{2,1,0:T(8,128)(2,1)} custom-call(s32[1]{0:T(128)S(6)} %sub.35.active_ref, s32[1]{0:T(128)} %bitcast.1.tensor_ref, f32[256,1]{1,0:T(8,128)} %copy.19.weight_ref, bf16[256,3584]{1,0:T(8,128)(2,1)} %shard_map.123.done_ref, bf16[256,128]{1,0:T(8,128)(2,1)} %shard_map.124.refs_0_.refs_3_, bf16[256,128]{1,0:T(8,128)(2,1)} %copy-done.15, ...), custom_call_target="tpu_custom_call" | custom-call | tf_op jit(solution)/shard_map/pallas_call | solution.py:412
  (103 shorter events, 32.3 us)
Async XLA Ops:
  0.6 11.6 %collective-permute-start.10 = (bf16[2,64,3584]{2,1,0:T(8,128)(2,1)}, bf16[2,64,3584]{2,1,0:T(8,128)(2,1)S(1)}, u32[]{:S(2)}, u32[]{:S(2)}) collective-permute-start(bf16[2,64,3584]{2,1,0:T(8,128)(2,1)} %bitcast.34), channel_id=1, source_target_pairs={{128,129},{129,128},{130,131},{131,130},{132,133},{133,132},{134,1... | collective-permute-start | bytes 2752520 | tf_op jit(solution)/shard_map/ppermute | solution.py:270
  1.4 15.8 %collective-permute-start.12 = (bf16[3584,128]{1,0:T(8,128)(2,1)}, bf16[3584,128]{1,0:T(8,128)(2,1)S(1)}, u32[]{:S(2)}, u32[]{:S(2)}) collective-permute-start(bf16[3584,128]{1,0:T(8,128)(2,1)} %bitcast.26), channel_id=1, source_target_pairs={{128,131},{131,128},{129,130},{130,129},{132,135},{135,132},{133,1... | collective-permute-start | bytes 2752520 | tf_op jit(solution)/shard_map/ppermute | solution.py:305
  16.5 0.7 collective-permute-start.11
  20.7 25.5 %collective-permute-start.13 = (bf16[256,3584]{1,0:T(8,128)(2,1)}, bf16[256,3584]{1,0:T(8,128)(2,1)S(1)}, u32[]{:S(2)}, u32[]{:S(2)}) collective-permute-start(bf16[256,3584]{1,0:T(8,128)(2,1)} %shard_map.123.done_ref), channel_id=1, source_target_pairs={{128,0},{129,1},{130,2},{131,3},{132,4},{133,5},{134,6},{135,7},{1... | collective-permute-start | bytes 5505032 | tf_op jit(solution)/shard_map/ppermute | solution.py:449
  23.4 11.2 %collective-permute-start.2 = (s32[8,128]{1,0:T(8,128)S(1)}, s32[8,128]{1,0:T(8,128)S(1)}, u32[]{:S(2)}, u32[]{:S(2)}) collective-permute-start(s32[8,128]{1,0:T(8,128)S(1)} %broadcast_in_dim.11), channel_id=1, source_target_pairs={{0,6},{2,4},{4,2},{6,0},{8,14},{10,12},{12,10},{14,8},{16,22},{18,... | collective-permute-start | bytes 12296 | tf_op jit(solution)/shard_map/ppermute | solution.py:287
  26.7 7.8 %collective-permute-start = (s32[8,128]{1,0:T(8,128)S(1)}, s32[8,128]{1,0:T(8,128)S(1)}, u32[]{:S(2)}, u32[]{:S(2)}) collective-permute-start(s32[8,128]{1,0:T(8,128)S(1)} %broadcast_in_dim.11), channel_id=1, source_target_pairs={{0,2},{2,0},{4,6},{6,4},{8,10},{10,8},{12,14},{14,12},{16,18},{18,... | collective-permute-start | bytes 12296 | tf_op jit(solution)/shard_map/ppermute | solution.py:287
  29.1 5.5 %collective-permute-start.1 = (s32[8,128]{1,0:T(8,128)S(1)}, s32[8,128]{1,0:T(8,128)S(1)}, u32[]{:S(2)}, u32[]{:S(2)}) collective-permute-start(s32[8,128]{1,0:T(8,128)S(1)} %broadcast_in_dim.11), channel_id=1, source_target_pairs={{0,4},{2,6},{4,0},{6,2},{8,12},{10,14},{12,8},{14,10},{16,20},{18,... | collective-permute-start | bytes 12296 | tf_op jit(solution)/shard_map/ppermute | solution.py:287
  32.6 80.8 %collective-permute-start.19 = (bf16[1792,256]{1,0:T(8,128)(2,1)}, bf16[1792,256]{1,0:T(8,128)(2,1)}, u32[]{:S(2)}, u32[]{:S(2)}) collective-permute-start(bf16[1792,256]{1,0:T(8,128)(2,1)} %get-tuple-element.51), channel_id=1, source_target_pairs={{0,4},{4,8},{8,12},{12,0},{1,5},{5,9},{9,13},{13,1},{2,6},{6,10},{... | collective-permute-start | bytes 2752520 | tf_op jit(solution)/shard_map/ppermute | solution.py:343
  34.6 23.9 %collective-permute-start.5 = (s32[8,128]{1,0:T(8,128)S(1)}, s32[8,128]{1,0:T(8,128)S(1)}, u32[]{:S(2)}, u32[]{:S(2)}) collective-permute-start(s32[8,128]{1,0:T(8,128)S(1)} %add_add_fusion.1), channel_id=1, source_target_pairs={{0,24},{2,26},{4,28},{6,30},{8,16},{10,18},{12,20},{14,22},{16,8},... | collective-permute-start | bytes 12296 | tf_op jit(solution)/shard_map/ppermute | solution.py:287
  38.7 21.9 %collective-permute-start.3 = (s32[8,128]{1,0:T(8,128)S(1)}, s32[8,128]{1,0:T(8,128)S(1)}, u32[]{:S(2)}, u32[]{:S(2)}) collective-permute-start(s32[8,128]{1,0:T(8,128)S(1)} %add_add_fusion.1), channel_id=1, source_target_pairs={{0,16},{2,18},{4,20},{6,22},{8,24},{10,26},{12,28},{14,30},{16,0},... | collective-permute-start | bytes 12296 | tf_op jit(solution)/shard_map/ppermute | solution.py:287
  42.5 18.2 %collective-permute-start.4 = (s32[8,128]{1,0:T(8,128)S(1)}, s32[8,128]{1,0:T(8,128)S(1)}, u32[]{:S(2)}, u32[]{:S(2)}) collective-permute-start(s32[8,128]{1,0:T(8,128)S(1)} %add_add_fusion.1), channel_id=1, source_target_pairs={{0,8},{2,10},{4,12},{6,14},{8,0},{10,2},{12,4},{14,6},{16,24},{18,... | collective-permute-start | bytes 12296 | tf_op jit(solution)/shard_map/ppermute | solution.py:287
  46.2 67.3 %collective-permute-start.20 = (bf16[1792,256]{1,0:T(8,128)(2,1)}, bf16[1792,256]{1,0:T(8,128)(2,1)}, u32[]{:S(2)}, u32[]{:S(2)}) collective-permute-start(bf16[1792,256]{1,0:T(8,128)(2,1)} %get-tuple-element.52), channel_id=1, source_target_pairs={{0,8},{4,12},{8,0},{12,4},{1,9},{5,13},{9,1},{13,5},{2,10},{6,14},... | collective-permute-start | bytes 2752520 | tf_op jit(solution)/shard_map/ppermute | solution.py:343
  54.4 25.3 %copy-start.8 = (bf16[256,128]{1,0:T(8,128)(2,1)S(1)}, bf16[256,128]{1,0:T(8,128)(2,1)}, u32[]{:S(2)}) copy-start(bf16[256,128]{1,0:T(8,128)(2,1)} %shard_map.124.refs_0_.refs_3_) | copy-start | bytes 196612
  54.4 48.8 %copy-start.1 = (bf16[1,3584,128]{2,1,0:T(8,128)(2,1)S(1)}, bf16[1,3584,128]{2,1,0:T(8,128)(2,1)}, u32[]{:S(2)}) copy-start(bf16[1,3584,128]{2,1,0:T(8,128)(2,1)} %param.12) | copy-start | bytes 2752516
  58.6 54.8 %collective-permute-start.21 = (bf16[1792,256]{1,0:T(8,128)(2,1)}, bf16[1792,256]{1,0:T(8,128)(2,1)S(1)}, u32[]{:S(2)}, u32[]{:S(2)}) collective-permute-start(bf16[1792,256]{1,0:T(8,128)(2,1)} %get-tuple-element.53), channel_id=1, source_target_pairs={{0,12},{4,0},{8,4},{12,8},{1,13},{5,1},{9,5},{13,9},{2,14},{6,2},{... | collective-permute-start | bytes 2752520 | tf_op jit(solution)/shard_map/ppermute | solution.py:343
  60.6 29.8 %collective-permute-start.16 = (bf16[1040,256]{1,0:T(8,128)(2,1)}, bf16[1040,256]{1,0:T(8,128)(2,1)S(1)}, u32[]{:S(2)}, u32[]{:S(2)}) collective-permute-start(bf16[1040,256]{1,0:T(8,128)(2,1)} %get-tuple-element.43), channel_id=1, source_target_pairs={{0,4},{4,8},{8,12},{12,0},{1,5},{5,9},{9,13},{13,1},{2,6},{6,10},{... | collective-permute-start | bytes 1597448 | tf_op jit(solution)/shard_map/ppermute | solution.py:343
  60.7 2.1 %collective-permute-start.6 = (s32[8,128]{1,0:T(8,128)S(1)}, s32[8,128]{1,0:T(8,128)S(1)}, u32[]{:S(2)}, u32[]{:S(2)}) collective-permute-start(s32[8,128]{1,0:T(8,128)S(1)} %add_add_fusion), channel_id=1, source_target_pairs={{0,128},{1,129},{2,130},{3,131},{4,132},{5,133},{6,134},{7,135},{8... | collective-permute-start | bytes 12296 | tf_op jit(solution)/shard_map/ppermute | solution.py:451
  62.8 0.7 collective-permute-start.7
  63.5 0.7 collective-permute-start.8
  64.2 15.4 %collective-permute-start.9 = (s32[8,128]{1,0:T(8,128)S(1)}, s32[8,128]{1,0:T(8,128)S(1)}, u32[]{:S(2)}, u32[]{:S(2)}) collective-permute-start(s32[8,128]{1,0:T(8,128)S(1)} %add.82), channel_id=1, source_target_pairs={{128,0},{129,1},{130,2},{131,3},{132,4},{133,5},{134,6},{135,7},{1... | collective-permute-start | bytes 12296 | tf_op jit(solution)/shard_map/ppermute | solution.py:454
  79.6 7.7 %collective-permute-start.14 = (bf16[256,128]{1,0:T(8,128)(2,1)S(1)}, bf16[256,128]{1,0:T(8,128)(2,1)S(1)}, u32[]{:S(2)}, u32[]{:S(2)}) collective-permute-start(bf16[256,128]{1,0:T(8,128)(2,1)S(1)} %copy-done.8), channel_id=1, source_target_pairs={{0,1},{1,0},{2,3},{3,2},{4,5},{5,4},{6,7},{7,6},{8,9},{9,8},{10,11... | collective-permute-start | bytes 196616 | tf_op jit(solution)/shard_map/ppermute | solution.py:435
  87.9 15.3 %collective-permute-start.17 = (bf16[1040,256]{1,0:T(8,128)(2,1)}, bf16[1040,256]{1,0:T(8,128)(2,1)S(1)}, u32[]{:S(2)}, u32[]{:S(2)}) collective-permute-start(bf16[1040,256]{1,0:T(8,128)(2,1)} %get-tuple-element.44), channel_id=1, source_target_pairs={{0,8},{4,12},{8,0},{12,4},{1,9},{5,13},{9,1},{13,5},{2,10},{6,14},... | collective-permute-start | bytes 1597448 | tf_op jit(solution)/shard_map/ppermute | solution.py:343
  90.3 23.1 %collective-permute-start.18 = (bf16[1040,256]{1,0:T(8,128)(2,1)}, bf16[1040,256]{1,0:T(8,128)(2,1)S(1)}, u32[]{:S(2)}, u32[]{:S(2)}) collective-permute-start(bf16[1040,256]{1,0:T(8,128)(2,1)} %get-tuple-element.45), channel_id=1, source_target_pairs={{0,12},{4,0},{8,4},{12,8},{1,13},{5,1},{9,5},{13,9},{2,14},{6,2},{... | collective-permute-start | bytes 1597448 | tf_op jit(solution)/shard_map/ppermute | solution.py:343
  103.2 68.3 %collective-permute-start.15 = (bf16[3584,128]{1,0:T(8,128)(2,1)S(1)}, bf16[3584,128]{1,0:T(8,128)(2,1)}, u32[]{:S(2)}, u32[]{:S(2)}) collective-permute-start(bf16[3584,128]{1,0:T(8,128)(2,1)S(1)} %bitcast.31), channel_id=1, source_target_pairs={{0,3},{3,0},{1,2},{2,1},{4,7},{7,4},{5,6},{6,5},{8,11},{11,8},{9,1... | collective-permute-start | bytes 2752520 | tf_op jit(solution)/shard_map/ppermute | solution.py:305
  120.7 35.1 %copy-start.17 = (f32[1,256]{1,0:T(1,128)S(1)}, f32[1,256]{1,0:T(1,128)}, u32[]{:S(2)}) copy-start(f32[1,256]{1,0:T(1,128)} %reshape.226.refs_4_) | copy-start | bytes 3076
  120.7 13.2 %collective-permute-start.22 = (bf16[4,56,1024]{2,1,0:T(8,128)(2,1)}, bf16[4,56,1024]{2,1,0:T(8,128)(2,1)S(1)}, u32[]{:S(2)}, u32[]{:S(2)}) collective-permute-start(bf16[4,56,1024]{2,1,0:T(8,128)(2,1)} %get-tuple-element.55), channel_id=1, source_target_pairs={{0,2},{2,0},{16,18},{18,16},{32,34},{34,32},{48,50},{50,48},{64,66... | collective-permute-start | bytes 1376264 | tf_op jit(solution)/shard_map/ppermute | solution.py:29
  122.5 13.6 %collective-permute-start.23 = (bf16[4,56,1024]{2,1,0:T(8,128)(2,1)}, bf16[4,56,1024]{2,1,0:T(8,128)(2,1)S(1)}, u32[]{:S(2)}, u32[]{:S(2)}) collective-permute-start(bf16[4,56,1024]{2,1,0:T(8,128)(2,1)} %get-tuple-element.56), channel_id=1, source_target_pairs={{0,16},{2,18},{16,0},{18,2},{32,48},{34,50},{48,32},{50,34},{64,80... | collective-permute-start | bytes 1376264 | tf_op jit(solution)/shard_map/ppermute | solution.py:29
  122.8 22.1 %collective-permute-start.24 = (bf16[4,56,1024]{2,1,0:T(8,128)(2,1)}, bf16[4,56,1024]{2,1,0:T(8,128)(2,1)S(1)}, u32[]{:S(2)}, u32[]{:S(2)}) collective-permute-start(bf16[4,56,1024]{2,1,0:T(8,128)(2,1)} %get-tuple-element.57), channel_id=1, source_target_pairs={{0,18},{2,16},{16,2},{18,0},{32,50},{34,48},{48,34},{50,32},{64,82... | collective-permute-start | bytes 1376264 | tf_op jit(solution)/shard_map/ppermute | solution.py:29
  148.1 12.7 %collective-permute-start.25 = (bf16[56,1024]{1,0:T(8,128)(2,1)}, bf16[56,1024]{1,0:T(8,128)(2,1)S(1)}, u32[]{:S(2)}, u32[]{:S(2)}) collective-permute-start(bf16[56,1024]{1,0:T(8,128)(2,1)} %get-tuple-element.59), channel_id=1, source_target_pairs={{0,32},{2,34},{16,48},{18,50},{32,0},{34,2},{48,16},{50,18},{64,96... | collective-permute-start | bytes 344072 | tf_op jit(solution)/shard_map/ppermute | solution.py:29
  151.3 10.6 %collective-permute-start.26 = (bf16[56,1024]{1,0:T(8,128)(2,1)}, bf16[56,1024]{1,0:T(8,128)(2,1)S(1)}, u32[]{:S(2)}, u32[]{:S(2)}) collective-permute-start(bf16[56,1024]{1,0:T(8,128)(2,1)} %get-tuple-element.60), channel_id=1, source_target_pairs={{0,64},{2,66},{16,80},{18,82},{32,96},{34,98},{48,112},{50,114},{6... | collective-permute-start | bytes 344072 | tf_op jit(solution)/shard_map/ppermute | solution.py:29
  155.8 10.3 %collective-permute-start.27 = (bf16[56,1024]{1,0:T(8,128)(2,1)}, bf16[56,1024]{1,0:T(8,128)(2,1)S(1)}, u32[]{:S(2)}, u32[]{:S(2)}) collective-permute-start(bf16[56,1024]{1,0:T(8,128)(2,1)} %get-tuple-element.61), channel_id=1, source_target_pairs={{0,96},{2,98},{16,112},{18,114},{32,64},{34,66},{48,80},{50,82},{6... | collective-permute-start | bytes 344072 | tf_op jit(solution)/shard_map/ppermute | solution.py:29
  168.3 10.0 %collective-permute-start.28 = (f32[1,56]{1,0:T(1,128)}, f32[1,56]{1,0:T(1,128)S(1)}, u32[]{:S(2)}, u32[]{:S(2)}) collective-permute-start(f32[1,56]{1,0:T(1,128)} %get-tuple-element.63), channel_id=1, source_target_pairs={{0,1},{1,0},{2,3},{3,2},{4,5},{5,4},{6,7},{7,6},{8,9},{9,8},{10,11... | collective-permute-start | bytes 680 | tf_op jit(solution)/shard_map/ppermute | solution.py:19
  (18 other events, 111.4 us)

commit v6 on v5

--- a/solution.py
+++ b/solution.py
@@ -52,24 +52,42 @@
 
 
 def forward_kernel(y_ref, x_ref, gain_ref, wv_ref, pattern_ref, *refs):
-    turned_ref, operand_refs, normed_t_ref, mixed_ref = refs[-7], refs[-6:-2], refs[-2], refs[-1]
+    turned_ref, operand_refs, normed_t_ref = refs[-6], refs[-5:-1], refs[-1]
     heads, seq = pattern_ref.shape[1:3]
     x = x_ref[...].astype(F32)
     normed = (x * rms_of(x) * gain_ref[...]).astype(BF16)
     normed_t_ref[...] = normed.T
-    values = dot(normed, wv_ref[...], ((1,), (0,))).astype(BF16)
+    deal(operand_refs, normed_t_ref, y_ref[0])
+    values_t = dot(normed, wv_ref[...], ((1,), (0,))).astype(BF16).T
+    turned = [pattern_ref[part].reshape(heads * seq, seq).T for part in range(2)]
     for part in range(2):
-        at = slice(part * seq, (part + 1) * seq)
-        pattern = pattern_ref[part].reshape(heads * seq, seq)
-        turned_ref[part] = pattern.T
-        mixed = dot(pattern, values[at], ((1,), (0,))).astype(BF16)
-        for h in range(heads):
-            mixed_ref[at, h * HEAD_DIM : (h + 1) * HEAD_DIM] = mixed[h * seq : (h + 1) * seq]
-    mixed_t = mixed_ref[...].T
-    above = mixed_t.shape[0]
+        turned_ref[part] = turned[part]
+    pattern = jnp.concatenate(turned, axis=0).T
+    end = operand_refs[0].shape[0]
     for operand_ref in operand_refs:
-        operand_ref[:above] = mixed_t
-    deal([r.at[above:] for r in operand_refs], normed_t_ref, y_ref[0])
+        operand_ref[end - HEAD_DIM - heads * seq : end - HEAD_DIM] = pattern
+        operand_ref[end - HEAD_DIM :] = values_t
+
+
+def mixed_kernel(*refs):
+    count = len(refs) // 2
+    for operand_ref, mixed_ref in zip(refs[:count], refs[count:]):
+        end = operand_ref.shape[0]
+        heads = mixed_ref.shape[1] // HEAD_DIM
+        seq = mixed_ref.shape[0] // 4
+        for p in range(2):
+            lanes = slice(p * 2 * seq, (p + 1) * 2 * seq)
+            pattern = operand_ref[end - HEAD_DIM - heads * seq : end - HEAD_DIM, lanes].astype(F32)
+            values_t = operand_ref[end - HEAD_DIM :, lanes]
+            lane = lax.broadcasted_iota(jnp.int32, pattern.shape, 1)
+            for part in range(2):
+                mine = jnp.where(lane // seq == part, pattern, 0.0).astype(BF16)
+                mixed = dot(mine, values_t, ((1,), (1,))).astype(BF16)
+                row = (2 * p + part) * seq
+                for h in range(heads):
+                    mixed_ref[row : row + seq, h * HEAD_DIM : (h + 1) * HEAD_DIM] = mixed[
+                        h * seq : (h + 1) * seq
+                    ]
 
 
 def add_values(step, dy, wo_ref, turned_refs, values_ref, mixed_ref):
@@ -200,7 +218,7 @@
         weight = rows[0:1] + rows[1:2] - chosen
         dy = (weight * dy_ref[...].astype(F32)).astype(BF16)
         values_t = (weight * values_ref[...].astype(F32)).astype(BF16)
-        output = output + dot(dy, mixed_ref[...], ((1,), (1,)))
+        output = output + dot(dy, mixed_ref[...], ((1,), (0,)))
         value = value + dot(normed_ref[...], values_t, ((1,), (1,)))
     total_ref[:, :HEAD_DIM] = value
     total_ref[:, HEAD_DIM:] = output
@@ -312,13 +330,13 @@
 
     y_index = yi.astype(jnp.int32).reshape(1)
 
-    above = heads * HEAD_DIM
+    operand_rows = width // NY + heads * seq + HEAD_DIM
 
     def forward(p, *earlier):
         return pl.pallas_call(
             forward_kernel,
             out_shape=(shaped(2, seq, heads * seq),)
-            + (shaped(above + width // NY, tokens),) * NY,
+            + (shaped(operand_rows, tokens),) * NY,
             grid_spec=pltpu.PrefetchScalarGridSpec(
                 num_scalar_prefetch=1,
                 grid=(1,),
@@ -330,8 +348,8 @@
                 ]
                 + [ANY] * len(earlier),
                 out_specs=(pl.BlockSpec((2, seq, heads * seq), lambda i, y: (0, 0, 0)),)
-                + (pl.BlockSpec((above + width // NY, half), lambda i, y: (0, p)),) * NY,
-                scratch_shapes=[pltpu.VMEM((width, half), BF16), pltpu.VMEM((half, above), BF16)],
+                + (pl.BlockSpec((operand_rows, half), lambda i, y: (0, p)),) * NY,
+                scratch_shapes=[pltpu.VMEM((width, half), BF16)],
             ),
             input_output_aliases={5 + n: 1 + n for n in range(len(earlier))},
         )(y_index, x, norm_gain, wv, patterns, *earlier)
@@ -483,6 +501,12 @@
     first_own = ((zi % 2) * NX + xi).astype(jnp.int32).reshape(1)
     group = width // NY // 2
 
+    mixed_all = pl.pallas_call(
+        mixed_kernel,
+        out_shape=(shaped(tokens, heads * HEAD_DIM),) * NY,
+        in_specs=[VMEM] * NY,
+        out_specs=(VMEM,) * NY,
+    )(*operands)
     parts = pl.pallas_call(
         products_kernel,
         out_shape=(shaped(4, share_rows, columns),) * 4,
@@ -494,14 +518,14 @@
             + [pl.BlockSpec((HEAD_DIM, tokens), lambda i, own: (2 * group // HEAD_DIM, 0))] * NY
             + [pl.BlockSpec((EXTRA, tokens), lambda i, own: ((2 * group + HEAD_DIM) // EXTRA, 0))]
             * NY
-            + [pl.BlockSpec((group, tokens), lambda i, own: (i + above // group, 0))] * NY
-            + [whole_of(above, tokens)] * NY,
+            + [pl.BlockSpec((group, tokens), lambda i, own: (i, 0))] * NY
+            + [whole_of(tokens, heads * HEAD_DIM)] * NY,
             out_specs=(pl.BlockSpec((2, share_rows, columns), lambda i, own: (i, 0, 0)),) * 4,
             scratch_shapes=[pltpu.VMEM((group, columns), F32)],
         ),
     )(
         first_own, scale.reshape(1), *after(tuple(blocks), other_0), *blocks, *blocks,
-        *operands, *operands,
+        *operands, *mixed_all,
     )
     got = [parts[0]] + [over_xz(parts[k], k) for k in (1, 2, 3)]
     parts = pl.pallas_call(

time: 180 us -> 171 us (0.950)
  the two profiles are of different devices: /device:TPU:40 before, /device:TPU:4 now
where the time goes in v6:
time: 171 us; the launch traced here: 169 us
  starting transfers between devices  58.5 us (34%)
  waiting for transfers between devices  51.7 us (30%)
  Pallas kernels  42.7 us (25%)
  local copies, waits for them, and re-layouts  11.1 us (6%)
  other arithmetic  3.16 us (2%)
    ppermute x6, waiting for transfers between devices, over_xz(): return lax.ppermute(block, ('z', 'x'), route)  26.3 us
    ppermute x8, starting transfers between devices, exchanged(): return lax.ppermute(block, ('pipe', 'z', 'y', 'x'), route)  21.2 us
    ppermute x6, waiting for transfers between devices, around(): return lax.ppermute(block, 'y', [(i, (i + shift) % NY) for i in range(NY)])  18.8 us
    ppermute x6, starting transfers between devices, over_xz(): return lax.ppermute(block, ('z', 'x'), route)  12 us
    pallas_call x2, Pallas kernels, values_of(): pl.pallas_call(kernel, out_shape=out_shape, grid_spec=pltpu.PrefetchScala...  8.87 us
    ppermute x6, starting transfers between devices, around(): return lax.ppermute(block, 'y', [(i, (i + shift) % NY) for i in range(NY)])  8.74 us
    pallas_call x2, Pallas kernels, forward(): pl.pallas_call(forward_kernel, out_shape=(shaped(2, seq, heads * seq),) +...  7 us
    pallas_call x1, Pallas kernels, section_step(): pl.pallas_call(products_kernel, out_shape=(shaped(4, share_rows, columns)...  6.15 us
  transfers between devices with their start and end apart: 29, of which 11 were waited for; matrix products, arithmetic and copies ran while one was open for 5% of the time, Pallas kernels for 24%

profile of v6, /device:TPU:4, one launch (start us, length us, event | category | flops | bytes accessed | tf_op | source)
XLA Modules:
  0.0 168.9 jit_solution(905453428875890252)
XLA Ops:
  4.7 3.5 %shard_map.120 = (bf16[2,64,448]{2,1,0:T(8,128)(2,1)}, bf16[1472,256]{1,0:T(8,128)(2,1)}, bf16[1472,256]{1,0:T(8,128)(2,1)}, bf16[1472,256]{1,0:T(8,128)(2,1)}, bf16[1472,256]{1,0:T(8,128)(2,1)}) custom-call(s32[1]{0:T(128)} %bitcast.6.y_ref, bf16[256,3584]{1,0:T(8,128)(2,1)} %bitcast.20, f32[1,3584]{1,0:T(1,128)} %refs_5_.3, bf16[3584,128]{1,0:T(8,128)(2,1)} %bitcast.27, ...), custom_call_target="tpu_custom_call" | custom-call | tf_op jit(solution)/shard_map/pallas_call | solution.py:336
  8.2 3.5 %shard_map.121 = (bf16[2,64,448]{2,1,0:T(8,128)(2,1)}, bf16[1472,256]{1,0:T(8,128)(2,1)}, bf16[1472,256]{1,0:T(8,128)(2,1)}, bf16[1472,256]{1,0:T(8,128)(2,1)}, bf16[1472,256]{1,0:T(8,128)(2,1)}) custom-call(s32[1]{0:T(128)} %bitcast.6.y_ref, bf16[256,3584]{1,0:T(8,128)(2,1)} %bitcast.21, ...), custom_call_target="tpu_custom_call", output_to_operand_aliasing={{1}: (5, {}), {2}: (6, {}), {3}: (7, {}), {4}: (8, {})} | custom-call | tf_op jit(solution)/shard_map/pallas_call | solution.py:336
  12.6 3.3 %shard_map.122 = (bf16[256,128]{1,0:T(8,128)(2,1)}, bf16[256,3584]{1,0:T(8,128)(2,1)}) custom-call(s32[1]{0:T(128)} %bitcast.active_ref.upper_ref, s32[1]{0:T(128)} %bitcast.1.tensor_ref, bf16[2,64,3584]{2,1,0:T(8,128)(2,1)} %bitcast.35, bf16[2,64,3584]{2,1,0:T(8,128)(2,1)} %copy-done.6, f32[256,1]{1,0:T(8,128)} %reshape.237.mask_ref, ...), custom_call_target="tpu_custom_call" | custom-call | tf_op jit(solution)/shard_map/pallas_call | solution.py:385
  17.5 2.6 %shard_map.123.done_ref = bf16[256,3584]{1,0:T(8,128)(2,1)} custom-call(s32[1]{0:T(128)} %bitcast.active_ref.upper_ref, bf16[256,128]{1,0:T(8,128)(2,1)} %get-tuple-element.44.refs_0_.refs_1_, bf16[256,128]{1,0:T(8,128)(2,1)} %copy-done.16, bf16[3584,128]{1,0:T(8,128)(2,1)} %bitcast.29, bf16[3584,128]{1,0:T(8,128)(2,1)} %copy-done.7, ...), custom_call_target="tpu_custom_call" | custom-call | tf_op jit(solution)/shard_map/pallas_call | solution.py:404
  22.7 4.1 %collective-permute-start.2 = (s32[8,128]{1,0:T(8,128)S(1)}, s32[8,128]{1,0:T(8,128)S(1)}, u32[]{:S(2)}, u32[]{:S(2)}) collective-permute-start(s32[8,128]{1,0:T(8,128)S(1)} %broadcast_in_dim.11), channel_id=1, source_target_pairs={{0,6},{2,4},{4,2},{6,0},{8,14},{10,12},{12,10},{14,8},{16,22},{18,... | collective-permute-start | bytes 12296 | tf_op jit(solution)/shard_map/ppermute | solution.py:305
  26.8 2.7 %collective-permute-start = (s32[8,128]{1,0:T(8,128)S(1)}, s32[8,128]{1,0:T(8,128)S(1)}, u32[]{:S(2)}, u32[]{:S(2)}) collective-permute-start(s32[8,128]{1,0:T(8,128)S(1)} %broadcast_in_dim.11), channel_id=1, source_target_pairs={{0,2},{2,0},{4,6},{6,4},{8,10},{10,8},{12,14},{14,12},{16,18},{18,... | collective-permute-start | bytes 12296 | tf_op jit(solution)/shard_map/ppermute | solution.py:305
  29.6 2.4 %collective-permute-start.1 = (s32[8,128]{1,0:T(8,128)S(1)}, s32[8,128]{1,0:T(8,128)S(1)}, u32[]{:S(2)}, u32[]{:S(2)}) collective-permute-start(s32[8,128]{1,0:T(8,128)S(1)} %broadcast_in_dim.11), channel_id=1, source_target_pairs={{0,4},{2,6},{4,0},{6,2},{8,12},{10,14},{12,8},{14,10},{16,20},{18,... | collective-permute-start | bytes 12296 | tf_op jit(solution)/shard_map/ppermute | solution.py:305
  32.3 2.7 %collective-permute-done.1 = s32[8,128]{1,0:T(8,128)S(1)} collective-permute-done((s32[8,128]{1,0:T(8,128)S(1)}, s32[8,128]{1,0:T(8,128)S(1)}, u32[]{:S(2)}, u32[]{:S(2)}) %collective-permute-start.1) | collective-permute-done | bytes 4128 | tf_op jit(solution)/shard_map/ppermute | solution.py:305
  35.1 6.1 %collective-permute-start.5 = (s32[8,128]{1,0:T(8,128)S(1)}, s32[8,128]{1,0:T(8,128)S(1)}, u32[]{:S(2)}, u32[]{:S(2)}) collective-permute-start(s32[8,128]{1,0:T(8,128)S(1)} %add_add_fusion.1), channel_id=1, source_target_pairs={{0,24},{2,26},{4,28},{6,30},{8,16},{10,18},{12,20},{14,22},{16,8},... | collective-permute-start | bytes 12296 | tf_op jit(solution)/shard_map/ppermute | solution.py:305
  41.2 2.0 %collective-permute-start.3 = (s32[8,128]{1,0:T(8,128)S(1)}, s32[8,128]{1,0:T(8,128)S(1)}, u32[]{:S(2)}, u32[]{:S(2)}) collective-permute-start(s32[8,128]{1,0:T(8,128)S(1)} %add_add_fusion.1), channel_id=1, source_target_pairs={{0,16},{2,18},{4,20},{6,22},{8,24},{10,26},{12,28},{14,30},{16,0},... | collective-permute-start | bytes 12296 | tf_op jit(solution)/shard_map/ppermute | solution.py:305
  43.3 2.5 %collective-permute-start.4 = (s32[8,128]{1,0:T(8,128)S(1)}, s32[8,128]{1,0:T(8,128)S(1)}, u32[]{:S(2)}, u32[]{:S(2)}) collective-permute-start(s32[8,128]{1,0:T(8,128)S(1)} %add_add_fusion.1), channel_id=1, source_target_pairs={{0,8},{2,10},{4,12},{6,14},{8,0},{10,2},{12,4},{14,6},{16,24},{18,... | collective-permute-start | bytes 12296 | tf_op jit(solution)/shard_map/ppermute | solution.py:305
  46.3 3.2 %collective-permute-start.20 = (bf16[1472,256]{1,0:T(8,128)(2,1)}, bf16[1472,256]{1,0:T(8,128)(2,1)}, u32[]{:S(2)}, u32[]{:S(2)}) collective-permute-start(bf16[1472,256]{1,0:T(8,128)(2,1)} %get-tuple-element.56), channel_id=1, source_target_pairs={{0,8},{4,12},{8,0},{12,4},{1,9},{5,13},{9,1},{13,5},{2,10},{6,14},... | collective-permute-start | bytes 2261000 | tf_op jit(solution)/shard_map/ppermute | solution.py:361
  58.3 5.6 %shard_map.124.refs_0_.refs_3_ = bf16[256,128]{1,0:T(8,128)(2,1)} custom-call(s32[1]{0:T(128)S(6)} %sub.35.active_ref, bf16[256,3584]{1,0:T(8,128)(2,1)} %copy-done, bf16[896,3584]{1,0:T(8,128)(2,1)} %bitcast.25, bf16[2,64,448]{2,1,0:T(8,128)(2,1)} %get-tuple-element.38.a_ref, bf16[2,64,448]{2,1,0:T(8,128)(2,1)} %get-tuple-element.43.b_ref), custom_call_target="tpu_custom_call" | custom-call | tf_op jit(solution)/shard_map/pallas_call | solution.py:385
  64.0 4.2 %shard_map.126 = (bf16[1040,256]{1,0:T(8,128)(2,1)}, bf16[1040,256]{1,0:T(8,128)(2,1)}, bf16[1040,256]{1,0:T(8,128)(2,1)}, bf16[1040,256]{1,0:T(8,128)(2,1)}) custom-call(s32[1]{0:T(128)} %bitcast.active_ref.upper_ref, s32[1]{0:T(128)} %bitcast.6.y_ref, bf16[256,3584]{1,0:T(8,128)(2,1)} %get-tuple-element.45.refs_6_.refs_0_, ...), custom_call_target="tpu_custom_call" | custom-call | tf_op jit(solution)/shard_map/pallas_call | solution.py:488
  68.4 2.8 %collective-permute-done.9 = s32[8,128]{1,0:T(8,128)S(1)} collective-permute-done((s32[8,128]{1,0:T(8,128)S(1)}, s32[8,128]{1,0:T(8,128)S(1)}, u32[]{:S(2)}, u32[]{:S(2)}) %collective-permute-start.9) | collective-permute-done | bytes 4128 | tf_op jit(solution)/shard_map/ppermute | solution.py:472
  71.5 2.6 %collective-permute-start.18 = (bf16[1040,256]{1,0:T(8,128)(2,1)}, bf16[1040,256]{1,0:T(8,128)(2,1)S(1)}, u32[]{:S(2)}, u32[]{:S(2)}) collective-permute-start(bf16[1040,256]{1,0:T(8,128)(2,1)} %get-tuple-element.49), channel_id=1, source_target_pairs={{0,12},{4,0},{8,4},{12,8},{1,13},{5,1},{9,5},{13,9},{2,14},{6,2},{... | collective-permute-start | bytes 1597448 | tf_op jit(solution)/shard_map/ppermute | solution.py:361
  74.1 9.1 %collective-permute-done.20.refs_2_.refs_14_ = bf16[1472,256]{1,0:T(8,128)(2,1)} collective-permute-done((bf16[1472,256]{1,0:T(8,128)(2,1)}, bf16[1472,256]{1,0:T(8,128)(2,1)}, u32[]{:S(2)}, u32[]{:S(2)}) %collective-permute-start.20) | collective-permute-done | bytes 753696 | tf_op jit(solution)/shard_map/ppermute | solution.py:361
  83.1 2.6 %collective-permute-start.15 = (bf16[3584,128]{1,0:T(8,128)(2,1)S(1)}, bf16[3584,128]{1,0:T(8,128)(2,1)}, u32[]{:S(2)}, u32[]{:S(2)}) collective-permute-start(bf16[3584,128]{1,0:T(8,128)(2,1)S(1)} %bitcast.31), channel_id=1, source_target_pairs={{0,3},{3,0},{1,2},{2,1},{4,7},{7,4},{5,6},{6,5},{8,11},{11,8},{9,1... | collective-permute-start | bytes 2752520 | tf_op jit(solution)/shard_map/ppermute | solution.py:323
  85.8 5.3 %collective-permute-start.14 = (bf16[256,128]{1,0:T(8,128)(2,1)S(1)}, bf16[256,128]{1,0:T(8,128)(2,1)S(1)}, u32[]{:S(2)}, u32[]{:S(2)}) collective-permute-start(bf16[256,128]{1,0:T(8,128)(2,1)S(1)} %copy-done.8), channel_id=1, source_target_pairs={{0,1},{1,0},{2,3},{3,2},{4,5},{5,4},{6,7},{7,6},{8,9},{9,8},{10,11... | collective-permute-start | bytes 196616 | tf_op jit(solution)/shard_map/ppermute | solution.py:453
  92.2 3.3 %shard_map.127 = (bf16[256,896]{1,0:T(8,128)(2,1)}, bf16[256,896]{1,0:T(8,128)(2,1)}, bf16[256,896]{1,0:T(8,128)(2,1)}, bf16[256,896]{1,0:T(8,128)(2,1)}) custom-call(bf16[1472,256]{1,0:T(8,128)(2,1)} %get-tuple-element.54.refs_0_.refs_12_, bf16[1472,256]{1,0:T(8,128)(2,1)} %copy-done.5, bf16[1472,256]{1,0:T(8,128)(2,1)} %collective-permute-done.20.refs_2_.refs_14_, ...), custom_call_target="tpu_custom_call" | custom-call | tf_op jit(solution)/shard_map/pallas_call | solution.py:504
  95.6 9.8 %collective-permute-done.17.refs_2_.refs_6_.refs_10_ = bf16[1040,256]{1,0:T(8,128)(2,1)S(1)} collective-permute-done((bf16[1040,256]{1,0:T(8,128)(2,1)}, bf16[1040,256]{1,0:T(8,128)(2,1)S(1)}, u32[]{:S(2)}, u32[]{:S(2)}) %collective-permute-start.17) | collective-permute-done | bytes 532512 | tf_op jit(solution)/shard_map/ppermute | solution.py:361
  106.4 6.1 %shard_map.128 = (bf16[4,56,1024]{2,1,0:T(8,128)(2,1)}, bf16[4,56,1024]{2,1,0:T(8,128)(2,1)}, bf16[4,56,1024]{2,1,0:T(8,128)(2,1)}, bf16[4,56,1024]{2,1,0:T(8,128)(2,1)}) custom-call(s32[1]{0:T(128)} %bitcast.13.own_ref, f32[1]{0:T(128)} %bitcast.14.scale_ref, bf16[1040,256]{1,0:T(8,128)(2,1)} %get-tuple-element.50.refs_0_.refs_4_.refs_8_, ...), custom_call_target="tpu_custom_call" | custom-call | tf_op jit(solution)/shard_map/pallas_call | solution.py:510
  118.0 7.4 %collective-permute-done.22.b_ref = bf16[4,56,1024]{2,1,0:T(8,128)(2,1)S(1)} collective-permute-done((bf16[4,56,1024]{2,1,0:T(8,128)(2,1)}, bf16[4,56,1024]{2,1,0:T(8,128)(2,1)S(1)}, u32[]{:S(2)}, u32[]{:S(2)}) %collective-permute-start.22) | collective-permute-done | bytes 458784 | tf_op jit(solution)/shard_map/ppermute | solution.py:29
  125.4 2.5 %collective-permute-done.23.c_ref = bf16[4,56,1024]{2,1,0:T(8,128)(2,1)S(1)} collective-permute-done((bf16[4,56,1024]{2,1,0:T(8,128)(2,1)}, bf16[4,56,1024]{2,1,0:T(8,128)(2,1)S(1)}, u32[]{:S(2)}, u32[]{:S(2)}) %collective-permute-start.23) | collective-permute-done | bytes 458784 | tf_op jit(solution)/shard_map/ppermute | solution.py:29
  127.9 8.1 %collective-permute-done.24.d_ref = bf16[4,56,1024]{2,1,0:T(8,128)(2,1)S(1)} collective-permute-done((bf16[4,56,1024]{2,1,0:T(8,128)(2,1)}, bf16[4,56,1024]{2,1,0:T(8,128)(2,1)S(1)}, u32[]{:S(2)}, u32[]{:S(2)}) %collective-permute-start.24) | collective-permute-done | bytes 458784 | tf_op jit(solution)/shard_map/ppermute | solution.py:29
  136.7 2.3 %shard_map.129 = (f32[56,1024]{1,0:T(8,128)}, bf16[56,1024]{1,0:T(8,128)(2,1)}, bf16[56,1024]{1,0:T(8,128)(2,1)}, bf16[56,1024]{1,0:T(8,128)(2,1)}) custom-call(s32[1]{0:T(128)} %bitcast.12.own_ref, bf16[4,56,1024]{2,1,0:T(8,128)(2,1)} %get-tuple-element.62.a_ref, bf16[4,56,1024]{2,1,0:T(8,128)(2,1)} %copy-done.9, bf16[4,56,1024]{2,1,0:T(8,128)(2,1)} %copy-done.10, ...), custom_call_target="tpu_custom_call" | custom-call | tf_op jit(solution)/shard_map/pallas_call | solution.py:531
  139.1 3.2 %collective-permute-start.25 = (bf16[56,1024]{1,0:T(8,128)(2,1)}, bf16[56,1024]{1,0:T(8,128)(2,1)S(1)}, u32[]{:S(2)}, u32[]{:S(2)}) collective-permute-start(bf16[56,1024]{1,0:T(8,128)(2,1)} %get-tuple-element.67), channel_id=1, source_target_pairs={{0,32},{2,34},{16,48},{18,50},{32,0},{34,2},{48,16},{50,18},{64,96... | collective-permute-start | bytes 344072 | tf_op jit(solution)/shard_map/ppermute | solution.py:29
  142.3 5.2 %collective-permute-start.26 = (bf16[56,1024]{1,0:T(8,128)(2,1)}, bf16[56,1024]{1,0:T(8,128)(2,1)S(1)}, u32[]{:S(2)}, u32[]{:S(2)}) collective-permute-start(bf16[56,1024]{1,0:T(8,128)(2,1)} %get-tuple-element.68), channel_id=1, source_target_pairs={{0,64},{2,66},{16,80},{18,82},{32,96},{34,98},{48,112},{50,114},{6... | collective-permute-start | bytes 344072 | tf_op jit(solution)/shard_map/ppermute | solution.py:29
  147.5 5.8 %collective-permute-done.26.c_ref = bf16[56,1024]{1,0:T(8,128)(2,1)S(1)} collective-permute-done((bf16[56,1024]{1,0:T(8,128)(2,1)}, bf16[56,1024]{1,0:T(8,128)(2,1)S(1)}, u32[]{:S(2)}, u32[]{:S(2)}) %collective-permute-start.26) | collective-permute-done | bytes 114720 | tf_op jit(solution)/shard_map/ppermute | solution.py:29
  153.3 2.6 %collective-permute-done.27.d_ref = bf16[56,1024]{1,0:T(8,128)(2,1)S(1)} collective-permute-done((bf16[56,1024]{1,0:T(8,128)(2,1)}, bf16[56,1024]{1,0:T(8,128)(2,1)S(1)}, u32[]{:S(2)}, u32[]{:S(2)}) %collective-permute-start.27) | collective-permute-done | bytes 114720 | tf_op jit(solution)/shard_map/ppermute | solution.py:29
  158.0 2.8 %collective-permute-start.28 = (f32[1,56]{1,0:T(1,128)}, f32[1,56]{1,0:T(1,128)S(1)}, u32[]{:S(2)}, u32[]{:S(2)}) collective-permute-start(f32[1,56]{1,0:T(1,128)} %get-tuple-element.71), channel_id=1, source_target_pairs={{0,1},{1,0},{2,3},{3,2},{4,5},{5,4},{6,7},{7,6},{8,9},{9,8},{10,11... | collective-permute-start | bytes 680 | tf_op jit(solution)/shard_map/ppermute | solution.py:19
  161.6 5.0 %shard_map.125 = bf16[1,128,3584]{2,1,0:T(8,128)(2,1)} custom-call(s32[1]{0:T(128)S(6)} %sub.35.active_ref, s32[1]{0:T(128)} %bitcast.1.tensor_ref, f32[256,1]{1,0:T(8,128)} %copy.19.weight_ref, bf16[256,3584]{1,0:T(8,128)(2,1)} %shard_map.123.done_ref, bf16[256,128]{1,0:T(8,128)(2,1)} %shard_map.124.refs_0_.refs_3_, bf16[256,128]{1,0:T(8,128)(2,1)} %copy-done.15, ...), custom_call_target="tpu_custom_call" | custom-call | tf_op jit(solution)/shard_map/pallas_call | solution.py:430
  (104 shorter events, 32.5 us)
Async XLA Ops:
  0.6 11.0 %collective-permute-start.10 = (bf16[2,64,3584]{2,1,0:T(8,128)(2,1)}, bf16[2,64,3584]{2,1,0:T(8,128)(2,1)S(1)}, u32[]{:S(2)}, u32[]{:S(2)}) collective-permute-start(bf16[2,64,3584]{2,1,0:T(8,128)(2,1)} %bitcast.34), channel_id=1, source_target_pairs={{128,129},{129,128},{130,131},{131,130},{132,133},{133,132},{134,1... | collective-permute-start | bytes 2752520 | tf_op jit(solution)/shard_map/ppermute | solution.py:288
  1.4 15.2 %collective-permute-start.12 = (bf16[3584,128]{1,0:T(8,128)(2,1)}, bf16[3584,128]{1,0:T(8,128)(2,1)S(1)}, u32[]{:S(2)}, u32[]{:S(2)}) collective-permute-start(bf16[3584,128]{1,0:T(8,128)(2,1)} %bitcast.26), channel_id=1, source_target_pairs={{128,131},{131,128},{129,130},{130,129},{132,135},{135,132},{133,1... | collective-permute-start | bytes 2752520 | tf_op jit(solution)/shard_map/ppermute | solution.py:323
  15.9 0.7 collective-permute-start.11
  17.5 35.3 %copy-start.19 = (f32[2,2,64]{2,1,0:T(2,128)S(1)}, f32[2,2,64]{2,1,0:T(2,128)}, u32[]{:S(2)}) copy-start(f32[2,2,64]{2,1,0:T(2,128)} %param.15) | copy-start | bytes 3076
  17.5 36.7 %copy-start.18 = (f32[2,2]{1,0:T(2,128)S(1)}, f32[2,2]{1,0:T(2,128)}, u32[]{:S(2)}) copy-start(f32[2,2]{1,0:T(2,128)} %param.16) | copy-start | bytes 52
  20.0 37.0 %collective-permute-start.13 = (bf16[256,3584]{1,0:T(8,128)(2,1)}, bf16[256,3584]{1,0:T(8,128)(2,1)S(1)}, u32[]{:S(2)}, u32[]{:S(2)}) collective-permute-start(bf16[256,3584]{1,0:T(8,128)(2,1)} %shard_map.123.done_ref), channel_id=1, source_target_pairs={{128,0},{129,1},{130,2},{131,3},{132,4},{133,5},{134,6},{135,7},{1... | collective-permute-start | bytes 5505032 | tf_op jit(solution)/shard_map/ppermute | solution.py:467
  22.7 9.2 %collective-permute-start.2 = (s32[8,128]{1,0:T(8,128)S(1)}, s32[8,128]{1,0:T(8,128)S(1)}, u32[]{:S(2)}, u32[]{:S(2)}) collective-permute-start(s32[8,128]{1,0:T(8,128)S(1)} %broadcast_in_dim.11), channel_id=1, source_target_pairs={{0,6},{2,4},{4,2},{6,0},{8,14},{10,12},{12,10},{14,8},{16,22},{18,... | collective-permute-start | bytes 12296 | tf_op jit(solution)/shard_map/ppermute | solution.py:305
  26.8 5.5 %collective-permute-start = (s32[8,128]{1,0:T(8,128)S(1)}, s32[8,128]{1,0:T(8,128)S(1)}, u32[]{:S(2)}, u32[]{:S(2)}) collective-permute-start(s32[8,128]{1,0:T(8,128)S(1)} %broadcast_in_dim.11), channel_id=1, source_target_pairs={{0,2},{2,0},{4,6},{6,4},{8,10},{10,8},{12,14},{14,12},{16,18},{18,... | collective-permute-start | bytes 12296 | tf_op jit(solution)/shard_map/ppermute | solution.py:305
  29.6 5.5 %collective-permute-start.1 = (s32[8,128]{1,0:T(8,128)S(1)}, s32[8,128]{1,0:T(8,128)S(1)}, u32[]{:S(2)}, u32[]{:S(2)}) collective-permute-start(s32[8,128]{1,0:T(8,128)S(1)} %broadcast_in_dim.11), channel_id=1, source_target_pairs={{0,4},{2,6},{4,0},{6,2},{8,12},{10,14},{12,8},{14,10},{16,20},{18,... | collective-permute-start | bytes 12296 | tf_op jit(solution)/shard_map/ppermute | solution.py:305
  35.1 11.3 %collective-permute-start.5 = (s32[8,128]{1,0:T(8,128)S(1)}, s32[8,128]{1,0:T(8,128)S(1)}, u32[]{:S(2)}, u32[]{:S(2)}) collective-permute-start(s32[8,128]{1,0:T(8,128)S(1)} %add_add_fusion.1), channel_id=1, source_target_pairs={{0,24},{2,26},{4,28},{6,30},{8,16},{10,18},{12,20},{14,22},{16,8},... | collective-permute-start | bytes 12296 | tf_op jit(solution)/shard_map/ppermute | solution.py:305
  41.2 8.3 %collective-permute-start.3 = (s32[8,128]{1,0:T(8,128)S(1)}, s32[8,128]{1,0:T(8,128)S(1)}, u32[]{:S(2)}, u32[]{:S(2)}) collective-permute-start(s32[8,128]{1,0:T(8,128)S(1)} %add_add_fusion.1), channel_id=1, source_target_pairs={{0,16},{2,18},{4,20},{6,22},{8,24},{10,26},{12,28},{14,30},{16,0},... | collective-permute-start | bytes 12296 | tf_op jit(solution)/shard_map/ppermute | solution.py:305
  43.3 8.2 %collective-permute-start.4 = (s32[8,128]{1,0:T(8,128)S(1)}, s32[8,128]{1,0:T(8,128)S(1)}, u32[]{:S(2)}, u32[]{:S(2)}) collective-permute-start(s32[8,128]{1,0:T(8,128)S(1)} %add_add_fusion.1), channel_id=1, source_target_pairs={{0,8},{2,10},{4,12},{6,14},{8,0},{10,2},{12,4},{14,6},{16,24},{18,... | collective-permute-start | bytes 12296 | tf_op jit(solution)/shard_map/ppermute | solution.py:305
  45.8 25.7 %collective-permute-start.19 = (bf16[1472,256]{1,0:T(8,128)(2,1)}, bf16[1472,256]{1,0:T(8,128)(2,1)S(1)}, u32[]{:S(2)}, u32[]{:S(2)}) collective-permute-start(bf16[1472,256]{1,0:T(8,128)(2,1)} %get-tuple-element.55), channel_id=1, source_target_pairs={{0,4},{4,8},{8,12},{12,0},{1,5},{5,9},{9,13},{13,1},{2,6},{6,10},{... | collective-permute-start | bytes 2261000 | tf_op jit(solution)/shard_map/ppermute | solution.py:361
  46.3 36.8 %collective-permute-start.20 = (bf16[1472,256]{1,0:T(8,128)(2,1)}, bf16[1472,256]{1,0:T(8,128)(2,1)}, u32[]{:S(2)}, u32[]{:S(2)}) collective-permute-start(bf16[1472,256]{1,0:T(8,128)(2,1)} %get-tuple-element.56), channel_id=1, source_target_pairs={{0,8},{4,12},{8,0},{12,4},{1,9},{5,13},{9,1},{13,5},{2,10},{6,14},... | collective-permute-start | bytes 2261000 | tf_op jit(solution)/shard_map/ppermute | solution.py:361
  49.5 36.2 %collective-permute-start.21 = (bf16[1472,256]{1,0:T(8,128)(2,1)}, bf16[1472,256]{1,0:T(8,128)(2,1)}, u32[]{:S(2)}, u32[]{:S(2)}) collective-permute-start(bf16[1472,256]{1,0:T(8,128)(2,1)} %get-tuple-element.57), channel_id=1, source_target_pairs={{0,12},{4,0},{8,4},{12,8},{1,13},{5,1},{9,5},{13,9},{2,14},{6,2},{... | collective-permute-start | bytes 2261000 | tf_op jit(solution)/shard_map/ppermute | solution.py:361
  51.4 2.1 %collective-permute-start.6 = (s32[8,128]{1,0:T(8,128)S(1)}, s32[8,128]{1,0:T(8,128)S(1)}, u32[]{:S(2)}, u32[]{:S(2)}) collective-permute-start(s32[8,128]{1,0:T(8,128)S(1)} %add_add_fusion), channel_id=1, source_target_pairs={{0,128},{1,129},{2,130},{3,131},{4,132},{5,133},{6,134},{7,135},{8... | collective-permute-start | bytes 12296 | tf_op jit(solution)/shard_map/ppermute | solution.py:469
  53.5 0.8 collective-permute-start.7
  54.3 0.7 collective-permute-start.8
  55.0 16.1 %collective-permute-start.9 = (s32[8,128]{1,0:T(8,128)S(1)}, s32[8,128]{1,0:T(8,128)S(1)}, u32[]{:S(2)}, u32[]{:S(2)}) collective-permute-start(s32[8,128]{1,0:T(8,128)S(1)} %add.82), channel_id=1, source_target_pairs={{128,0},{129,1},{130,2},{131,3},{132,4},{133,5},{134,6},{135,7},{1... | collective-permute-start | bytes 12296 | tf_op jit(solution)/shard_map/ppermute | solution.py:472
  68.1 27.4 %collective-permute-start.16 = (bf16[1040,256]{1,0:T(8,128)(2,1)}, bf16[1040,256]{1,0:T(8,128)(2,1)S(1)}, u32[]{:S(2)}, u32[]{:S(2)}) collective-permute-start(bf16[1040,256]{1,0:T(8,128)(2,1)} %get-tuple-element.47), channel_id=1, source_target_pairs={{0,4},{4,8},{8,12},{12,0},{1,5},{5,9},{9,13},{13,1},{2,6},{6,10},{... | collective-permute-start | bytes 1597448 | tf_op jit(solution)/shard_map/ppermute | solution.py:361
  71.1 34.2 %collective-permute-start.17 = (bf16[1040,256]{1,0:T(8,128)(2,1)}, bf16[1040,256]{1,0:T(8,128)(2,1)S(1)}, u32[]{:S(2)}, u32[]{:S(2)}) collective-permute-start(bf16[1040,256]{1,0:T(8,128)(2,1)} %get-tuple-element.48), channel_id=1, source_target_pairs={{0,8},{4,12},{8,0},{12,4},{1,9},{5,13},{9,1},{13,5},{2,10},{6,14},... | collective-permute-start | bytes 1597448 | tf_op jit(solution)/shard_map/ppermute | solution.py:361
  71.5 33.9 %collective-permute-start.18 = (bf16[1040,256]{1,0:T(8,128)(2,1)}, bf16[1040,256]{1,0:T(8,128)(2,1)S(1)}, u32[]{:S(2)}, u32[]{:S(2)}) collective-permute-start(bf16[1040,256]{1,0:T(8,128)(2,1)} %get-tuple-element.49), channel_id=1, source_target_pairs={{0,12},{4,0},{8,4},{12,8},{1,13},{5,1},{9,5},{13,9},{2,14},{6,2},{... | collective-permute-start | bytes 1597448 | tf_op jit(solution)/shard_map/ppermute | solution.py:361
  83.1 78.5 %collective-permute-start.15 = (bf16[3584,128]{1,0:T(8,128)(2,1)S(1)}, bf16[3584,128]{1,0:T(8,128)(2,1)}, u32[]{:S(2)}, u32[]{:S(2)}) collective-permute-start(bf16[3584,128]{1,0:T(8,128)(2,1)S(1)} %bitcast.31), channel_id=1, source_target_pairs={{0,3},{3,0},{1,2},{2,1},{4,7},{7,4},{5,6},{6,5},{8,11},{11,8},{9,1... | collective-permute-start | bytes 2752520 | tf_op jit(solution)/shard_map/ppermute | solution.py:323
  85.8 9.8 %collective-permute-start.14 = (bf16[256,128]{1,0:T(8,128)(2,1)S(1)}, bf16[256,128]{1,0:T(8,128)(2,1)S(1)}, u32[]{:S(2)}, u32[]{:S(2)}) collective-permute-start(bf16[256,128]{1,0:T(8,128)(2,1)S(1)} %copy-done.8), channel_id=1, source_target_pairs={{0,1},{1,0},{2,3},{3,2},{4,5},{5,4},{6,7},{7,6},{8,9},{9,8},{10,11... | collective-permute-start | bytes 196616 | tf_op jit(solution)/shard_map/ppermute | solution.py:453
  112.6 34.9 %copy-start.17 = (f32[1,256]{1,0:T(1,128)S(1)}, f32[1,256]{1,0:T(1,128)}, u32[]{:S(2)}) copy-start(f32[1,256]{1,0:T(1,128)} %reshape.226.refs_4_) | copy-start | bytes 3076
  112.6 12.8 %collective-permute-start.22 = (bf16[4,56,1024]{2,1,0:T(8,128)(2,1)}, bf16[4,56,1024]{2,1,0:T(8,128)(2,1)S(1)}, u32[]{:S(2)}, u32[]{:S(2)}) collective-permute-start(bf16[4,56,1024]{2,1,0:T(8,128)(2,1)} %get-tuple-element.63), channel_id=1, source_target_pairs={{0,2},{2,0},{16,18},{18,16},{32,34},{34,32},{48,50},{50,48},{64,66... | collective-permute-start | bytes 1376264 | tf_op jit(solution)/shard_map/ppermute | solution.py:29
  114.3 13.6 %collective-permute-start.23 = (bf16[4,56,1024]{2,1,0:T(8,128)(2,1)}, bf16[4,56,1024]{2,1,0:T(8,128)(2,1)S(1)}, u32[]{:S(2)}, u32[]{:S(2)}) collective-permute-start(bf16[4,56,1024]{2,1,0:T(8,128)(2,1)} %get-tuple-element.64), channel_id=1, source_target_pairs={{0,16},{2,18},{16,0},{18,2},{32,48},{34,50},{48,32},{50,34},{64,80... | collective-permute-start | bytes 1376264 | tf_op jit(solution)/shard_map/ppermute | solution.py:29
  116.2 19.8 %collective-permute-start.24 = (bf16[4,56,1024]{2,1,0:T(8,128)(2,1)}, bf16[4,56,1024]{2,1,0:T(8,128)(2,1)S(1)}, u32[]{:S(2)}, u32[]{:S(2)}) collective-permute-start(bf16[4,56,1024]{2,1,0:T(8,128)(2,1)} %get-tuple-element.65), channel_id=1, source_target_pairs={{0,18},{2,16},{16,2},{18,0},{32,50},{34,48},{48,34},{50,32},{64,82... | collective-permute-start | bytes 1376264 | tf_op jit(solution)/shard_map/ppermute | solution.py:29
  139.1 8.4 %collective-permute-start.25 = (bf16[56,1024]{1,0:T(8,128)(2,1)}, bf16[56,1024]{1,0:T(8,128)(2,1)S(1)}, u32[]{:S(2)}, u32[]{:S(2)}) collective-permute-start(bf16[56,1024]{1,0:T(8,128)(2,1)} %get-tuple-element.67), channel_id=1, source_target_pairs={{0,32},{2,34},{16,48},{18,50},{32,0},{34,2},{48,16},{50,18},{64,96... | collective-permute-start | bytes 344072 | tf_op jit(solution)/shard_map/ppermute | solution.py:29
  142.3 11.1 %collective-permute-start.26 = (bf16[56,1024]{1,0:T(8,128)(2,1)}, bf16[56,1024]{1,0:T(8,128)(2,1)S(1)}, u32[]{:S(2)}, u32[]{:S(2)}) collective-permute-start(bf16[56,1024]{1,0:T(8,128)(2,1)} %get-tuple-element.68), channel_id=1, source_target_pairs={{0,64},{2,66},{16,80},{18,82},{32,96},{34,98},{48,112},{50,114},{6... | collective-permute-start | bytes 344072 | tf_op jit(solution)/shard_map/ppermute | solution.py:29
  147.5 8.4 %collective-permute-start.27 = (bf16[56,1024]{1,0:T(8,128)(2,1)}, bf16[56,1024]{1,0:T(8,128)(2,1)S(1)}, u32[]{:S(2)}, u32[]{:S(2)}) collective-permute-start(bf16[56,1024]{1,0:T(8,128)(2,1)} %get-tuple-element.69), channel_id=1, source_target_pairs={{0,96},{2,98},{16,112},{18,114},{32,64},{34,66},{48,80},{50,82},{6... | collective-permute-start | bytes 344072 | tf_op jit(solution)/shard_map/ppermute | solution.py:29
  158.0 10.4 %collective-permute-start.28 = (f32[1,56]{1,0:T(1,128)}, f32[1,56]{1,0:T(1,128)S(1)}, u32[]{:S(2)}, u32[]{:S(2)}) collective-permute-start(f32[1,56]{1,0:T(1,128)} %get-tuple-element.71), channel_id=1, source_target_pairs={{0,1},{1,0},{2,3},{3,2},{4,5},{5,4},{6,7},{7,6},{8,9},{9,8},{10,11... | collective-permute-start | bytes 680 | tf_op jit(solution)/shard_map/ppermute | solution.py:19
  (18 other events, 132.3 us)
